TPU v7x, 256 devices: a whole 4x4x8 slice. The times are simulated.
256 devices in a mesh: grp: 4 (over x_hi, core), inf: 64 (over y, z, x_lo).
Axes of the slice: x: 4 (x_hi: 2, x_lo: 2; x = x_hi * 2 + x_lo), y: 4, z: 8, core: 2. Of those that a mesh axis runs over, the one named last changes fastest.
Arguments:
- range_one: float32 [1408], replicated, may hold values from 0.05 to 1
- range_two: float32 [1408], replicated, may hold values from 0.05 to 1
- flop_weight: int32 [1024], P('grp'), may hold values from 0 to 24, as said below
- board_mask: int32 [1024, 1408], P('grp', 'inf'), may hold values 0 or 1
- runout: int32 [1024, 4, 2], P('grp'), may hold values from 0 to 51
- strength: int32 [1024, 4, 1408], P('grp', None, 'inf'), may hold values from 0 to 1073741823
Outputs:
- turn_reach: float32 [512, 6, 1408], P(('grp', 'inf'))
- preflop_reach: float32 [1408], P('inf')
Inputs may be any that keep to these rules, and one draw needn't show every extreme that they name: `flop_weight`: slots 256 g to 256 g + 255 belong to group g; in each group the slots with nonzero weight come first; nonzero weights are 4, 12 or 24; exactly 512 slots in all have nonzero weight, every group has at least half of 128 of them, and the busiest group has exactly 256.
All inputs are finite; a program needn't handle non-finite values. No bound on the sum of `board_mask` on one device may be relied on, other than what follows from the above.
Results may differ from a plain program's by a relative error of at most 0.0003.
Values may be sent and summed in bfloat16 or wider, within the bound.
No kernel may reach another device: no remote copies, remote signals or barrier semaphores. Data moves between devices by JAX's collectives and lax.ppermute only.
A program may use at most 64 MiB of HBM per device.

v0:
```python
import math

import jax
import jax.numpy as jnp
import numpy as np
from jax import lax
from jax.sharding import Mesh
from jax.sharding import PartitionSpec as P

HANDS = 1326
H = 1408
ITERS = 4
FLOP_GRP = 128
GRP = ("grp_0", "grp_1")
INF = ("inf_0", "inf_1", "inf_2")
GRP_INF = ("grp_0", "grp_1", "inf_0", "inf_1", "inf_2")


EPSILON = 0.01
FOLD_VALUE = -0.1


def sent_to_all(x, axis):
    copies = jnp.broadcast_to(x, (lax.axis_size(axis), *x.shape))
    return lax.all_to_all(copies, axis, split_axis=0, concat_axis=0, tiled=True)


def in_order(parts, dim):
    parts = jnp.moveaxis(parts, 0, dim)
    dims = parts.shape
    return parts.reshape(*dims[:dim], dims[dim] * dims[dim + 1], *dims[dim + 2 :])


def gathered_copies(x, axis, dim):
    parts = sent_to_all(x, axis)
    return in_order(parts, dim)


def sent_together(arrays, axis, split_dim, concat_dim, along):
    widths = [math.prod(a.shape[along:]) for a in arrays]
    both = jnp.concatenate(
        [a.reshape(*a.shape[:along], w) for a, w in zip(arrays, widths)], axis=along
    )
    filled = lax.all_to_all(both, axis, split_axis=split_dim, concat_axis=concat_dim, tiled=True)
    parts = jnp.split(filled, [sum(widths[:k]) for k in range(1, len(widths))], axis=along)
    return tuple(
        (b.reshape(*filled.shape[:along], *a.shape[along:]) for a, b in zip(arrays, parts))
    )


def side_by_side(arrays, axis, split_dim, concat_dim, along):
    widths = [a.shape[along] for a in arrays]
    both = jnp.concatenate(arrays, axis=along)
    filled = lax.all_to_all(both, axis, split_axis=split_dim, concat_axis=concat_dim, tiled=True)
    return tuple(jnp.split(filled, [sum(widths[:k]) for k in range(1, len(widths))], axis=along))


def one_axis_at_a_time(x, axes):
    for axis in axes:
        x = lax.psum(x, axis)
    return x


def hand_cards(slot_total, real_total):
    low_list = []
    high_list = []
    for first_card in range(52):
        for second_card in range(first_card + 1, 52):
            low_list.append(first_card)
            high_list.append(second_card)
    low_table = np.full(slot_total, 52, np.int32)
    high_table = np.full(slot_total, 53, np.int32)
    used_count = min(slot_total, real_total)
    low_table[:used_count] = np.array(low_list[:used_count], np.int32)
    high_table[:used_count] = np.array(high_list[:used_count], np.int32)
    return (low_table, high_table)


def action_share(first_regret, second_regret):
    return (first_regret + EPSILON) / (first_regret + second_regret + 2.0 * EPSILON)


def pair_values(totals, my_key, my_low, my_high, other_key, other_cols, other_low, other_high):
    compat = (my_low[:, None] != other_low[None, :]) & (my_low[:, None] != other_high[None, :])
    compat = (
        compat
        & (my_high[:, None] != other_low[None, :])
        & (my_high[:, None] != other_high[None, :])
    )
    mine_key = my_key[:, :, None]
    their_key = other_key[:, None, :]
    both_live = compat[None, :, :] & (mine_key >= 0) & (their_key >= 0)
    weight_mat = both_live.astype(jnp.bfloat16)
    sign_mat = jnp.sign(mine_key - their_key).astype(jnp.bfloat16) * weight_mat
    sign_sum = totals[0] + jnp.einsum(
        "smo,sco->scm", sign_mat, other_cols, preferred_element_type=jnp.float32
    )
    summed_weight_total = totals[1] + jnp.einsum(
        "smo,sco->scm", weight_mat, other_cols, preferred_element_type=jnp.float32
    )
    return (sign_sum, summed_weight_total)


def slot_route(counts, group_id, per_group, groups, capacity):
    group_ids = jnp.arange(groups)
    own_count = jnp.sum(jnp.where(group_ids == group_id, counts, 0), dtype=jnp.int32)
    own_rows = jnp.arange(capacity)
    earlier = (group_ids < group_id).astype(jnp.int32)
    place = jnp.sum(
        jnp.minimum(counts[None, :], own_rows[:, None] + earlier[None, :]), axis=1, dtype=jnp.int32
    )
    target = group_ids[:, None] * per_group + jnp.arange(per_group)[None, :]
    match = (place[None, None, :] == target[:, :, None]) & (own_rows < own_count)[None, None, :]
    is_valid = jnp.any(match, axis=2)
    source = jnp.sum(jnp.where(match, own_rows[None, None, :], 0), axis=2, dtype=jnp.int32).reshape(
        -1
    )
    return (source, is_valid)


def place_rows(member, route_pair):
    source, is_valid = route_pair
    groups, per_group = is_valid.shape
    taken_rows = jnp.take(member, source, axis=0).reshape((groups, per_group) + member.shape[1:])
    keep_mask = is_valid.reshape((groups, per_group) + (1,) * (member.ndim - 1))
    return jnp.where(keep_mask, taken_rows, jnp.zeros_like(taken_rows))


def add_sources(member):
    return jnp.sum(member, axis=0, dtype=member.dtype)


def solve(
    key_rows,
    board_rows,
    run_cards,
    weight,
    my_low,
    my_high,
    my_ids,
    range_one,
    range_two,
    values_of,
    sum_groups,
    flop_total,
):
    slot_count, hand_width = board_rows.shape
    payoff_value_scale = 1.0 / HANDS
    flop_live = ((board_rows == 1) & (my_ids < HANDS)[None, :]).astype(jnp.float32)
    flop_share = weight.astype(jnp.float32) / flop_total
    player_two_total = range_two[None, :] * flop_live
    zero_flop = jnp.zeros((slot_count, hand_width), jnp.float32)
    root_check = root_bet = facing_call_fold = fc_call = zero_flop
    ac_check = ac_bet = fb_fold = fb_call = zero_flop
    pre_fold = jnp.zeros((hand_width,), jnp.float32)
    pre_cont = jnp.zeros((hand_width,), jnp.float32)
    turn_sum = jnp.zeros((slot_count, 6, hand_width), jnp.float32)
    pre_sum = jnp.zeros((hand_width,), jnp.float32)
    for counter in range(ITERS):
        share_pre = action_share(pre_cont, pre_fold)
        one_range = range_one * share_pre
        player_one_total = one_range[None, :] * flop_live
        share_root = action_share(root_check, root_bet)
        facing_call_share = action_share(facing_call_fold, fc_call)
        share_ac = action_share(ac_check, ac_bet)
        share_fb = action_share(fb_fold, fb_call)
        player_one_check_share = player_one_total * share_root
        player_one_check_bet_fold = player_one_check_share * facing_call_share
        player_two_check_check = player_two_total * share_ac
        player_two_bet_fold = player_two_total * share_fb
        reach_columns = jnp.stack(
            [
                player_two_total,
                player_two_check_check,
                player_two_bet_fold,
                player_one_total,
                player_one_check_share,
                player_one_check_bet_fold,
            ],
            axis=1,
        ).astype(jnp.bfloat16)
        turn_card = run_cards[:, counter, 0:1]
        river_card = run_cards[:, counter, 1:2]
        blocked = (my_low[None, :] == turn_card) | (my_low[None, :] == river_card)
        blocked = blocked | (my_high[None, :] == turn_card) | (my_high[None, :] == river_card)
        is_alive = (flop_live > 0) & jnp.logical_not(blocked)
        key_now = jnp.where(is_alive, key_rows[:, counter, :], -1)
        sign_sum, summed_weight_total = values_of(key_now, reach_columns)
        v_cc = 0.5 * payoff_value_scale * sign_sum[:, 1, :]
        check_bet_fold_value = (
            -0.5
            * payoff_value_scale
            * (summed_weight_total[:, 0, :] - summed_weight_total[:, 1, :])
        )
        check_bet_call_value = 1.5 * payoff_value_scale * (sign_sum[:, 0, :] - sign_sum[:, 1, :])
        v_bf = 0.5 * payoff_value_scale * summed_weight_total[:, 2, :]
        v_bc = 1.5 * payoff_value_scale * (sign_sum[:, 0, :] - sign_sum[:, 2, :])
        w_cc = 0.5 * payoff_value_scale * sign_sum[:, 4, :]
        check_bet_fold_weight = 0.5 * payoff_value_scale * summed_weight_total[:, 5, :]
        check_bet_call_weight = 1.5 * payoff_value_scale * (sign_sum[:, 4, :] - sign_sum[:, 5, :])
        w_bf = (
            -0.5
            * payoff_value_scale
            * (summed_weight_total[:, 3, :] - summed_weight_total[:, 4, :])
        )
        w_bc = 1.5 * payoff_value_scale * (sign_sum[:, 3, :] - sign_sum[:, 4, :])
        facing_call_utility = (
            facing_call_share * check_bet_fold_value
            + (1.0 - facing_call_share) * check_bet_call_value
        )
        v_check = v_cc + facing_call_utility
        v_bet = v_bf + v_bc
        u_root = share_root * v_check + (1.0 - share_root) * v_bet
        strategy_bet_share = check_bet_fold_weight + check_bet_call_weight
        u_ac = share_ac * w_cc + (1.0 - share_ac) * strategy_bet_share
        u_fb = share_fb * w_bf + (1.0 - share_fb) * w_bc
        facing_call_fold = jnp.maximum(
            facing_call_fold + check_bet_fold_value - facing_call_utility, 0.0
        )
        fc_call = jnp.maximum(fc_call + check_bet_call_value - facing_call_utility, 0.0)
        root_check = jnp.maximum(root_check + v_check - u_root, 0.0)
        root_bet = jnp.maximum(root_bet + v_bet - u_root, 0.0)
        ac_check = jnp.maximum(ac_check + w_cc - u_ac, 0.0)
        ac_bet = jnp.maximum(ac_bet + strategy_bet_share - u_ac, 0.0)
        fb_fold = jnp.maximum(fb_fold + w_bf - u_fb, 0.0)
        fb_call = jnp.maximum(fb_call + w_bc - u_fb, 0.0)
        cont_value = sum_groups(jnp.sum(flop_share[:, None] * u_root, axis=0))
        u_pre = share_pre * cont_value + (1.0 - share_pre) * FOLD_VALUE
        pre_cont = jnp.maximum(pre_cont + cont_value - u_pre, 0.0)
        pre_fold = jnp.maximum(pre_fold + FOLD_VALUE - u_pre, 0.0)
        iter_weight = float(counter + 1)
        turn_row_block = jnp.stack(
            [
                player_one_check_share,
                player_one_total - player_one_check_share,
                player_one_check_share - player_one_check_bet_fold,
                player_two_check_check,
                player_two_total - player_two_bet_fold,
                player_two_total - player_two_check_check,
            ],
            axis=1,
        )
        turn_sum = turn_sum + iter_weight * turn_row_block
        pre_sum = pre_sum + iter_weight * one_range
    return (turn_sum, pre_sum)


def on_device(range_one, range_two, flop_weight, board_mask, runout, strength):
    groups = lax.axis_size(GRP)
    shards = lax.axis_size(INF)
    shard_id = lax.axis_index(INF)
    group_id = lax.axis_index(GRP)
    low_table, high_table = hand_cards(H, HANDS)
    low_all = jnp.asarray(low_table)
    high_all = jnp.asarray(high_table)
    capacity = strength.shape[0]
    hand_block = strength.shape[2]
    flop_total = 12.0 * FLOP_GRP * groups
    live_count = jnp.sum((flop_weight > 0).astype(jnp.int32), dtype=jnp.int32)
    counts = gathered_copies(live_count[None], GRP, 0)
    route_pair = slot_route(counts, group_id, FLOP_GRP, groups, capacity)
    arrived = sent_together(
        (
            place_rows(flop_weight, route_pair),
            place_rows(board_mask, route_pair),
            place_rows(runout, route_pair),
            place_rows(strength, route_pair),
        ),
        GRP,
        0,
        0,
        2,
    )
    weight = add_sources(arrived[0])
    board_rows = add_sources(arrived[1])
    run_cards = add_sources(arrived[2])
    key_rows = add_sources(arrived[3])
    local_count = key_rows.shape[0] // shards
    flop_keys, flop_board = side_by_side((key_rows, board_rows[:, None, :]), INF, 0, 2, 1)
    first_slot = shard_id * local_count
    runs_here = lax.dynamic_slice_in_dim(run_cards, first_slot, local_count, 0)
    weight_here = lax.dynamic_slice_in_dim(weight, first_slot, local_count, 0)

    def whole_values(key_now, reach_columns):
        zero_sums = jnp.zeros(reach_columns.shape, jnp.float32)

        def add_block(totals, block_id):
            first_row = block_id * 128
            other_key = lax.dynamic_slice_in_dim(key_now, first_row, 128, 1)
            other_cols = lax.dynamic_slice_in_dim(reach_columns, first_row, 128, 2)
            other_low = lax.dynamic_slice_in_dim(low_all, first_row, 128)
            other_high = lax.dynamic_slice_in_dim(high_all, first_row, 128)
            return (
                pair_values(
                    totals, key_now, low_all, high_all, other_key, other_cols, other_low, other_high
                ),
                None,
            )

        totals, unused = lax.scan(add_block, (zero_sums, zero_sums), jnp.arange(H // 128))
        return totals

    def whole_sum(values):
        return one_axis_at_a_time(values, GRP_INF)

    turn_sum, pre_sum = solve(
        flop_keys,
        flop_board[:, 0, :],
        runs_here,
        weight_here,
        low_all,
        high_all,
        jnp.arange(H),
        range_one,
        range_two,
        whole_values,
        whole_sum,
        flop_total,
    )
    pre_block = lax.dynamic_slice_in_dim(pre_sum, shard_id * hand_block, hand_block)
    total_weight = ITERS * (ITERS + 1) / 2.0
    turn_final = turn_sum / total_weight
    return (turn_final, pre_block / total_weight)


def solution(mesh):
    split = Mesh(mesh.devices.reshape(2, 2, 4, 8, 2), ("grp_0", "grp_1", "inf_0", "inf_1", "inf_2"))
    return jax.shard_map(
        on_device,
        mesh=split,
        in_specs=(P(), P(), P(GRP), P(GRP, INF), P(GRP, None, None), P(GRP, None, INF)),
        out_specs=(P(GRP_INF, None, None), P(INF)),
        check_vma=False,
    )
```

profile of v0, /device:TPU:8, one launch (start us, length us, event | category | flops | bytes accessed | tf_op | source)
XLA Modules:
  0.0 307.0 jit_solution(2844996688964480917)
XLA Ops:
  0.6 1.4 fusion.95
  2.0 1.2 broadcast_in_dim.103
  3.2 4.3 %all-to-all-start = ((s32[4,1,1]{2,1,0:T(1,128)}), s32[4,1,1]{2,1,0:T(1,128)S(1)}, u32[]{:S(2)}, u32[]{:S(2)}) async-start(s32[4,1,1]{2,1,0:T(1,128)} %broadcast_in_dim.103), calls=%async_computation | async-start | bytes 4096 | tf_op jit(solution)/shard_map/all_to_all | solution.py:25
  7.7 1.1 copy.247
  10.6 2.2 all-to-all-done
  14.9 3.5 %gather_fusion = s32[512]{0:T(512)S(1)} fusion(s32[256]{0:T(256)S(1)} %copy-done, s32[1024]{0:T(1024)S(1)} %pad_clamp_fusion), kind=kCustom, calls=%fused_computation | custom fusion | bytes 6144 | tf_op jit(solution)/shard_map/jit(_take)/gather | solution.py:124
  18.4 2.1 gather_fusion.3
  20.9 2.1 gather_fusion.2
  23.3 1.0 gather_fusion.1
  25.2 3.4 %all-to-all-start.1 = ((s32[4,128,119]{1,2,0:T(8,128)}), s32[4,128,119]{1,2,0:T(8,128)S(1)}, u32[]{:S(2)}, u32[]{:S(2)}) async-start(s32[4,128,119]{1,2,0:T(8,128)} %copy.249), calls=%async_computation.1 | async-start | bytes 491520 | tf_op jit(solution)/shard_map/all_to_all | solution.py:44
  28.7 7.3 %all-to-all-done.1 = s32[4,128,119]{1,2,0:T(8,128)S(1)} async-done(((s32[4,128,119]{1,2,0:T(8,128)}), s32[4,128,119]{1,2,0:T(8,128)S(1)}, u32[]{:S(2)}, u32[]{:S(2)}) %all-to-all-start.1) | async-done | bytes 243744 | tf_op jit(solution)/shard_map/all_to_all | solution.py:44
  37.2 12.1 %all-to-all-start.2 = ((s32[64,1,220]{2,1,0:T(1,128)}), s32[64,1,220]{2,1,0:T(1,128)S(1)}, u32[]{:S(2)}, u32[]{:S(2)}) async-start(s32[64,1,220]{2,1,0:T(1,128)} %reshape.922), calls=%async_computation.2 | async-start | bytes 131072 | tf_op jit(solution)/shard_map/all_to_all | solution.py:54
  49.5 9.3 %all-to-all-done.2 = s32[64,1,220]{2,1,0:T(1,128)S(1)} async-done(((s32[64,1,220]{2,1,0:T(1,128)}), s32[64,1,220]{2,1,0:T(1,128)S(1)}, u32[]{:S(2)}, u32[]{:S(2)}) %all-to-all-start.2) | async-done | bytes 56352 | tf_op jit(solution)/shard_map/all_to_all | solution.py:54
  61.6 42.5 %while.42 = (s32[]{:T(128)}, f32[2,6,1408]{2,1,0:T(8,128)S(1)}, f32[2,6,1408]{2,1,0:T(8,128)S(1)}, s32[11]{0:T(128)S(1)}, bf16[2,6,1408]{2,0,1:T(2,128)(2,1)S(1)...) while((s32[]{:T(128)}, f32[2,6,1408]{2,1,0:T(8,128)S(1)}, ...), condition=%wide.region_9.10_spmd.clone.clone, body=%wide.region_8.9_spmd.sunk.clone.clone.sunk | while | flops 12866567 | bytes 872650 | solution.py:300
  64.5 0.9 convolution_add_fusion.12
  68.4 0.9 convolution_add_fusion.12
  72.3 0.9 convolution_add_fusion.12
  76.1 0.9 convolution_add_fusion.12
  80.0 0.9 convolution_add_fusion.12
  83.8 0.9 convolution_add_fusion.12
  87.7 0.9 convolution_add_fusion.12
  91.6 0.9 convolution_add_fusion.12
  95.4 0.9 convolution_add_fusion.12
  99.3 0.9 convolution_add_fusion.12
  103.2 0.9 convolution_add_fusion.12
  104.3 6.5 %psum.105 = f32[1408]{0:T(1024)S(1)} all-reduce(f32[1408]{0:T(1024)S(1)} %get-tuple-element.455), channel_id=1, replica_groups=mesh['grp_0'=2,'grp_1'=2,'inf_0'=4,'inf_1'=8,'inf_2'=2] {'grp_0'}, use_global_device_ids=true, to_apply=%region_12.13 | all-reduce | flops 1408 | bytes 11264 | tf_op jit(solution)/shard_map/psum | solution.py:60
  110.8 2.5 psum.106
  113.3 9.2 %psum.107 = f32[1408]{0:T(1024)S(1)} all-reduce(f32[1408]{0:T(1024)S(1)} %psum.106), channel_id=1, replica_groups=mesh['grp_0'=2,'grp_1'=2,'inf_0'=4,'inf_1'=8,'inf_2'=2] {'inf_0'}, use_global_device_ids=true, to_apply=%region_14.15 | all-reduce | flops 1408 | bytes 11264 | tf_op jit(solution)/shard_map/psum | solution.py:60
  122.4 15.2 %psum.108 = f32[1408]{0:T(1024)S(1)} all-reduce(f32[1408]{0:T(1024)S(1)} %psum.107), channel_id=1, replica_groups=mesh['grp_0'=2,'grp_1'=2,'inf_0'=4,'inf_1'=8,'inf_2'=2] {'inf_1'}, use_global_device_ids=true, to_apply=%region_15.16 | all-reduce | flops 1408 | bytes 11264 | tf_op jit(solution)/shard_map/psum | solution.py:60
  137.6 5.0 %psum.109 = f32[1408]{0:T(1024)S(1)} all-reduce(f32[1408]{0:T(1024)S(1)} %psum.108), channel_id=1, replica_groups=mesh['grp_0'=2,'grp_1'=2,'inf_0'=4,'inf_1'=8,'inf_2'=2] {'inf_2'}, use_global_device_ids=true, to_apply=%region_16.17 | all-reduce | flops 1408 | bytes 11264 | tf_op jit(solution)/shard_map/psum | solution.py:60
  143.0 42.5 %while.43 = (s32[]{:T(128)}, f32[2,6,1408]{2,1,0:T(8,128)S(1)}, f32[2,6,1408]{2,1,0:T(8,128)S(1)}, s32[11]{0:T(128)S(1)}, bf16[2,6,1408]{2,0,1:T(2,128)(2,1)S(1)...) while((s32[]{:T(128)}, f32[2,6,1408]{2,1,0:T(8,128)S(1)}, ...), condition=%wide.region_18.19_spmd.clone.clone, body=%wide.region_17.18_spmd.sunk.clone.clone.sunk | while | flops 12866567 | bytes 872650 | solution.py:300
  146.0 0.9 convolution_add_fusion.14
  149.8 0.9 convolution_add_fusion.14
  153.7 0.9 convolution_add_fusion.14
  157.5 0.9 convolution_add_fusion.14
  161.4 0.9 convolution_add_fusion.14
  165.3 0.9 convolution_add_fusion.14
  185.7 6.5 %psum.110 = f32[1408]{0:T(1024)S(1)} all-reduce(f32[1408]{0:T(1024)S(1)} %get-tuple-element.450), channel_id=1, replica_groups=mesh['grp_0'=2,'grp_1'=2,'inf_0'=4,'inf_1'=8,'inf_2'=2] {'grp_0'}, use_global_device_ids=true, to_apply=%region_20.21 | all-reduce | flops 1408 | bytes 11264 | tf_op jit(solution)/shard_map/psum | solution.py:60
  192.2 2.5 psum.111
  194.6 8.9 %psum.112 = f32[1408]{0:T(1024)S(1)} all-reduce(f32[1408]{0:T(1024)S(1)} %psum.111), channel_id=1, replica_groups=mesh['grp_0'=2,'grp_1'=2,'inf_0'=4,'inf_1'=8,'inf_2'=2] {'inf_0'}, use_global_device_ids=true, to_apply=%region_22.23 | all-reduce | flops 1408 | bytes 11264 | tf_op jit(solution)/shard_map/psum | solution.py:60
  203.6 15.6 %psum.113 = f32[1408]{0:T(1024)S(1)} all-reduce(f32[1408]{0:T(1024)S(1)} %psum.112), channel_id=1, replica_groups=mesh['grp_0'=2,'grp_1'=2,'inf_0'=4,'inf_1'=8,'inf_2'=2] {'inf_1'}, use_global_device_ids=true, to_apply=%region_23.24 | all-reduce | flops 1408 | bytes 11264 | tf_op jit(solution)/shard_map/psum | solution.py:60
  219.2 5.0 %psum.114 = f32[1408]{0:T(1024)S(1)} all-reduce(f32[1408]{0:T(1024)S(1)} %psum.113), channel_id=1, replica_groups=mesh['grp_0'=2,'grp_1'=2,'inf_0'=4,'inf_1'=8,'inf_2'=2] {'inf_2'}, use_global_device_ids=true, to_apply=%region_24.25 | all-reduce | flops 1408 | bytes 11264 | tf_op jit(solution)/shard_map/psum | solution.py:60
  224.7 42.4 %while.44 = (s32[]{:T(128)}, f32[2,6,1408]{2,1,0:T(8,128)S(1)}, f32[2,6,1408]{2,1,0:T(8,128)S(1)}, s32[11]{0:T(128)S(1)}, bf16[2,6,1408]{2,0,1:T(2,128)(2,1)S(1)...) while((s32[]{:T(128)}, f32[2,6,1408]{2,1,0:T(8,128)S(1)}, ...), condition=%wide.region_26.27_spmd.clone.clone, body=%wide.region_25.26_spmd.sunk.clone.clone.sunk | while | flops 12866567 | bytes 872650 | solution.py:300
  267.3 6.5 %psum.115 = f32[1408]{0:T(1024)S(1)} all-reduce(f32[1408]{0:T(1024)S(1)} %fusion.65), channel_id=1, replica_groups=mesh['grp_0'=2,'grp_1'=2,'inf_0'=4,'inf_1'=8,'inf_2'=2] {'grp_0'}, use_global_device_ids=true, to_apply=%region_28.29 | all-reduce | flops 1408 | bytes 11264 | tf_op jit(solution)/shard_map/psum | solution.py:60
  273.9 2.5 psum.116
  276.3 8.8 %psum.117 = f32[1408]{0:T(1024)S(1)} all-reduce(f32[1408]{0:T(1024)S(1)} %psum.116), channel_id=1, replica_groups=mesh['grp_0'=2,'grp_1'=2,'inf_0'=4,'inf_1'=8,'inf_2'=2] {'inf_0'}, use_global_device_ids=true, to_apply=%region_30.31 | all-reduce | flops 1408 | bytes 11264 | tf_op jit(solution)/shard_map/psum | solution.py:60
  285.1 15.2 %psum.118 = f32[1408]{0:T(1024)S(1)} all-reduce(f32[1408]{0:T(1024)S(1)} %psum.117), channel_id=1, replica_groups=mesh['grp_0'=2,'grp_1'=2,'inf_0'=4,'inf_1'=8,'inf_2'=2] {'inf_1'}, use_global_device_ids=true, to_apply=%region_31.32 | all-reduce | flops 1408 | bytes 11264 | tf_op jit(solution)/shard_map/psum | solution.py:60
  300.3 5.0 %psum.119 = f32[1408]{0:T(1024)S(1)} all-reduce(f32[1408]{0:T(1024)S(1)} %psum.118), channel_id=1, replica_groups=mesh['grp_0'=2,'grp_1'=2,'inf_0'=4,'inf_1'=8,'inf_2'=2] {'inf_2'}, use_global_device_ids=true, to_apply=%region_32.33 | all-reduce | flops 1408 | bytes 11264 | tf_op jit(solution)/shard_map/psum | solution.py:60
  (395 shorter events, 101.1 us)
Async XLA Ops:
  0.6 14.2 %copy-start = (s32[256]{0:T(256)S(1)}, s32[256]{0:T(256)}, u32[]{:S(2)}) copy-start(s32[256]{0:T(256)} %param.16) | copy-start | bytes 3076
  3.2 9.5 %all-to-all-start = ((s32[4,1,1]{2,1,0:T(1,128)}), s32[4,1,1]{2,1,0:T(1,128)S(1)}, u32[]{:S(2)}, u32[]{:S(2)}) async-start(s32[4,1,1]{2,1,0:T(1,128)} %broadcast_in_dim.103), calls=%async_computation | async-start | bytes 4096 | tf_op jit(solution)/shard_map/all_to_all | solution.py:25
  24.3 4.3 %copy-start.4 = (f32[1408]{0:T(1024)S(1)}, f32[1408]{0:T(1024)}, u32[]{:S(2)}) copy-start(f32[1408]{0:T(1024)} %param.14) | copy-start | bytes 16900
  25.2 10.7 %all-to-all-start.1 = ((s32[4,128,119]{1,2,0:T(8,128)}), s32[4,128,119]{1,2,0:T(8,128)S(1)}, u32[]{:S(2)}, u32[]{:S(2)}) async-start(s32[4,128,119]{1,2,0:T(8,128)} %copy.249), calls=%async_computation.1 | async-start | bytes 491520 | tf_op jit(solution)/shard_map/all_to_all | solution.py:44
  37.2 21.7 %all-to-all-start.2 = ((s32[64,1,220]{2,1,0:T(1,128)}), s32[64,1,220]{2,1,0:T(1,128)S(1)}, u32[]{:S(2)}, u32[]{:S(2)}) async-start(s32[64,1,220]{2,1,0:T(1,128)} %reshape.922), calls=%async_computation.2 | async-start | bytes 131072 | tf_op jit(solution)/shard_map/all_to_all | solution.py:54
  60.4 0.7 copy-start.3
  60.4 0.9 copy-start.1
  60.4 0.9 copy-start.2
where the time goes:
time: 308 us; the launch traced here: 307 us
  blocking collectives  115 us (37%)
  matrix products  49.2 us (16%)
  local copies, waits for them, and re-layouts  42.2 us (14%)
  other arithmetic  38.1 us (12%)
  loops' own time  23 us (7%)
  starting transfers between devices  19.8 us (6%)
  waiting for transfers between devices  18.8 us (6%)
    psum x15, blocking collectives, one_axis_at_a_time(): x = lax.psum(x, axis)  115 us
    dot_general x33, matrix products, pair_values(): jnp.einsum('smo,sco->scm', sign_mat, other_cols, preferred_element_type=j...  30.7 us
    and x33, other arithmetic, pair_values(): compat & (my_high[:, None] != other_low[None, :])  29.5 us
    another operation x3, loops' own time, whole_values(): lax.scan(add_block, (zero_sums, zero_sums), jnp.arange(H // 128))  23 us
    dynamic_slice x33, local copies, waits for them, and re-layouts, whole_values(): lax.scan(add_block, (zero_sums, zero_sums), jnp.arange(H // 128))  19.5 us
    dot_general x33, matrix products, pair_values(): jnp.einsum('smo,sco->scm', weight_mat, other_cols, preferred_element_type...  18.4 us
    all_to_all x1, starting transfers between devices, side_by_side(): lax.all_to_all(both, axis, split_axis=split_dim, concat_axis=concat_dim,...  12.1 us
    gather x9, local copies, waits for them, and re-layouts, place_rows(): jnp.take(member, source, axis=0)  9.47 us
  transfers between devices with their start and end apart: 3, of which 3 were waited for; matrix products, arithmetic and copies ran while one was open for 1% of the time, Pallas kernels for 0%

commit v1 on v0

v1 whole, which is shorter than its diff:
```python
import math

import jax
import jax.numpy as jnp
import numpy as np
from jax import lax
from jax.experimental import pallas as pl
from jax.experimental.pallas import tpu as pltpu
from jax.sharding import Mesh
from jax.sharding import PartitionSpec as P

HANDS = 1326
H = 1408
ITERS = 4
FLOP_GRP = 128
GRP = ("grp_0", "grp_1")
INF = ("inf_0", "inf_1", "inf_2")
GRP_INF = ("grp_0", "grp_1", "inf_0", "inf_1", "inf_2")


EPSILON = 0.01
FOLD_VALUE = -0.1


def sent_to_all(x, axis):
    copies = jnp.broadcast_to(x, (lax.axis_size(axis), *x.shape))
    return lax.all_to_all(copies, axis, split_axis=0, concat_axis=0, tiled=True)


def in_order(parts, dim):
    parts = jnp.moveaxis(parts, 0, dim)
    dims = parts.shape
    return parts.reshape(*dims[:dim], dims[dim] * dims[dim + 1], *dims[dim + 2 :])


def gathered_copies(x, axis, dim):
    parts = sent_to_all(x, axis)
    return in_order(parts, dim)


def sent_together(arrays, axis, split_dim, concat_dim, along):
    widths = [math.prod(a.shape[along:]) for a in arrays]
    both = jnp.concatenate(
        [a.reshape(*a.shape[:along], w) for a, w in zip(arrays, widths)], axis=along
    )
    filled = lax.all_to_all(both, axis, split_axis=split_dim, concat_axis=concat_dim, tiled=True)
    parts = jnp.split(filled, [sum(widths[:k]) for k in range(1, len(widths))], axis=along)
    return tuple(
        (b.reshape(*filled.shape[:along], *a.shape[along:]) for a, b in zip(arrays, parts))
    )


def side_by_side(arrays, axis, split_dim, concat_dim, along):
    widths = [a.shape[along] for a in arrays]
    both = jnp.concatenate(arrays, axis=along)
    filled = lax.all_to_all(both, axis, split_axis=split_dim, concat_axis=concat_dim, tiled=True)
    return tuple(jnp.split(filled, [sum(widths[:k]) for k in range(1, len(widths))], axis=along))


def hand_cards(slot_total, real_total):
    low_list = []
    high_list = []
    for first_card in range(52):
        for second_card in range(first_card + 1, 52):
            low_list.append(first_card)
            high_list.append(second_card)
    low_table = np.full(slot_total, 52, np.int32)
    high_table = np.full(slot_total, 53, np.int32)
    used_count = min(slot_total, real_total)
    low_table[:used_count] = np.array(low_list[:used_count], np.int32)
    high_table[:used_count] = np.array(high_list[:used_count], np.int32)
    return (low_table, high_table)


def action_share(first_regret, second_regret):
    return (first_regret + EPSILON) / (first_regret + second_regret + 2.0 * EPSILON)


def slot_route(counts, group_id, per_group, groups, capacity):
    group_ids = jnp.arange(groups)
    own_count = jnp.sum(jnp.where(group_ids == group_id, counts, 0), dtype=jnp.int32)
    own_rows = jnp.arange(capacity)
    earlier = (group_ids < group_id).astype(jnp.int32)
    place = jnp.sum(
        jnp.minimum(counts[None, :], own_rows[:, None] + earlier[None, :]), axis=1, dtype=jnp.int32
    )
    target = group_ids[:, None] * per_group + jnp.arange(per_group)[None, :]
    match = (place[None, None, :] == target[:, :, None]) & (own_rows < own_count)[None, None, :]
    is_valid = jnp.any(match, axis=2)
    source = jnp.sum(jnp.where(match, own_rows[None, None, :], 0), axis=2, dtype=jnp.int32).reshape(
        -1
    )
    return (source, is_valid)


def place_rows(member, route_pair):
    source, is_valid = route_pair
    groups, per_group = is_valid.shape
    taken_rows = jnp.take(member, source, axis=0).reshape((groups, per_group) + member.shape[1:])
    keep_mask = is_valid.reshape((groups, per_group) + (1,) * (member.ndim - 1))
    return jnp.where(keep_mask, taken_rows, jnp.zeros_like(taken_rows))


def add_sources(member):
    return jnp.sum(member, axis=0, dtype=member.dtype)


SCALE = 1.0 / HANDS
BLOCK = 128
FIRST_SUM = ("grp_0", "inf_0", "inf_2")


def compat_kernel(low_ref, high_ref, out_ref):
    low_row = low_ref[...]
    high_row = high_ref[...]
    for first in range(0, H, BLOCK):
        low_col = jnp.broadcast_to(low_ref[:, first : first + BLOCK], (BLOCK, BLOCK)).T
        high_col = jnp.broadcast_to(high_ref[:, first : first + BLOCK], (BLOCK, BLOCK)).T
        for start in range(0, H, BLOCK):
            low_here = low_row[:, start : start + BLOCK]
            high_here = high_row[:, start : start + BLOCK]
            apart = (low_col != low_here) & (low_col != high_here)
            apart = apart & (high_col != low_here) & (high_col != high_here)
            out_ref[first : first + BLOCK, start : start + BLOCK] = jnp.where(
                apart, 1.0, 0.0
            ).astype(jnp.bfloat16)


def compat_matrix(low, high):
    return pl.pallas_call(
        compat_kernel,
        out_shape=jax.ShapeDtypeStruct((H, H), jnp.bfloat16),
        name="compat",
    )(low.reshape(1, H), high.reshape(1, H))


def pair_sums(key_ref, counter, columns, compat_ref, col_ref, lhs_ref, sign_ref, sums_ref, weight_ref):
    alive = (key_ref[counter] >= 0).astype(jnp.float32)
    col_ref[...] = jnp.zeros((16, H), jnp.float32)
    for k, column in columns.items():
        col_ref[2 * k : 2 * k + 2, :] = column * alive
    lhs_ref[...] = col_ref[...].astype(jnp.bfloat16)
    weight_ref[...] = jnp.dot(lhs_ref[...], compat_ref[...], preferred_element_type=jnp.float32)
    row_flop = lax.broadcasted_iota(jnp.int32, (16, H), 0) & 1

    def one_flop(flop, carry):
        key_row = key_ref[counter, flop : flop + 1, :]
        for first in range(0, H, BLOCK):
            key_col = jnp.broadcast_to(key_row[:, first : first + BLOCK], (BLOCK, BLOCK)).T
            for start in range(0, H, BLOCK):
                key_here = key_row[:, start : start + BLOCK]
                sign = jnp.where(
                    key_here > key_col, 1.0, jnp.where(key_here < key_col, -1.0, 0.0)
                ).astype(jnp.bfloat16)
                sign_ref[first : first + BLOCK, start : start + BLOCK] = (
                    sign * compat_ref[first : first + BLOCK, start : start + BLOCK]
                )
        total = jnp.dot(lhs_ref[...], sign_ref[...], preferred_element_type=jnp.float32)
        sums_ref[...] = jnp.where(row_flop == flop, total, sums_ref[...])
        return carry

    for flop in range(2):
        one_flop(flop, 0)
    sign_sum = {k: sums_ref[2 * k : 2 * k + 2, :] * alive for k in columns}
    weight_sum = {k: weight_ref[2 * k : 2 * k + 2, :] * alive for k in columns}
    return sign_sum, weight_sum


def two_values(sign_sum, weight_sum, share_root, share_fc):
    v_cc = 0.5 * SCALE * sign_sum[1]
    v_cbf = -0.5 * SCALE * (weight_sum[0] - weight_sum[1])
    v_cbc = 1.5 * SCALE * (sign_sum[0] - sign_sum[1])
    v_bf = 0.5 * SCALE * weight_sum[2]
    v_bc = 1.5 * SCALE * (sign_sum[0] - sign_sum[2])
    u_fc = share_fc * v_cbf + (1.0 - share_fc) * v_cbc
    v_check = v_cc + u_fc
    v_bet = v_bf + v_bc
    u_root = share_root * v_check + (1.0 - share_root) * v_bet
    return v_cbf, v_cbc, u_fc, v_check, v_bet, u_root


def one_values(sign_sum, weight_sum, share_ac, share_fb):
    w_cc = 0.5 * SCALE * sign_sum[4]
    w_cbf = 0.5 * SCALE * weight_sum[5]
    w_cbc = 1.5 * SCALE * (sign_sum[4] - sign_sum[5])
    w_bf = -0.5 * SCALE * (weight_sum[3] - weight_sum[4])
    w_bc = 1.5 * SCALE * (sign_sum[3] - sign_sum[4])
    x_bet = w_cbf + w_cbc
    u_ac = share_ac * w_cc + (1.0 - share_ac) * x_bet
    u_fb = share_fb * w_bf + (1.0 - share_fb) * w_bc
    return w_cc, x_bet, u_ac, w_bf, w_bc, u_fb


def two_regrets(regrets, values):
    root_check, root_bet, fc_fold, fc_call = regrets
    v_cbf, v_cbc, u_fc, v_check, v_bet, u_root = values
    return (
        jnp.maximum(root_check + v_check - u_root, 0.0),
        jnp.maximum(root_bet + v_bet - u_root, 0.0),
        jnp.maximum(fc_fold + v_cbf - u_fc, 0.0),
        jnp.maximum(fc_call + v_cbc - u_fc, 0.0),
    )


def one_regrets(regrets, values):
    ac_check, ac_bet, fb_fold, fb_call = regrets
    w_cc, x_bet, u_ac, w_bf, w_bc, u_fb = values
    return (
        jnp.maximum(ac_check + w_cc - u_ac, 0.0),
        jnp.maximum(ac_bet + x_bet - u_ac, 0.0),
        jnp.maximum(fb_fold + w_bf - u_fb, 0.0),
        jnp.maximum(fb_call + w_bc - u_fb, 0.0),
    )


def pre_step(pre_cont, pre_fold, cont_value):
    share_pre = action_share(pre_cont, pre_fold)
    u_pre = share_pre * cont_value + (1.0 - share_pre) * FOLD_VALUE
    return (
        jnp.maximum(pre_cont + cont_value - u_pre, 0.0),
        jnp.maximum(pre_fold + FOLD_VALUE - u_pre, 0.0),
    )


def one_columns(one_all, share_root, share_fc):
    one_check = one_all * share_root
    return {3: one_all, 4: one_check, 5: one_check * share_fc}


def two_columns(two_all, share_ac, share_fb):
    return {0: two_all, 1: two_all * share_ac, 2: two_all * share_fb}


def one_rows(columns):
    return columns[4], columns[3] - columns[4], columns[4] - columns[5]


def two_rows(columns):
    return columns[1], columns[0] - columns[2], columns[0] - columns[1]


def flop_value(share, u_root):
    part = share * u_root
    return part[0:1, :] + part[1:2, :]


def first_kernel(
    key_ref, live_ref, one_ref, two_ref, share_ref, compat_ref,
    cont_ref, root_check_ref, root_bet_ref, fc_fold_ref, fc_call_ref,
    ac_check_ref, ac_bet_ref, fb_fold_ref, fb_call_ref, share_root_ref, share_fc_ref, turn_ref,
    col_ref, lhs_ref, sign_ref, sums_ref, weight_ref,
):
    scratch = (compat_ref, col_ref, lhs_ref, sign_ref, sums_ref, weight_ref)
    live = live_ref[...]
    share = share_ref[...]
    zero = jnp.zeros((2, H), jnp.float32)
    zero_row = jnp.zeros((1, H), jnp.float32)
    two_all = two_ref[...] * live
    start = action_share(zero, zero)
    one_all = one_ref[...] * action_share(zero_row, zero_row) * live
    one_cols = one_columns(one_all, start, start)
    two_cols = two_columns(two_all, start, start)
    sign_sum, weight_sum = pair_sums(key_ref, 0, {**two_cols, **one_cols}, *scratch)
    values = two_values(sign_sum, weight_sum, start, start)
    cont_ref[0:1, :] = flop_value(share, values[5])
    regrets = two_regrets((zero, zero, zero, zero), values)
    others = one_regrets((zero, zero, zero, zero), one_values(sign_sum, weight_sum, start, start))
    turns = [*one_rows(one_cols), *two_rows(two_cols)]

    share_root = action_share(regrets[0], regrets[1])
    share_fc = action_share(regrets[2], regrets[3])
    two_cols = two_columns(
        two_all, action_share(others[0], others[1]), action_share(others[2], others[3])
    )
    sign_sum, weight_sum = pair_sums(key_ref, 1, two_cols, *scratch)
    values = two_values(sign_sum, weight_sum, share_root, share_fc)
    cont_ref[1:2, :] = flop_value(share, values[5])
    regrets = two_regrets(regrets, values)
    for k, row in enumerate(two_rows(two_cols)):
        turns[3 + k] = turns[3 + k] + 2.0 * row
    root_check_ref[...], root_bet_ref[...], fc_fold_ref[...], fc_call_ref[...] = regrets
    ac_check_ref[...], ac_bet_ref[...], fb_fold_ref[...], fb_call_ref[...] = others
    share_root_ref[...] = share_root
    share_fc_ref[...] = share_fc
    for k in range(6):
        turn_ref[k] = turns[k]


def second_kernel(
    key_ref, live_ref, one_ref, two_ref, share_ref, compat_ref, sums_in_ref,
    root_check_ref, root_bet_ref, fc_fold_ref, fc_call_ref,
    ac_check_ref, ac_bet_ref, fb_fold_ref, fb_call_ref, share_root_ref, share_fc_ref, turn_ref,
    cont_ref, out_root_ref, out_fc_ref, out_turn_ref, out_pre_ref,
    col_ref, lhs_ref, sign_ref, sums_ref, weight_ref,
):
    scratch = (compat_ref, col_ref, lhs_ref, sign_ref, sums_ref, weight_ref)
    live = live_ref[...]
    zero_row = jnp.zeros((1, H), jnp.float32)
    two_all = two_ref[...] * live
    one_range = one_ref[...]
    turns = [turn_ref[k] for k in range(6)]
    pre_sum = one_range * action_share(zero_row, zero_row)
    pre_cont, pre_fold = pre_step(zero_row, zero_row, sums_in_ref[0:1, :])
    one_now = one_range * action_share(pre_cont, pre_fold)
    pre_sum = pre_sum + 2.0 * one_now
    one_cols = one_columns(one_now * live, share_root_ref[...], share_fc_ref[...])
    for k, row in enumerate(one_rows(one_cols)):
        turns[k] = turns[k] + 2.0 * row
    others = (ac_check_ref[...], ac_bet_ref[...], fb_fold_ref[...], fb_call_ref[...])
    share_ac = action_share(others[0], others[1])
    share_fb = action_share(others[2], others[3])
    sign_sum, weight_sum = pair_sums(key_ref, 1, one_cols, *scratch)
    others = one_regrets(others, one_values(sign_sum, weight_sum, share_ac, share_fb))

    pre_cont, pre_fold = pre_step(pre_cont, pre_fold, sums_in_ref[1:2, :])
    one_now = one_range * action_share(pre_cont, pre_fold)
    pre_sum = pre_sum + 3.0 * one_now
    regrets = (root_check_ref[...], root_bet_ref[...], fc_fold_ref[...], fc_call_ref[...])
    share_root = action_share(regrets[0], regrets[1])
    share_fc = action_share(regrets[2], regrets[3])
    share_ac = action_share(others[0], others[1])
    share_fb = action_share(others[2], others[3])
    one_cols = one_columns(one_now * live, share_root, share_fc)
    two_cols = two_columns(two_all, share_ac, share_fb)
    for k, row in enumerate((*one_rows(one_cols), *two_rows(two_cols))):
        turns[k] = turns[k] + 3.0 * row
    sign_sum, weight_sum = pair_sums(key_ref, 2, {**two_cols, **one_cols}, *scratch)
    values = two_values(sign_sum, weight_sum, share_root, share_fc)
    cont_ref[...] = flop_value(share_ref[...], values[5])
    regrets = two_regrets(regrets, values)
    others = one_regrets(others, one_values(sign_sum, weight_sum, share_ac, share_fb))
    two_cols = two_columns(
        two_all, action_share(others[0], others[1]), action_share(others[2], others[3])
    )
    for k, row in enumerate(two_rows(two_cols)):
        turns[3 + k] = turns[3 + k] + 4.0 * row
    out_root_ref[...] = action_share(regrets[0], regrets[1])
    out_fc_ref[...] = action_share(regrets[2], regrets[3])
    for k in range(6):
        out_turn_ref[k] = turns[k]
    out_pre_ref[0:1, :] = pre_cont
    out_pre_ref[1:2, :] = pre_fold
    out_pre_ref[2:3, :] = pre_sum


def pair_scratch():
    return [
        pltpu.VMEM((16, H), jnp.float32),
        pltpu.VMEM((16, H), jnp.bfloat16),
        pltpu.VMEM((H, H), jnp.bfloat16),
        pltpu.VMEM((16, H), jnp.float32),
        pltpu.VMEM((16, H), jnp.float32),
    ]


def rows_of(*shapes):
    return [jax.ShapeDtypeStruct(shape, jnp.float32) for shape in shapes]


def solve(key_now, live, range_one, range_two, flop_share, compat, whole_sum):
    one_row = range_one.reshape(1, H)
    shared = (key_now, live, one_row, range_two.reshape(1, H), flop_share[:, None], compat)
    pair = (2, H)
    first = pl.pallas_call(
        first_kernel,
        out_shape=rows_of(*([pair] * 11), (6, 2, H)),
        scratch_shapes=pair_scratch(),
        name="first",
    )(*shared)
    second = pl.pallas_call(
        second_kernel,
        out_shape=rows_of((1, H), pair, pair, (6, 2, H), (3, H)),
        scratch_shapes=pair_scratch(),
        name="second",
    )(*shared, whole_sum(first[0]), *first[1:])
    cont_value, share_root, share_fc, turns, pre = second
    pre_cont, pre_fold = pre_step(pre[0:1], pre[1:2], whole_sum(cont_value))
    one_range = one_row * action_share(pre_cont, pre_fold)
    columns = one_columns(one_range * live, share_root, share_fc)
    last = jnp.concatenate([jnp.stack(one_rows(columns)) * 4.0, jnp.zeros((3, 2, H))])
    return jnp.swapaxes(turns + last, 0, 1), (pre[2:3] + 4.0 * one_range).reshape(H)


def spread_sum(x, axis):
    rows, width = x.shape
    return jnp.sum(sent_to_all(x.reshape(1, rows * width), axis), axis=0).reshape(rows, width)


def whole_sum(x):
    x = x + lax.ppermute(x, "grp_1", [(0, 1), (1, 0)])
    return spread_sum(spread_sum(x, FIRST_SUM), "inf_1")


def on_device(range_one, range_two, flop_weight, board_mask, runout, strength):
    groups = lax.axis_size(GRP)
    shards = lax.axis_size(INF)
    shard_id = lax.axis_index(INF)
    group_id = lax.axis_index(GRP)
    low_table, high_table = hand_cards(H, HANDS)
    low_all = jnp.asarray(low_table)
    high_all = jnp.asarray(high_table)
    capacity = strength.shape[0]
    hand_block = strength.shape[2]
    flop_total = 12.0 * FLOP_GRP * groups
    live_count = jnp.sum((flop_weight > 0).astype(jnp.int32), dtype=jnp.int32)
    counts = gathered_copies(live_count[None], GRP, 0)
    route_pair = slot_route(counts, group_id, FLOP_GRP, groups, capacity)
    arrived = sent_together(
        (
            place_rows(flop_weight, route_pair),
            place_rows(board_mask, route_pair),
            place_rows(runout, route_pair),
            place_rows(strength, route_pair),
        ),
        GRP,
        0,
        0,
        2,
    )
    weight = add_sources(arrived[0])
    board_rows = add_sources(arrived[1])
    run_cards = add_sources(arrived[2])
    key_rows = add_sources(arrived[3])
    local_count = key_rows.shape[0] // shards
    flop_keys, flop_board = side_by_side((key_rows, board_rows[:, None, :]), INF, 0, 2, 1)
    first_slot = shard_id * local_count
    runs_here = lax.dynamic_slice_in_dim(run_cards, first_slot, local_count, 0)
    weight_here = lax.dynamic_slice_in_dim(weight, first_slot, local_count, 0)

    flop_live = (flop_board[:, 0, :] == 1) & (jnp.arange(H) < HANDS)[None, :]
    keys = []
    for counter in range(ITERS - 1):
        turn_card = runs_here[:, counter, 0:1]
        river_card = runs_here[:, counter, 1:2]
        blocked = (low_all[None, :] == turn_card) | (low_all[None, :] == river_card)
        blocked = blocked | (high_all[None, :] == turn_card) | (high_all[None, :] == river_card)
        keys.append(jnp.where(flop_live & ~blocked, flop_keys[:, counter, :], -1))
    turn_sum, pre_sum = solve(
        jnp.stack(keys),
        flop_live.astype(jnp.float32),
        range_one,
        range_two,
        weight_here.astype(jnp.float32) / flop_total,
        compat_matrix(low_all, high_all),
        whole_sum,
    )
    pre_block = lax.dynamic_slice_in_dim(pre_sum, shard_id * hand_block, hand_block)
    total_weight = ITERS * (ITERS + 1) / 2.0
    turn_final = turn_sum / total_weight
    return (turn_final, pre_block / total_weight)


def solution(mesh):
    split = Mesh(mesh.devices.reshape(2, 2, 4, 8, 2), ("grp_0", "grp_1", "inf_0", "inf_1", "inf_2"))
    return jax.shard_map(
        on_device,
        mesh=split,
        in_specs=(P(), P(), P(GRP), P(GRP, INF), P(GRP, None, None), P(GRP, None, INF)),
        out_specs=(P(GRP_INF, None, None), P(INF)),
        check_vma=False,
    )
```

time: 308 us -> 145 us (0.47)
  blocking collectives: 115 us -> 34.9 us
  matrix products: 49.2 us -> 0 us
  Pallas kernels: 0 us -> 29.9 us
  other arithmetic: 38.1 us -> 11.4 us
  loops' own time: 23 us -> 0 us
  local copies, waits for them, and re-layouts: 42.2 us -> 20.1 us
  waiting for transfers between devices: 18.8 us -> 23.6 us
  starting transfers between devices: 19.8 us -> 23.3 us
    psum x15 -> x0, blocking collectives: 115 us -> none  [one_axis_at_a_time(): x = lax.psum(x, axis)]
    dot_general x66 -> x0, matrix products: 49.2 us -> none  [the longest x33 30.7 us: pair_values(): jnp.einsum('smo,sco->scm', sign_mat, other_cols, preferred_element_type=j...]
    all_to_all x0 -> x3, blocking collectives: none -> 34.9 us  [sent_to_all(): return lax.all_to_all(copies, axis, split_axis=0, concat_axis=0, tiled=True)]
    pallas_call x0 -> x3, Pallas kernels: none -> 29.9 us  [the longest x1 12.6 us: solve(): pl.pallas_call(first_kernel, out_shape=rows_of(*[pair] * 11, (6, 2, H)),...]
    and x33 -> x0, other arithmetic: 29.5 us -> none  [pair_values(): compat & (my_high[:, None] != other_low[None, :])]
    dynamic_slice x132 -> x0, local copies, waits for them, and re-layouts: 25 us -> none  [the longest x33 19.5 us: whole_values(): lax.scan(add_block, (zero_sums, zero_sums), jnp.arange(H // 128))]
    another operation x3 -> x0, loops' own time: 23 us -> none  [whole_values(): lax.scan(add_block, (zero_sums, zero_sums), jnp.arange(H // 128))]
    all_to_all x1 -> x2, waiting for transfers between devices: 2.18 us -> 10.3 us  [sent_to_all(): return lax.all_to_all(copies, axis, split_axis=0, concat_axis=0, tiled=True)]
  transfers between devices with their start and end apart: 3 -> 6, of which waited for: 3 -> 6; matrix products, arithmetic and copies ran while one was open for 1% -> 3% of each run, Pallas kernels for 0% -> 3%
where the time goes in v1:
time: 145 us; the launch traced here: 144 us
  blocking collectives  34.9 us (24%)
  Pallas kernels  29.9 us (21%)
  waiting for transfers between devices  23.6 us (16%)
  starting transfers between devices  23.3 us (16%)
  local copies, waits for them, and re-layouts  20.1 us (14%)
  other arithmetic  11.4 us (8%)
    all_to_all x3, blocking collectives, sent_to_all(): return lax.all_to_all(copies, axis, split_axis=0, concat_axis=0, tiled=True)  34.9 us
    pallas_call x1, Pallas kernels, solve(): pl.pallas_call(first_kernel, out_shape=rows_of(*[pair] * 11, (6, 2, H)),...  12.6 us
    pallas_call x1, Pallas kernels, solve(): pl.pallas_call(second_kernel, out_shape=rows_of((1, H), pair, pair, (6, 2...  12.3 us
    all_to_all x1, starting transfers between devices, side_by_side(): lax.all_to_all(both, axis, split_axis=split_dim, concat_axis=concat_dim,...  12.1 us
    all_to_all x2, waiting for transfers between devices, sent_to_all(): return lax.all_to_all(copies, axis, split_axis=0, concat_axis=0, tiled=True)  10.3 us
    gather x9, local copies, waits for them, and re-layouts, place_rows(): jnp.take(member, source, axis=0)  9.57 us
    all_to_all x1, waiting for transfers between devices, side_by_side(): lax.all_to_all(both, axis, split_axis=split_dim, concat_axis=concat_dim,...  9.42 us
    all_to_all x2, starting transfers between devices, sent_to_all(): return lax.all_to_all(copies, axis, split_axis=0, concat_axis=0, tiled=True)  7.64 us
  transfers between devices with their start and end apart: 6, of which 6 were waited for; matrix products, arithmetic and copies ran while one was open for 3% of the time, Pallas kernels for 3%

profile of v1, /device:TPU:8, one launch (start us, length us, event | category | flops | bytes accessed | tf_op | source)
XLA Modules:
  0.0 144.2 jit_solution(3044038895398529144)
XLA Ops:
  0.6 1.3 fusion.6
  1.9 1.2 broadcast_in_dim.140
  3.2 4.3 %all-to-all-start = ((s32[4,1,1]{2,1,0:T(1,128)}), s32[4,1,1]{2,1,0:T(1,128)S(1)}, u32[]{:S(2)}, u32[]{:S(2)}) async-start(s32[4,1,1]{2,1,0:T(1,128)} %broadcast_in_dim.140), calls=%async_computation | async-start | bytes 4096 | tf_op jit(solution)/shard_map/all_to_all | solution.py:27
  7.5 0.8 copy.70
  8.4 0.9 copy.72
  9.3 1.1 copy.74
  10.4 2.3 %all-to-all-done = s32[4,1,1]{2,1,0:T(1,128)S(1)} async-done(((s32[4,1,1]{2,1,0:T(1,128)}), s32[4,1,1]{2,1,0:T(1,128)S(1)}, u32[]{:S(2)}, u32[]{:S(2)}) %all-to-all-start) | async-done | bytes 48 | tf_op jit(solution)/shard_map/all_to_all | solution.py:27
  12.8 0.6 fusion.14
  13.6 0.6 iota_compare_fusion.1
  14.5 0.3 select_reduce_fusion
  14.8 3.6 %gather_fusion = s32[512]{0:T(512)S(1)} fusion(s32[256]{0:T(256)} %param.10, s32[1024]{0:T(1024)S(1)} %pad_clamp_fusion), kind=kCustom, calls=%fused_computation | custom fusion | bytes 6144 | tf_op jit(solution)/shard_map/jit(_take)/gather | solution.py:99
  18.4 1.0 gather_fusion.1
  19.6 2.1 %gather_fusion.2 = s32[512,4,2]{1,2,0:T(2,128)S(1)} fusion(s32[256,4,2]{1,2,0:T(2,128)S(1)} %copy.72, s32[1024]{0:T(1024)S(1)} %pad_clamp_fusion), kind=kCustom, calls=%fused_computation.2 | custom fusion | bytes 34816 | tf_op jit(solution)/shard_map/jit(_take)/gather | solution.py:99
  21.9 2.1 %gather_fusion.3 = s32[512,4,22]{2,1,0:T(4,128)S(1)} fusion(s32[256,4,22]{2,1,0:T(4,128)S(1)} %copy.74, s32[1024]{0:T(1024)S(1)} %pad_clamp_fusion), kind=kCustom, calls=%fused_computation.3 | custom fusion | bytes 362496 | tf_op jit(solution)/shard_map/jit(_take)/gather | solution.py:99
  24.0 0.4 copy.75
  24.6 0.7 copy.76
  25.3 3.4 %all-to-all-start.1 = ((s32[4,128,119]{1,2,0:T(8,128)}), s32[4,128,119]{1,2,0:T(8,128)S(1)}, u32[]{:S(2)}, u32[]{:S(2)}) async-start(s32[4,128,119]{1,2,0:T(8,128)} %copy.76), calls=%async_computation.1 | async-start | bytes 491520 | tf_op jit(solution)/shard_map/all_to_all | solution.py:46
  28.7 0.6 reshape.971.two_ref
  29.3 0.6 reshape.970.one_ref
  29.9 5.0 %compat.1.compat_ref = bf16[1408,1408]{1,0:T(8,128)(2,1)} custom-call(s32[1,1408]{1,0:T(1,128)} %constant.133.low_ref, s32[1,1408]{1,0:T(1,128)} %constant.134.high_ref), custom_call_target="tpu_custom_call" | custom-call | tf_op jit(solution)/shard_map/compat/pallas_call | solution.py:130
  34.9 1.1 all-to-all-done.1
  36.1 0.7 copy.83.share_ref
  36.8 0.2 copy.77
  37.1 0.9 reshape.1009
  38.0 12.1 %all-to-all-start.2 = ((s32[64,1,220]{2,1,0:T(1,128)}), s32[64,1,220]{2,1,0:T(1,128)S(1)}, u32[]{:S(2)}, u32[]{:S(2)}) async-start(s32[64,1,220]{2,1,0:T(1,128)} %reshape.1009), calls=%async_computation.2 | async-start | bytes 131072 | tf_op jit(solution)/shard_map/all_to_all | solution.py:56
  50.3 9.4 %all-to-all-done.2 = s32[64,1,220]{2,1,0:T(1,128)S(1)} async-done(((s32[64,1,220]{2,1,0:T(1,128)}), s32[64,1,220]{2,1,0:T(1,128)S(1)}, u32[]{:S(2)}, u32[]{:S(2)}) %all-to-all-start.2) | async-done | bytes 56352 | tf_op jit(solution)/shard_map/all_to_all | solution.py:56
  59.7 0.5 broadcast.760
  60.2 0.8 reduce.12
  61.3 0.3 all_to_all.37
  61.6 0.6 fusion.2
  62.3 0.6 pad_add_fusion.2.key_ref
  63.0 12.6 %first.1 = (f32[2,1408]{1,0:T(2,128)}, f32[2,1408]{1,0:T(2,128)}, f32[2,1408]{1,0:T(2,128)}, f32[2,1408]{1,0:T(2,128)}, f32[2,1408]{1,0:T(2,128)}, /*index=5*/f3...) custom-call(s32[3,2,1408]{2,1,0:T(2,128)} %pad_add_fusion.2.key_ref,, ...), custom_call_target="tpu_custom_call" | custom-call | tf_op jit(solution)/shard_map/first/pallas_call | solution.py:364
  75.6 1.4 collective-permute-done
  77.0 0.7 add.151
  77.8 13.0 %all_to_all.49 = f32[16,1,2816]{2,1,0:T(1,128)S(1)} all-to-all(f32[16,1,2816]{2,1,0:T(1,128)S(1)} %broadcast_in_dim.162), channel_id=1, replica_groups=mesh['grp_0'=2,'grp_1'=2,'inf_0'=4,'inf_1'=8,'inf_2'=2] {'grp_0','inf_0'..., dimensions={0} | all-to-all | bytes 360448 | tf_op jit(solution)/shard_map/all_to_all | solution.py:27
  91.0 11.0 %all_to_all.50 = f32[8,1,2816]{2,1,0:T(1,128)S(1)} all-to-all(f32[8,1,2816]{2,1,0:T(1,128)S(1)} %broadcast_in_dim.163), channel_id=1, replica_groups=mesh['grp_0'=2,'grp_1'=2,'inf_0'=4,'inf_1'=8,'inf_2'=2] {'inf_1'}, dimensions={0} | all-to-all | bytes 180224 | tf_op jit(solution)/shard_map/all_to_all | solution.py:27
  102.1 0.6 reshape.973.sums_in_ref
  102.7 12.3 %second.1 = (f32[1,1408]{1,0:T(1,128)}, f32[2,1408]{1,0:T(2,128)}, f32[2,1408]{1,0:T(2,128)}, f32[6,2,1408]{2,1,0:T(2,128)}, f32[3,1408]{1,0:T(4,128)}) custom-call(s32[3,2,1408]{2,1,0:T(2,128)} %pad_add_fusion.2.key_ref, f32[2,1408]{1,0:T(2,128)} %get-tuple-element.38.live_ref, f32[1,1408]{1,0:T(1,128)} %reshape.970.one_ref, f32[1,1408]{1,0:T(1,128)} %reshape.971.two_ref, ...), custom_call_target="tpu_custom_call" | custom-call | tf_op jit(solution)/shard_map/second/pallas_call | solution.py:370
  115.1 1.4 collective-permute-done.1
  116.5 0.7 add_reduce_fusion
  117.3 10.9 %all_to_all.51 = f32[16,1,1408]{2,1,0:T(1,128)S(1)} all-to-all(f32[16,1,1408]{2,1,0:T(1,128)S(1)} %broadcast_in_dim.164), channel_id=1, replica_groups=mesh['grp_0'=2,'grp_1'=2,'inf_0'=4,'inf_1'=8,'inf_2'=2] {'grp_0','inf_0'..., dimensions={0} | all-to-all | bytes 180224 | tf_op jit(solution)/shard_map/all_to_all | solution.py:27
  128.2 0.6 broadcast_in_dim.165
  128.9 3.3 %all-to-all-start.6 = ((f32[8,1,1408]{2,1,0:T(1,128)}), f32[8,1,1408]{2,1,0:T(1,128)S(1)}, u32[]{:S(2)}, u32[]{:S(2)}) async-start(f32[8,1,1408]{2,1,0:T(1,128)} %broadcast_in_dim.165), calls=%async_computation.6 | async-start | bytes 90112 | tf_op jit(solution)/shard_map/all_to_all | solution.py:27
  132.2 8.1 %all-to-all-done.6 = f32[8,1,1408]{2,1,0:T(1,128)S(1)} async-done(((f32[8,1,1408]{2,1,0:T(1,128)}), f32[8,1,1408]{2,1,0:T(1,128)S(1)}, u32[]{:S(2)}, u32[]{:S(2)}) %all-to-all-start.6) | async-done | bytes 45088 | tf_op jit(solution)/shard_map/all_to_all | solution.py:27
  140.3 0.9 fusion.17
  141.2 0.7 fusion.16
  142.0 1.6 %multiply_bitcast_fusion = f32[2,6,1408]{2,0,1:T(2,128)} fusion(f32[6,2,1408]{2,1,0:T(2,128)} %get-tuple-element.31, f32[3,2,1408]{2,1,0:T(2,128)S(1)} %maximum_multiply_fusion), kind=kLoop, calls=%fused_computation.10 | loop fusion | flops 33792 | bytes 168960 | tf_op jit(solution)/shard_map/div | solution.py:449
  143.6 0.6 fusion.15
  (50 shorter events, 2.4 us)
Async XLA Ops:
  3.2 9.5 %all-to-all-start = ((s32[4,1,1]{2,1,0:T(1,128)}), s32[4,1,1]{2,1,0:T(1,128)S(1)}, u32[]{:S(2)}, u32[]{:S(2)}) async-start(s32[4,1,1]{2,1,0:T(1,128)} %broadcast_in_dim.140), calls=%async_computation | async-start | bytes 4096 | tf_op jit(solution)/shard_map/all_to_all | solution.py:27
  19.6 9.1 %copy-start.3 = (f32[1408]{0:T(1024)S(1)}, f32[1408]{0:T(1024)}, u32[]{:S(2)}) copy-start(f32[1408]{0:T(1024)} %param.9) | copy-start | bytes 16900
  19.6 9.7 %copy-start = (f32[1408]{0:T(1024)S(1)}, f32[1408]{0:T(1024)}, u32[]{:S(2)}) copy-start(f32[1408]{0:T(1024)} %param.8) | copy-start | bytes 16900
  25.3 10.7 %all-to-all-start.1 = ((s32[4,128,119]{1,2,0:T(8,128)}), s32[4,128,119]{1,2,0:T(8,128)S(1)}, u32[]{:S(2)}, u32[]{:S(2)}) async-start(s32[4,128,119]{1,2,0:T(8,128)} %copy.76), calls=%async_computation.1 | async-start | bytes 491520 | tf_op jit(solution)/shard_map/all_to_all | solution.py:46
  29.9 32.3 %copy-start.1 = (s32[1408]{0:T(1024)S(1)}, s32[1408]{0:T(1024)}, u32[]{:S(2)}) copy-start(s32[1408]{0:T(1024)} %constant.128.clone) | copy-start | bytes 16900
  29.9 32.3 %copy-start.2 = (s32[1408]{0:T(1024)S(1)}, s32[1408]{0:T(1024)}, u32[]{:S(2)}) copy-start(s32[1408]{0:T(1024)} %constant.127.clone) | copy-start | bytes 16900
  38.0 21.7 %all-to-all-start.2 = ((s32[64,1,220]{2,1,0:T(1,128)}), s32[64,1,220]{2,1,0:T(1,128)S(1)}, u32[]{:S(2)}, u32[]{:S(2)}) async-start(s32[64,1,220]{2,1,0:T(1,128)} %reshape.1009), calls=%async_computation.2 | async-start | bytes 131072 | tf_op jit(solution)/shard_map/all_to_all | solution.py:56
  75.6 1.4 %collective-permute-start = (f32[2,1408]{1,0:T(2,128)}, f32[2,1408]{1,0:T(2,128)S(1)}, u32[]{:S(2)}, u32[]{:S(2)}) collective-permute-start(f32[2,1408]{1,0:T(2,128)} %get-tuple-element.19), channel_id=1, source_target_pairs={{0,64},{64,0},{1,65},{65,1},{2,66},{66,2},{3,67},{67,3},{4,68},{68... | collective-permute-start | bytes 33800 | tf_op jit(solution)/shard_map/ppermute | solution.py:390
  115.1 1.4 collective-permute-start.1
  128.9 11.4 %all-to-all-start.6 = ((f32[8,1,1408]{2,1,0:T(1,128)}), f32[8,1,1408]{2,1,0:T(1,128)S(1)}, u32[]{:S(2)}, u32[]{:S(2)}) async-start(f32[8,1,1408]{2,1,0:T(1,128)} %broadcast_in_dim.165), calls=%async_computation.6 | async-start | bytes 90112 | tf_op jit(solution)/shard_map/all_to_all | solution.py:27

commit v2 on v1

v2 whole, which is shorter than its diff:
```python
import jax
import jax.numpy as jnp
import numpy as np
from jax import lax
from jax.experimental import pallas as pl
from jax.experimental.pallas import tpu as pltpu
from jax.sharding import Mesh
from jax.sharding import PartitionSpec as P

HANDS = 1326
H = 1408
ITERS = 4
FLOP_GRP = 128
GRP = ("grp_0", "grp_1")
INF = ("inf_0", "inf_1", "inf_2")
GRP_INF = ("grp_0", "grp_1", "inf_0", "inf_1", "inf_2")


EPSILON = 0.01
FOLD_VALUE = -0.1


def sent_to_all(x, axis):
    copies = jnp.broadcast_to(x, (lax.axis_size(axis), *x.shape))
    return lax.all_to_all(copies, axis, split_axis=0, concat_axis=0, tiled=True)


def hand_cards(slot_total, real_total):
    low_list = []
    high_list = []
    for first_card in range(52):
        for second_card in range(first_card + 1, 52):
            low_list.append(first_card)
            high_list.append(second_card)
    low_table = np.full(slot_total, 52, np.int32)
    high_table = np.full(slot_total, 53, np.int32)
    used_count = min(slot_total, real_total)
    low_table[:used_count] = np.array(low_list[:used_count], np.int32)
    high_table[:used_count] = np.array(high_list[:used_count], np.int32)
    return (low_table, high_table)


def action_share(first_regret, second_regret):
    return (first_regret + EPSILON) / (first_regret + second_regret + 2.0 * EPSILON)


SCALE = 1.0 / HANDS
FLOP_TOTAL = 12.0 * FLOP_GRP * 4
LINE = 128
PART = 256
BLOCK = 128
WIDE = 256
DEEP = 256
PADDED = 1536
FIRST_SUM = ("grp_1", "inf_0", "inf_2")
SECOND_SUM = ("grp_0", "inf_1")


def compat_kernel(low_ref, high_ref, out_ref):
    def rows(step, carry):
        first = pl.multiple_of(step * BLOCK, BLOCK)
        low_col = jnp.broadcast_to(low_ref[:, pl.ds(first, BLOCK)], (BLOCK, BLOCK)).T
        high_col = jnp.broadcast_to(high_ref[:, pl.ds(first, BLOCK)], (BLOCK, BLOCK)).T
        for start in range(0, PADDED, BLOCK):
            low_here = low_ref[:, start : start + BLOCK]
            high_here = high_ref[:, start : start + BLOCK]
            apart = (low_col != low_here) & (low_col != high_here)
            apart = apart & (high_col != low_here) & (high_col != high_here)
            out_ref[pl.ds(first, BLOCK), start : start + BLOCK] = jnp.where(
                apart, 1.0, 0.0
            ).astype(jnp.bfloat16)
        return carry

    lax.fori_loop(0, H // BLOCK, rows, 0)


def compat_matrix(low, high):
    return pl.pallas_call(
        compat_kernel,
        out_shape=jax.ShapeDtypeStruct((H, PADDED), jnp.bfloat16),
        name="compat",
    )(low, high)


def pair_sums(key_ref, counter, columns, compat_ref, lhs_ref, low_ref, sums_ref, col_ref):
    alive = (key_ref[counter, :, :H] >= 0).astype(jnp.float32)
    lhs_ref[...] = jnp.zeros((16, H), jnp.float32)
    for k, column in columns.items():
        lhs_ref[2 * k : 2 * k + 2, :] = column * alive
    low_ref[...] = lhs_ref[...].astype(jnp.bfloat16)

    def key_column(step, carry):
        first = pl.multiple_of(step * BLOCK, BLOCK)
        for flop in range(2):
            keys = key_ref[counter, flop : flop + 1, pl.ds(first, BLOCK)]
            col_ref[flop, pl.ds(first, BLOCK), :] = jnp.broadcast_to(keys, (BLOCK, BLOCK)).T
        return carry

    lax.fori_loop(0, H // BLOCK, key_column, 0)

    def mine(step, carry):
        start = pl.multiple_of(step * WIDE, WIDE)
        weight_total = jnp.zeros((16, WIDE), jnp.float32)
        totals = [jnp.zeros((16, WIDE), jnp.float32) for flop in range(2)]
        rows = [key_ref[counter, flop : flop + 1, pl.ds(start, WIDE)] for flop in range(2)]
        for first in range(0, H, DEEP):
            depth = min(DEEP, H - first)
            lhs = low_ref[:, first : first + depth]
            most = compat_ref[first : first + depth, pl.ds(start, WIDE)]
            least = -most
            weight_total = weight_total + jnp.dot(lhs, most, preferred_element_type=jnp.float32)
            for flop in range(2):
                parts = []
                key_col = col_ref[flop, first : first + depth, :]
                for lane in range(0, WIDE, BLOCK):
                    gap = rows[flop][:, lane : lane + BLOCK] - key_col
                    parts.append(gap.astype(jnp.float32).astype(jnp.bfloat16))
                sign = jnp.concatenate(parts, axis=1) if len(parts) > 1 else parts[0]
                sign = jnp.minimum(jnp.maximum(sign, least), most)
                totals[flop] = totals[flop] + jnp.dot(
                    lhs, sign, preferred_element_type=jnp.float32
                )
        row_flop = lax.broadcasted_iota(jnp.int32, (16, WIDE), 0) & 1
        sums_ref[0, :, pl.ds(start, WIDE)] = jnp.where(row_flop == 0, totals[0], totals[1])
        sums_ref[1, :, pl.ds(start, WIDE)] = weight_total
        return carry

    lax.fori_loop(0, PADDED // WIDE, mine, 0)
    sign_sum = {k: sums_ref[0, 2 * k : 2 * k + 2, :H] * alive for k in columns}
    weight_sum = {k: sums_ref[1, 2 * k : 2 * k + 2, :H] * alive for k in columns}
    return sign_sum, weight_sum


def two_values(sign_sum, weight_sum, share_root, share_fc):
    v_cc = 0.5 * SCALE * sign_sum[1]
    v_cbf = -0.5 * SCALE * (weight_sum[0] - weight_sum[1])
    v_cbc = 1.5 * SCALE * (sign_sum[0] - sign_sum[1])
    v_bf = 0.5 * SCALE * weight_sum[2]
    v_bc = 1.5 * SCALE * (sign_sum[0] - sign_sum[2])
    u_fc = share_fc * v_cbf + (1.0 - share_fc) * v_cbc
    v_check = v_cc + u_fc
    v_bet = v_bf + v_bc
    u_root = share_root * v_check + (1.0 - share_root) * v_bet
    return v_cbf, v_cbc, u_fc, v_check, v_bet, u_root


def one_values(sign_sum, weight_sum, share_ac, share_fb):
    w_cc = 0.5 * SCALE * sign_sum[4]
    w_cbf = 0.5 * SCALE * weight_sum[5]
    w_cbc = 1.5 * SCALE * (sign_sum[4] - sign_sum[5])
    w_bf = -0.5 * SCALE * (weight_sum[3] - weight_sum[4])
    w_bc = 1.5 * SCALE * (sign_sum[3] - sign_sum[4])
    x_bet = w_cbf + w_cbc
    u_ac = share_ac * w_cc + (1.0 - share_ac) * x_bet
    u_fb = share_fb * w_bf + (1.0 - share_fb) * w_bc
    return w_cc, x_bet, u_ac, w_bf, w_bc, u_fb


def two_regrets(regrets, values):
    root_check, root_bet, fc_fold, fc_call = regrets
    v_cbf, v_cbc, u_fc, v_check, v_bet, u_root = values
    return (
        jnp.maximum(root_check + v_check - u_root, 0.0),
        jnp.maximum(root_bet + v_bet - u_root, 0.0),
        jnp.maximum(fc_fold + v_cbf - u_fc, 0.0),
        jnp.maximum(fc_call + v_cbc - u_fc, 0.0),
    )


def one_regrets(regrets, values):
    ac_check, ac_bet, fb_fold, fb_call = regrets
    w_cc, x_bet, u_ac, w_bf, w_bc, u_fb = values
    return (
        jnp.maximum(ac_check + w_cc - u_ac, 0.0),
        jnp.maximum(ac_bet + x_bet - u_ac, 0.0),
        jnp.maximum(fb_fold + w_bf - u_fb, 0.0),
        jnp.maximum(fb_call + w_bc - u_fb, 0.0),
    )


def pre_step(pre_cont, pre_fold, cont_value):
    share_pre = action_share(pre_cont, pre_fold)
    u_pre = share_pre * cont_value + (1.0 - share_pre) * FOLD_VALUE
    return (
        jnp.maximum(pre_cont + cont_value - u_pre, 0.0),
        jnp.maximum(pre_fold + FOLD_VALUE - u_pre, 0.0),
    )


def one_columns(one_all, share_root, share_fc):
    one_check = one_all * share_root
    return {3: one_all, 4: one_check, 5: one_check * share_fc}


def two_columns(two_all, share_ac, share_fb):
    return {0: two_all, 1: two_all * share_ac, 2: two_all * share_fb}


def one_rows(columns):
    return columns[4], columns[3] - columns[4], columns[4] - columns[5]


def two_rows(columns):
    return columns[1], columns[0] - columns[2], columns[0] - columns[1]


def flop_value(share, u_root):
    part = share * u_root
    return part[0:1, :] + part[1:2, :]


def add_parts(parts_ref, start):
    total = parts_ref[0, :, start : start + H]
    for k in range(1, parts_ref.shape[0]):
        total = total + parts_ref[k, :, start : start + H]
    return total


def spread(copies_ref, start, value):
    for k in range(copies_ref.shape[0]):
        copies_ref[k, :, start : start + H] = value


def read_flops(arrived_ref, low_ref, high_ref, key_ref, live_ref, share_ref):
    used = key_ref.shape[0]
    shards = arrived_ref.shape[0]
    hand_block = H // shards
    for shard in range(shards):
        line = arrived_ref[shard] - 1
        for flop in range(2):
            for counter in range(used):
                first = LINE * flop + hand_block * counter
                key_ref[
                    counter, flop : flop + 1, hand_block * shard : hand_block * (shard + 1)
                ] = line[:, first : first + hand_block]
    live_ref[...] = (key_ref[0, :, :H] >= 0).astype(jnp.float32)
    low = low_ref[...]
    high = high_ref[...]
    for flop in range(2):
        first = LINE * flop + hand_block * used
        extra = arrived_ref[0, :, first : first + 1 + 2 * used]
        share_ref[flop : flop + 1, :] = extra[:, 0:1].astype(jnp.float32) / FLOP_TOTAL
        for counter in range(used):
            turn = extra[:, 1 + 2 * counter : 2 + 2 * counter]
            river = extra[:, 2 + 2 * counter : 3 + 2 * counter]
            blocked = (low == turn) | (low == river) | (high == turn) | (high == river)
            blocked = blocked | (lax.broadcasted_iota(jnp.int32, (1, PADDED), 1) >= H)
            row = key_ref[counter, flop : flop + 1, :]
            key_ref[counter, flop : flop + 1, :] = jnp.where(blocked, -1, row)


def first_kernel(
    arrived_ref, low_ref, high_ref, one_ref, two_ref, compat_ref,
    key_ref, live_ref, share_ref, cont_ref,
    root_check_ref, root_bet_ref, fc_fold_ref, fc_call_ref,
    ac_check_ref, ac_bet_ref, fb_fold_ref, fb_call_ref, share_root_ref, share_fc_ref, turn_ref,
    lhs_ref, low_part_ref, sums_ref, col_ref,
):
    scratch = (compat_ref, lhs_ref, low_part_ref, sums_ref, col_ref)
    read_flops(arrived_ref, low_ref, high_ref, key_ref, live_ref, share_ref)
    live = live_ref[...]
    share = share_ref[...]
    zero = jnp.zeros((2, H), jnp.float32)
    zero_row = jnp.zeros((1, H), jnp.float32)
    two_all = two_ref[...] * live
    start = action_share(zero, zero)
    one_all = one_ref[...] * action_share(zero_row, zero_row) * live
    one_cols = one_columns(one_all, start, start)
    two_cols = two_columns(two_all, start, start)
    sign_sum, weight_sum = pair_sums(key_ref, 0, {**two_cols, **one_cols}, *scratch)
    values = two_values(sign_sum, weight_sum, start, start)
    spread(cont_ref, 0, flop_value(share, values[5]))
    regrets = two_regrets((zero, zero, zero, zero), values)
    others = one_regrets((zero, zero, zero, zero), one_values(sign_sum, weight_sum, start, start))
    turns = [*one_rows(one_cols), *two_rows(two_cols)]

    share_root = action_share(regrets[0], regrets[1])
    share_fc = action_share(regrets[2], regrets[3])
    two_cols = two_columns(
        two_all, action_share(others[0], others[1]), action_share(others[2], others[3])
    )
    sign_sum, weight_sum = pair_sums(key_ref, 1, two_cols, *scratch)
    values = two_values(sign_sum, weight_sum, share_root, share_fc)
    spread(cont_ref, H, flop_value(share, values[5]))
    regrets = two_regrets(regrets, values)
    for k, row in enumerate(two_rows(two_cols)):
        turns[3 + k] = turns[3 + k] + 2.0 * row
    root_check_ref[...], root_bet_ref[...], fc_fold_ref[...], fc_call_ref[...] = regrets
    ac_check_ref[...], ac_bet_ref[...], fb_fold_ref[...], fb_call_ref[...] = others
    share_root_ref[...] = share_root
    share_fc_ref[...] = share_fc
    for k in range(6):
        turn_ref[k] = turns[k]


def second_kernel(
    key_ref, live_ref, one_ref, two_ref, share_ref, compat_ref, sums_in_ref,
    root_check_ref, root_bet_ref, fc_fold_ref, fc_call_ref,
    ac_check_ref, ac_bet_ref, fb_fold_ref, fb_call_ref, share_root_ref, share_fc_ref, turn_ref,
    cont_ref, out_root_ref, out_fc_ref, out_turn_ref, out_pre_ref,
    lhs_ref, low_ref, sums_ref, col_ref,
):
    scratch = (compat_ref, lhs_ref, low_ref, sums_ref, col_ref)
    live = live_ref[...]
    zero_row = jnp.zeros((1, H), jnp.float32)
    two_all = two_ref[...] * live
    one_range = one_ref[...]
    turns = [turn_ref[k] for k in range(6)]
    pre_sum = one_range * action_share(zero_row, zero_row)
    pre_cont, pre_fold = pre_step(zero_row, zero_row, add_parts(sums_in_ref, 0))
    one_now = one_range * action_share(pre_cont, pre_fold)
    pre_sum = pre_sum + 2.0 * one_now
    one_cols = one_columns(one_now * live, share_root_ref[...], share_fc_ref[...])
    for k, row in enumerate(one_rows(one_cols)):
        turns[k] = turns[k] + 2.0 * row
    others = (ac_check_ref[...], ac_bet_ref[...], fb_fold_ref[...], fb_call_ref[...])
    share_ac = action_share(others[0], others[1])
    share_fb = action_share(others[2], others[3])
    sign_sum, weight_sum = pair_sums(key_ref, 1, one_cols, *scratch)
    others = one_regrets(others, one_values(sign_sum, weight_sum, share_ac, share_fb))

    pre_cont, pre_fold = pre_step(pre_cont, pre_fold, add_parts(sums_in_ref, H))
    one_now = one_range * action_share(pre_cont, pre_fold)
    pre_sum = pre_sum + 3.0 * one_now
    regrets = (root_check_ref[...], root_bet_ref[...], fc_fold_ref[...], fc_call_ref[...])
    share_root = action_share(regrets[0], regrets[1])
    share_fc = action_share(regrets[2], regrets[3])
    share_ac = action_share(others[0], others[1])
    share_fb = action_share(others[2], others[3])
    one_cols = one_columns(one_now * live, share_root, share_fc)
    two_cols = two_columns(two_all, share_ac, share_fb)
    for k, row in enumerate((*one_rows(one_cols), *two_rows(two_cols))):
        turns[k] = turns[k] + 3.0 * row
    sign_sum, weight_sum = pair_sums(key_ref, 2, {**two_cols, **one_cols}, *scratch)
    values = two_values(sign_sum, weight_sum, share_root, share_fc)
    spread(cont_ref, 0, flop_value(share_ref[...], values[5]))
    regrets = two_regrets(regrets, values)
    others = one_regrets(others, one_values(sign_sum, weight_sum, share_ac, share_fb))
    two_cols = two_columns(
        two_all, action_share(others[0], others[1]), action_share(others[2], others[3])
    )
    for k, row in enumerate(two_rows(two_cols)):
        turns[3 + k] = turns[3 + k] + 4.0 * row
    out_root_ref[...] = action_share(regrets[0], regrets[1])
    out_fc_ref[...] = action_share(regrets[2], regrets[3])
    for k in range(6):
        out_turn_ref[k] = turns[k]
    out_pre_ref[0:1, :] = pre_cont
    out_pre_ref[1:2, :] = pre_fold
    out_pre_ref[2:3, :] = pre_sum


def pair_scratch():
    return [
        pltpu.VMEM((16, H), jnp.float32),
        pltpu.VMEM((16, H), jnp.bfloat16),
        pltpu.VMEM((2, 16, PADDED), jnp.float32),
        pltpu.VMEM((2, H, BLOCK), jnp.int32),
    ]


def rows_of(*shapes):
    return [jax.ShapeDtypeStruct(shape, jnp.float32) for shape in shapes]


def last_kernel(
    live_ref, one_ref, sums_in_ref, share_root_ref, share_fc_ref, turn_ref, pre_ref,
    out_ref, pre_out_ref,
):
    total_weight = ITERS * (ITERS + 1) / 2.0
    pre_cont, pre_fold = pre_step(pre_ref[0:1, :], pre_ref[1:2, :], add_parts(sums_in_ref, 0))
    one_now = one_ref[...] * action_share(pre_cont, pre_fold)
    columns = one_columns(one_now * live_ref[...], share_root_ref[...], share_fc_ref[...])
    for k, row in enumerate(one_rows(columns)):
        out_ref[k] = (turn_ref[k] + 4.0 * row) / total_weight
    for k in range(3, 6):
        out_ref[k] = turn_ref[k] / total_weight
    pre_out_ref[...] = (pre_ref[2:3, :] + 4.0 * one_now) / total_weight


def solve(arrived, range_one, range_two, low, high, compat):
    one_row = range_one.reshape(1, H)
    two_row = range_two.reshape(1, H)
    pair = (2, H)
    first_count = lax.axis_size(FIRST_SUM)
    key_now, live, share, cont, *state = pl.pallas_call(
        first_kernel,
        out_shape=[
            jax.ShapeDtypeStruct((ITERS - 1, 2, PADDED), jnp.int32),
            *rows_of(pair, (2, 1), (first_count, 1, 2 * H), *([pair] * 10), (6, 2, H)),
        ],
        scratch_shapes=pair_scratch(),
        name="first",
    )(arrived, low, high, one_row, two_row, compat)
    parts = whole_parts(cont)
    cont, share_root, share_fc, turns, pre = pl.pallas_call(
        second_kernel,
        out_shape=rows_of((first_count, 1, H), pair, pair, (6, 2, H), (3, H)),
        scratch_shapes=pair_scratch(),
        name="second",
    )(key_now, live, one_row, two_row, share, compat, parts, *state)
    parts = whole_parts(cont)
    turns, pre = pl.pallas_call(
        last_kernel,
        out_shape=rows_of((6, 2, H), (1, H)),
        name="last",
    )(live, one_row, parts, share_root, share_fc, turns, pre)
    return jnp.swapaxes(turns, 0, 1), pre.reshape(H)


def exchanged(copies, axis):
    return lax.all_to_all(copies, axis, split_axis=0, concat_axis=0, tiled=True)


def whole_parts(copies):
    part = jnp.sum(exchanged(copies, FIRST_SUM), axis=0)
    return sent_to_all(part, SECOND_SUM)


ROWS = 80


def pack_kernel(first_hand_ref, strength_ref, board_ref, weight_ref, cards_ref, out_ref):
    groups, rows, capacity = out_ref.shape
    hand_block = strength_ref.shape[0]
    used = ITERS - 1
    hand = first_hand_ref[0, 0] + lax.broadcasted_iota(jnp.int32, (hand_block, capacity), 0)
    flop_live = (board_ref[...] == 1) & (hand < HANDS)
    extra = used * hand_block
    for group in range(groups):
        for counter in range(used):
            out_ref[group, hand_block * counter : hand_block * (counter + 1), :] = jnp.where(
                flop_live, strength_ref[:, counter, :] + 1, 0
            )
        out_ref[group, extra : extra + 1, :] = weight_ref[...]
        for counter in range(used):
            row = extra + 1 + 2 * counter
            out_ref[group, row : row + 2, :] = cards_ref[counter]
        blank = extra + 1 + 2 * used
        out_ref[group, blank:, :] = jnp.zeros((rows - blank, capacity), jnp.int32)


def packed(first_hand, strength, board_mask, flop_weight, runout, groups):
    capacity = strength.shape[0]
    return pl.pallas_call(
        pack_kernel,
        out_shape=jax.ShapeDtypeStruct((groups, ROWS, capacity), jnp.int32),
        in_specs=[
            pl.BlockSpec(memory_space=pltpu.SMEM),
            *([pl.BlockSpec(memory_space=pltpu.VMEM)] * 4),
        ],
        name="pack",
    )(
        first_hand.astype(jnp.int32).reshape(1, 1),
        jnp.transpose(strength, (2, 1, 0)),
        board_mask.T,
        flop_weight.reshape(1, capacity),
        jnp.transpose(runout, (1, 2, 0)),
    )


def route_kernel(group_ref, slots_ref, out_ref):
    groups, rows, capacity = slots_ref.shape
    pairs = out_ref.shape[0]
    weight_row = (ITERS - 1) * (H // pairs)
    row = lax.broadcasted_iota(jnp.int32, (1, capacity), 1)
    counts = [
        jnp.sum((slots_ref[g, weight_row : weight_row + 1, :] > 0).astype(jnp.int32))
        for g in range(groups)
    ]
    totals = [[jnp.zeros((pairs, LINE), jnp.float32) for part in range(4)] for odd in range(2)]
    pair = lax.broadcasted_iota(jnp.int32, (pairs, capacity), 0)
    blank = jnp.zeros((LINE - rows, capacity), jnp.int32)
    for g in range(groups):
        place = -2 * pairs * group_ref[0, 0] + jnp.zeros((1, capacity), jnp.int32)
        for other in range(groups):
            place = place + jnp.minimum(counts[other], row + int(other < g))
        place = jnp.where(row < counts[g], place, -1)
        values = jnp.concatenate([slots_ref[g], blank])
        picks = [
            (place == 2 * pair + odd).astype(jnp.float32).astype(jnp.bfloat16) for odd in range(2)
        ]
        for part in range(4):
            digits = (values >> (8 * part)) & (PART - 1)
            digits = digits.astype(jnp.float32).astype(jnp.bfloat16)
            for odd in range(2):
                found = lax.dot_general(
                    picks[odd], digits, (((1,), (1,)), ((), ())), preferred_element_type=jnp.float32
                )
                totals[odd][part] = totals[odd][part] + found
    for odd in range(2):
        whole = jnp.zeros((pairs, LINE), jnp.int32)
        for part in range(4):
            whole = whole + (totals[odd][part].astype(jnp.int32) << (8 * part))
        out_ref[:, 0, LINE * odd : LINE * (odd + 1)] = whole


def route(slots, group_id, pairs):
    return pl.pallas_call(
        route_kernel,
        out_shape=jax.ShapeDtypeStruct((pairs, 1, 2 * LINE), jnp.int32),
        in_specs=[pl.BlockSpec(memory_space=pltpu.SMEM), pl.BlockSpec(memory_space=pltpu.VMEM)],
        name="route",
    )(group_id.astype(jnp.int32).reshape(1, 1), slots)


def on_device(range_one, range_two, flop_weight, board_mask, runout, strength):
    groups = lax.axis_size(GRP)
    shards = lax.axis_size(INF)
    shard_id = lax.axis_index(INF)
    hand_block = strength.shape[2]
    first_hand = shard_id * hand_block
    low, high = (jnp.asarray(table).reshape(1, PADDED) for table in hand_cards(PADDED, HANDS))
    slots = exchanged(
        packed(first_hand, strength, board_mask, flop_weight, runout, groups), GRP
    )
    arrived = exchanged(route(slots, lax.axis_index(GRP), shards), INF)
    turn_reach, pre_reach = solve(
        arrived, range_one, range_two, low, high, compat_matrix(low, high)
    )
    return turn_reach, lax.dynamic_slice_in_dim(pre_reach, first_hand, hand_block)


def solution(mesh):
    split = Mesh(mesh.devices.reshape(2, 2, 4, 8, 2), ("grp_0", "grp_1", "inf_0", "inf_1", "inf_2"))
    return jax.shard_map(
        on_device,
        mesh=split,
        in_specs=(P(), P(), P(GRP), P(GRP, INF), P(GRP, None, None), P(GRP, None, INF)),
        out_specs=(P(GRP_INF, None, None), P(INF)),
        check_vma=False,
    )
```

time: 145 us -> 123 us (0.85)
  local copies, waits for them, and re-layouts: 20.1 us -> 6.59 us
  other arithmetic: 11.4 us -> 0.18 us
  Pallas kernels: 29.9 us -> 37.1 us
  waiting for transfers between devices: 23.6 us -> 19.2 us
  starting transfers between devices: 23.3 us -> 20.2 us
  blocking collectives: 34.9 us -> 37.8 us
    all_to_all x0 -> x2, blocking collectives: none -> 20.6 us  [exchanged(): return lax.all_to_all(copies, axis, split_axis=0, concat_axis=0, tiled=True)]
    all_to_all x3 -> x1, blocking collectives: 34.9 us -> 17.3 us  [sent_to_all(): return lax.all_to_all(copies, axis, split_axis=0, concat_axis=0, tiled=True)]
    gather x9 -> x0, local copies, waits for them, and re-layouts: 9.57 us -> none  [place_rows(): jnp.take(member, source, axis=0)]
    pallas_call x3 -> x6, Pallas kernels: 29.9 us -> 37.1 us  [the longest x1 13.1 us: solve(): pl.pallas_call(first_kernel, out_shape=[jax.ShapeDtypeStruct((ITERS - 1,...]
    all_to_all x2 -> x1, starting transfers between devices: 7.64 us -> 3.73 us  [sent_to_all(): return lax.all_to_all(copies, axis, split_axis=0, concat_axis=0, tiled=True)]
    ppermute x2 -> x0, waiting for transfers between devices: 2.74 us -> none  [whole_sum(): x = x + lax.ppermute(x, 'grp_1', [(0, 1), (1, 0)])]
    reduce_sum x12 -> x2, other arithmetic: 2.67 us -> 0.18 us  [whole_parts(): part = jnp.sum(exchanged(copies, FIRST_SUM), axis=0)]
    div x2 -> x0, other arithmetic: 2.14 us -> none  [the longest x1 1.55 us: on_device(): turn_final = turn_sum / total_weight]
  transfers between devices with their start and end apart: 6 -> 3, of which waited for: 6 -> 3; matrix products, arithmetic and copies ran while one was open for 3% -> 2% of each run, Pallas kernels for 3% -> 5%
where the time goes in v2:
time: 123 us; the launch traced here: 122 us
  blocking collectives  37.8 us (31%)
  Pallas kernels  37.1 us (30%)
  starting transfers between devices  20.2 us (16%)
  waiting for transfers between devices  19.2 us (16%)
  local copies, waits for them, and re-layouts  6.59 us (5%)
    all_to_all x2, blocking collectives, exchanged(): return lax.all_to_all(copies, axis, split_axis=0, concat_axis=0, tiled=True)  20.6 us
    all_to_all x1, blocking collectives, sent_to_all(): return lax.all_to_all(copies, axis, split_axis=0, concat_axis=0, tiled=True)  17.3 us
    all_to_all x2, starting transfers between devices, exchanged(): return lax.all_to_all(copies, axis, split_axis=0, concat_axis=0, tiled=True)  16.5 us
    pallas_call x1, Pallas kernels, solve(): pl.pallas_call(first_kernel, out_shape=[jax.ShapeDtypeStruct((ITERS - 1,...  13.1 us
    pallas_call x1, Pallas kernels, solve(): pl.pallas_call(second_kernel, out_shape=rows_of((first_count, 1, H), pair...  12.4 us
    all_to_all x1, waiting for transfers between devices, sent_to_all(): return lax.all_to_all(copies, axis, split_axis=0, concat_axis=0, tiled=True)  10 us
    all_to_all x2, waiting for transfers between devices, exchanged(): return lax.all_to_all(copies, axis, split_axis=0, concat_axis=0, tiled=True)  9.17 us
    pallas_call x1, Pallas kernels, compat_matrix(): pl.pallas_call(compat_kernel, out_shape=jax.ShapeDtypeStruct((H, PADDED),...  5.98 us
  transfers between devices with their start and end apart: 3, of which 3 were waited for; matrix products, arithmetic and copies ran while one was open for 2% of the time, Pallas kernels for 5%

profile of v2, /device:TPU:8, one launch (start us, length us, event | category | flops | bytes accessed | tf_op | source)
XLA Modules:
  0.0 121.8 jit_solution(7150604258441390008)
XLA Ops:
  0.6 1.7 %pack.1 = s32[4,80,256]{2,1,0:T(8,128)} custom-call(s32[1,1]{1,0:T(1,128)} %bitcast.1.first_hand_ref, s32[22,4,256]{2,1,0:T(4,128)} %bitcast.9, s32[22,256]{1,0:T(8,128)} %bitcast.10, s32[1,256]{1,0:T(1,128)} %bitcast.12, s32[4,2,256]{2,1,0:T(2,128)} %bitcast.11), custom_call_target="tpu_custom_call" | custom-call | tf_op jit(solution)/shard_map/pack/pallas_call | solution.py:445
  2.4 4.3 %all-to-all-start = ((s32[4,80,256]{2,1,0:T(8,128)}), s32[4,80,256]{2,1,0:T(8,128)S(1)}, u32[]{:S(2)}, u32[]{:S(2)}) async-start(s32[4,80,256]{2,1,0:T(8,128)} %pack.1), calls=%async_computation | async-start | bytes 655360 | tf_op jit(solution)/shard_map/all_to_all | solution.py:412
  6.7 8.2 %all-to-all-done.slots_ref = s32[4,80,256]{2,1,0:T(8,128)S(1)} async-done(((s32[4,80,256]{2,1,0:T(8,128)}), s32[4,80,256]{2,1,0:T(8,128)S(1)}, u32[]{:S(2)}, u32[]{:S(2)}) %all-to-all-start) | async-done | bytes 327712 | tf_op jit(solution)/shard_map/all_to_all | solution.py:412
  14.9 0.0 copy-start
  14.9 0.7 copy-done
  15.6 2.3 %route.1 = s32[64,1,256]{2,1,0:T(1,128)} custom-call(s32[1,1]{1,0:T(1,128)} %bitcast.group_ref, s32[4,80,256]{2,1,0:T(8,128)} %copy-done), custom_call_target="tpu_custom_call" | custom-call | tf_op jit(solution)/shard_map/route/pallas_call | solution.py:499
  17.9 12.2 %all-to-all-start.1 = ((s32[64,1,256]{2,1,0:T(1,128)}), s32[64,1,256]{2,1,0:T(1,128)S(1)}, u32[]{:S(2)}, u32[]{:S(2)}) async-start(s32[64,1,256]{2,1,0:T(1,128)} %route.1), calls=%async_computation.1 | async-start | bytes 131072 | tf_op jit(solution)/shard_map/all_to_all | solution.py:412
  30.1 1.3 %reshape.38.one_ref = f32[1,1408]{1,0:T(1,128)} reshape(f32[1408]{0:T(1024)} %param.8) | data formatting | bytes 11264 | tf_op jit(solution)/shard_map/reshape | solution.py:382
  31.3 1.3 %reshape.39.two_ref = f32[1,1408]{1,0:T(1,128)} reshape(f32[1408]{0:T(1024)} %param.9) | data formatting | bytes 11264 | tf_op jit(solution)/shard_map/reshape | solution.py:383
  32.6 6.0 %compat.1.compat_ref = bf16[1408,1536]{1,0:T(8,128)(2,1)} custom-call(s32[1,1536]{1,0:T(1,128)} %constant.42.low_ref, s32[1,1536]{1,0:T(1,128)} %constant.43.high_ref), custom_call_target="tpu_custom_call" | custom-call | tf_op jit(solution)/shard_map/compat/pallas_call | solution.py:78
  38.6 1.0 all-to-all-done.1.arrived_ref
  39.6 0.0 copy-start.2
  39.6 0.6 copy-done.2
  40.2 13.1 %first.1 = (s32[3,2,1536]{2,1,0:T(2,128)}, f32[2,1408]{1,0:T(2,128)}, f32[2,1]{1,0:T(2,128)}, f32[16,1,2816]{2,1,0:T(1,128)}, f32[2,1408]{1,0:T(2,128)}, /*index...) custom-call(s32[64,1,256]{2,1,0:T(1,128)} %copy-done.2, ...), custom_call_target="tpu_custom_call" | custom-call | tf_op jit(solution)/shard_map/first/pallas_call | solution.py:386
  53.3 10.7 %all_to_all.30 = f32[16,1,2816]{2,1,0:T(1,128)S(1)} all-to-all(f32[16,1,2816]{2,1,0:T(1,128)} %get-tuple-element.27), channel_id=1, replica_groups=mesh['grp_0'=2,'grp_1'=2,'inf_0'=4,'inf_1'=8,'inf_2'=2] {'grp_1','inf_0'..., dimensions={0} | all-to-all | bytes 360448 | tf_op jit(solution)/shard_map/all_to_all | solution.py:412
  64.0 0.1 reduce_sum.18
  64.1 0.1 broadcast_in_dim.6
  64.2 17.3 %all_to_all.31.sums_in_ref = f32[16,1,2816]{2,1,0:T(1,128)} all-to-all(f32[16,1,2816]{2,1,0:T(1,128)S(1)} %broadcast_in_dim.6), channel_id=1, replica_groups=mesh['grp_0'=2,'grp_1'=2,'inf_0'=4,'inf_1'=8,'inf_2'=2] {'grp_0','inf_1'}, dimensions={0} | all-to-all | bytes 360448 | tf_op jit(solution)/shard_map/all_to_all | solution.py:25
  81.4 12.4 %second.1 = (f32[16,1,1408]{2,1,0:T(1,128)}, f32[2,1408]{1,0:T(2,128)}, f32[2,1408]{1,0:T(2,128)}, f32[6,2,1408]{2,1,0:T(2,128)}, f32[3,1408]{1,0:T(4,128)}) custom-call(s32[3,2,1536]{2,1,0:T(2,128)} %get-tuple-element.25.key_ref, f32[2,1408]{1,0:T(2,128)} %get-tuple-element.24.live_ref, f32[1,1408]{1,0:T(1,128)} %reshape.38.one_ref, ...), custom_call_target="tpu_custom_call" | custom-call | tf_op jit(solution)/shard_map/second/pallas_call | solution.py:396
  93.8 9.9 %all_to_all.32 = f32[16,1,1408]{2,1,0:T(1,128)S(1)} all-to-all(f32[16,1,1408]{2,1,0:T(1,128)} %get-tuple-element.39), channel_id=1, replica_groups=mesh['grp_0'=2,'grp_1'=2,'inf_0'=4,'inf_1'=8,'inf_2'=2] {'grp_1','inf_0'..., dimensions={0} | all-to-all | bytes 180224 | tf_op jit(solution)/shard_map/all_to_all | solution.py:412
  103.7 0.1 reduce_sum.19
  103.8 0.7 broadcast_in_dim.7
  104.4 3.7 %all-to-all-start.5 = ((f32[16,1,1408]{2,1,0:T(1,128)}), f32[16,1,1408]{2,1,0:T(1,128)S(1)}, u32[]{:S(2)}, u32[]{:S(2)}) async-start(f32[16,1,1408]{2,1,0:T(1,128)} %broadcast_in_dim.7), calls=%async_computation.5 | async-start | bytes 180224 | tf_op jit(solution)/shard_map/all_to_all | solution.py:25
  108.2 10.0 %all-to-all-done.5.sums_in_ref = f32[16,1,1408]{2,1,0:T(1,128)S(1)} async-done(((f32[16,1,1408]{2,1,0:T(1,128)}), f32[16,1,1408]{2,1,0:T(1,128)S(1)}, u32[]{:S(2)}, u32[]{:S(2)}) %all-to-all-start.5) | async-done | bytes 90144 | tf_op jit(solution)/shard_map/all_to_all | solution.py:25
  118.2 0.0 copy-start.1
  118.2 0.6 copy-done.1
  118.9 1.7 %last.1 = (f32[6,2,1408]{2,1,0:T(2,128)}, f32[1,1408]{1,0:T(1,128)}) custom-call(f32[2,1408]{1,0:T(2,128)} %get-tuple-element.24.live_ref, f32[1,1408]{1,0:T(1,128)} %reshape.38.one_ref, f32[16,1,1408]{2,1,0:T(1,128)} %copy-done.1, f32[2,1408]{1,0:T(2,128)} %get-tuple-element.40.share_root_ref, f32[2,1408]{1,0:T(2,128)} %get-tuple-element.41.share_fc_ref, ...), custom_call_target="tpu_custom_call" | custom-call | tf_op jit(solution)/shard_map/last/pallas_call | solution.py:403
  120.5 1.2 %dynamic-slice_bitcast_fusion = f32[22]{0:T(128)} fusion(f32[1,1408]{1,0:T(1,128)} %get-tuple-element.45, s32[]{:T(128)S(6)} %select_n.3), kind=kLoop, calls=%fused_computation | loop fusion | bytes 180 | tf_op jit(solution)/shard_map/dynamic_slice | solution.py:521
Async XLA Ops:
  2.4 12.5 %all-to-all-start = ((s32[4,80,256]{2,1,0:T(8,128)}), s32[4,80,256]{2,1,0:T(8,128)S(1)}, u32[]{:S(2)}, u32[]{:S(2)}) async-start(s32[4,80,256]{2,1,0:T(8,128)} %pack.1), calls=%async_computation | async-start | bytes 655360 | tf_op jit(solution)/shard_map/all_to_all | solution.py:412
  14.9 0.7 copy-start
  17.9 21.7 %all-to-all-start.1 = ((s32[64,1,256]{2,1,0:T(1,128)}), s32[64,1,256]{2,1,0:T(1,128)S(1)}, u32[]{:S(2)}, u32[]{:S(2)}) async-start(s32[64,1,256]{2,1,0:T(1,128)} %route.1), calls=%async_computation.1 | async-start | bytes 131072 | tf_op jit(solution)/shard_map/all_to_all | solution.py:412
  39.6 0.6 copy-start.2
  104.4 13.8 %all-to-all-start.5 = ((f32[16,1,1408]{2,1,0:T(1,128)}), f32[16,1,1408]{2,1,0:T(1,128)S(1)}, u32[]{:S(2)}, u32[]{:S(2)}) async-start(f32[16,1,1408]{2,1,0:T(1,128)} %broadcast_in_dim.7), calls=%async_computation.5 | async-start | bytes 180224 | tf_op jit(solution)/shard_map/all_to_all | solution.py:25
  118.2 0.6 copy-start.1

commit v3 on v2

--- a/solution.py
+++ b/solution.py
@@ -49,9 +49,9 @@
 LINE = 128
 PART = 256
 BLOCK = 128
-WIDE = 256
-DEEP = 256
-PADDED = 1536
+WIDE = 1408
+DEEP = 128
+PADDED = 1408
 FIRST_SUM = ("grp_1", "inf_0", "inf_2")
 SECOND_SUM = ("grp_0", "inf_1")
 
@@ -79,10 +79,11 @@
         compat_kernel,
         out_shape=jax.ShapeDtypeStruct((H, PADDED), jnp.bfloat16),
         name="compat",
+        compiler_params=pltpu.CompilerParams(vmem_limit_bytes=12 << 20),
     )(low, high)
 
 
-def pair_sums(key_ref, counter, columns, compat_ref, lhs_ref, low_ref, sums_ref, col_ref):
+def pair_sums(key_ref, counter, columns, compat_ref, lhs_ref, low_ref, sums_ref, col_ref, fetch=None):
     alive = (key_ref[counter, :, :H] >= 0).astype(jnp.float32)
     lhs_ref[...] = jnp.zeros((16, H), jnp.float32)
     for k, column in columns.items():
@@ -97,6 +98,8 @@
         return carry
 
     lax.fori_loop(0, H // BLOCK, key_column, 0)
+    if fetch is not None:
+        fetch.wait()
 
     def mine(step, carry):
         start = pl.multiple_of(step * WIDE, WIDE)
@@ -107,7 +110,6 @@
             depth = min(DEEP, H - first)
             lhs = low_ref[:, first : first + depth]
             most = compat_ref[first : first + depth, pl.ds(start, WIDE)]
-            least = -most
             weight_total = weight_total + jnp.dot(lhs, most, preferred_element_type=jnp.float32)
             for flop in range(2):
                 parts = []
@@ -116,7 +118,8 @@
                     gap = rows[flop][:, lane : lane + BLOCK] - key_col
                     parts.append(gap.astype(jnp.float32).astype(jnp.bfloat16))
                 sign = jnp.concatenate(parts, axis=1) if len(parts) > 1 else parts[0]
-                sign = jnp.minimum(jnp.maximum(sign, least), most)
+                one = jnp.bfloat16(1)
+                sign = jnp.minimum(jnp.maximum(sign, -one), one) * most
                 totals[flop] = totals[flop] + jnp.dot(
                     lhs, sign, preferred_element_type=jnp.float32
                 )
@@ -250,12 +253,14 @@
 
 
 def first_kernel(
-    arrived_ref, low_ref, high_ref, one_ref, two_ref, compat_ref,
+    arrived_ref, low_ref, high_ref, one_ref, two_ref, compat_hbm_ref,
     key_ref, live_ref, share_ref, cont_ref,
     root_check_ref, root_bet_ref, fc_fold_ref, fc_call_ref,
     ac_check_ref, ac_bet_ref, fb_fold_ref, fb_call_ref, share_root_ref, share_fc_ref, turn_ref,
-    lhs_ref, low_part_ref, sums_ref, col_ref,
+    lhs_ref, low_part_ref, sums_ref, col_ref, compat_ref, compat_sem,
 ):
+    fetch = pltpu.make_async_copy(compat_hbm_ref, compat_ref, compat_sem)
+    fetch.start()
     scratch = (compat_ref, lhs_ref, low_part_ref, sums_ref, col_ref)
     read_flops(arrived_ref, low_ref, high_ref, key_ref, live_ref, share_ref)
     live = live_ref[...]
@@ -267,7 +272,7 @@
     one_all = one_ref[...] * action_share(zero_row, zero_row) * live
     one_cols = one_columns(one_all, start, start)
     two_cols = two_columns(two_all, start, start)
-    sign_sum, weight_sum = pair_sums(key_ref, 0, {**two_cols, **one_cols}, *scratch)
+    sign_sum, weight_sum = pair_sums(key_ref, 0, {**two_cols, **one_cols}, *scratch, fetch)
     values = two_values(sign_sum, weight_sum, start, start)
     spread(cont_ref, 0, flop_value(share, values[5]))
     regrets = two_regrets((zero, zero, zero, zero), values)
@@ -294,12 +299,14 @@
 
 
 def second_kernel(
-    key_ref, live_ref, one_ref, two_ref, share_ref, compat_ref, sums_in_ref,
+    key_ref, live_ref, one_ref, two_ref, share_ref, compat_hbm_ref, sums_in_ref,
     root_check_ref, root_bet_ref, fc_fold_ref, fc_call_ref,
     ac_check_ref, ac_bet_ref, fb_fold_ref, fb_call_ref, share_root_ref, share_fc_ref, turn_ref,
     cont_ref, out_root_ref, out_fc_ref, out_turn_ref, out_pre_ref,
-    lhs_ref, low_ref, sums_ref, col_ref,
+    lhs_ref, low_ref, sums_ref, col_ref, compat_ref, compat_sem,
 ):
+    fetch = pltpu.make_async_copy(compat_hbm_ref, compat_ref, compat_sem)
+    fetch.start()
     scratch = (compat_ref, lhs_ref, low_ref, sums_ref, col_ref)
     live = live_ref[...]
     zero_row = jnp.zeros((1, H), jnp.float32)
@@ -316,7 +323,7 @@
     others = (ac_check_ref[...], ac_bet_ref[...], fb_fold_ref[...], fb_call_ref[...])
     share_ac = action_share(others[0], others[1])
     share_fb = action_share(others[2], others[3])
-    sign_sum, weight_sum = pair_sums(key_ref, 1, one_cols, *scratch)
+    sign_sum, weight_sum = pair_sums(key_ref, 1, one_cols, *scratch, fetch)
     others = one_regrets(others, one_values(sign_sum, weight_sum, share_ac, share_fb))
 
     pre_cont, pre_fold = pre_step(pre_cont, pre_fold, add_parts(sums_in_ref, H))
@@ -356,7 +363,17 @@
         pltpu.VMEM((16, H), jnp.bfloat16),
         pltpu.VMEM((2, 16, PADDED), jnp.float32),
         pltpu.VMEM((2, H, BLOCK), jnp.int32),
+        pltpu.VMEM((H, PADDED), jnp.bfloat16),
+        pltpu.SemaphoreType.DMA,
     ]
+
+
+def in_vmem(count):
+    return [pl.BlockSpec(memory_space=pltpu.VMEM)] * count
+
+
+def in_hbm():
+    return pl.BlockSpec(memory_space=pltpu.HBM)
 
 
 def rows_of(*shapes):
@@ -389,21 +406,26 @@
             jax.ShapeDtypeStruct((ITERS - 1, 2, PADDED), jnp.int32),
             *rows_of(pair, (2, 1), (first_count, 1, 2 * H), *([pair] * 10), (6, 2, H)),
         ],
+        in_specs=[*in_vmem(5), in_hbm()],
         scratch_shapes=pair_scratch(),
         name="first",
+        compiler_params=pltpu.CompilerParams(vmem_limit_bytes=20 << 20),
     )(arrived, low, high, one_row, two_row, compat)
     parts = whole_parts(cont)
     cont, share_root, share_fc, turns, pre = pl.pallas_call(
         second_kernel,
         out_shape=rows_of((first_count, 1, H), pair, pair, (6, 2, H), (3, H)),
+        in_specs=[*in_vmem(5), in_hbm(), *in_vmem(12)],
         scratch_shapes=pair_scratch(),
         name="second",
+        compiler_params=pltpu.CompilerParams(vmem_limit_bytes=20 << 20),
     )(key_now, live, one_row, two_row, share, compat, parts, *state)
     parts = whole_parts(cont)
     turns, pre = pl.pallas_call(
         last_kernel,
         out_shape=rows_of((6, 2, H), (1, H)),
         name="last",
+        compiler_params=pltpu.CompilerParams(vmem_limit_bytes=8 << 20),
     )(live, one_row, parts, share_root, share_fc, turns, pre)
     return jnp.swapaxes(turns, 0, 1), pre.reshape(H)
 
@@ -501,6 +523,7 @@
         out_shape=jax.ShapeDtypeStruct((pairs, 1, 2 * LINE), jnp.int32),
         in_specs=[pl.BlockSpec(memory_space=pltpu.SMEM), pl.BlockSpec(memory_space=pltpu.VMEM)],
         name="route",
+        compiler_params=pltpu.CompilerParams(vmem_limit_bytes=12 << 20),
     )(group_id.astype(jnp.int32).reshape(1, 1), slots)
 
 
@@ -516,7 +539,12 @@
     )
     arrived = exchanged(route(slots, lax.axis_index(GRP), shards), INF)
     turn_reach, pre_reach = solve(
-        arrived, range_one, range_two, low, high, compat_matrix(low, high)
+        arrived,
+        range_one,
+        range_two,
+        low,
+        high,
+        pltpu.with_memory_space_constraint(compat_matrix(low, high), pltpu.HBM),
     )
     return turn_reach, lax.dynamic_slice_in_dim(pre_reach, first_hand, hand_block)
 

time: 123 us -> 107 us (0.87)
  Pallas kernels: 37.1 us -> 22.4 us
  blocking collectives: 37.8 us -> 35.8 us
    pallas_call x1, Pallas kernels: 12.4 us -> 7.43 us  [solve(): pl.pallas_call(second_kernel, out_shape=rows_of((first_count, 1, H), pair...]
    pallas_call x1, Pallas kernels: 13.1 us -> 8.16 us  [solve(): pl.pallas_call(first_kernel, out_shape=[jax.ShapeDtypeStruct((ITERS - 1,...]
    pallas_call x1, Pallas kernels: 5.98 us -> 3.08 us  [compat_matrix(): pl.pallas_call(compat_kernel, out_shape=jax.ShapeDtypeStruct((H, PADDED),...]
    all_to_all x2, blocking collectives: 20.6 us -> 18.8 us  [exchanged(): return lax.all_to_all(copies, axis, split_axis=0, concat_axis=0, tiled=True)]
    unnamed x6 -> x10, local copies, waits for them, and re-layouts: 1.99 us -> 3.27 us
  transfers between devices with their start and end apart: 3 -> 3, of which waited for: 3 -> 3; matrix products, arithmetic and copies ran while one was open for 2% -> 1% of each run, Pallas kernels for 5% -> 3%
where the time goes in v3:
time: 107 us; the launch traced here: 106 us
  blocking collectives  35.8 us (33%)
  Pallas kernels  22.4 us (21%)
  starting transfers between devices  20.8 us (19%)
  waiting for transfers between devices  20 us (19%)
  local copies, waits for them, and re-layouts  6.03 us (6%)
    all_to_all x2, blocking collectives, exchanged(): return lax.all_to_all(copies, axis, split_axis=0, concat_axis=0, tiled=True)  18.8 us
    all_to_all x1, blocking collectives, sent_to_all(): return lax.all_to_all(copies, axis, split_axis=0, concat_axis=0, tiled=True)  17 us
    all_to_all x2, starting transfers between devices, exchanged(): return lax.all_to_all(copies, axis, split_axis=0, concat_axis=0, tiled=True)  16.5 us
    all_to_all x1, waiting for transfers between devices, sent_to_all(): return lax.all_to_all(copies, axis, split_axis=0, concat_axis=0, tiled=True)  10 us
    all_to_all x2, waiting for transfers between devices, exchanged(): return lax.all_to_all(copies, axis, split_axis=0, concat_axis=0, tiled=True)  9.98 us
    pallas_call x1, Pallas kernels, solve(): pl.pallas_call(first_kernel, out_shape=[jax.ShapeDtypeStruct((ITERS - 1,...  8.16 us
    pallas_call x1, Pallas kernels, solve(): pl.pallas_call(second_kernel, out_shape=rows_of((first_count, 1, H), pair...  7.43 us
    all_to_all x1, starting transfers between devices, sent_to_all(): return lax.all_to_all(copies, axis, split_axis=0, concat_axis=0, tiled=True)  4.34 us
  transfers between devices with their start and end apart: 3, of which 3 were waited for; matrix products, arithmetic and copies ran while one was open for 1% of the time, Pallas kernels for 3%

profile of v3, /device:TPU:8, one launch (start us, length us, event | category | flops | bytes accessed | tf_op | source)
XLA Modules:
  0.0 105.9 jit_solution(6433302163188046983)
XLA Ops:
  0.6 0.0 copy-start.2
  0.6 0.0 copy-start.4
  0.7 1.7 %pack.1 = s32[4,80,256]{2,1,0:T(8,128)} custom-call(s32[1,1]{1,0:T(1,128)} %bitcast.1.first_hand_ref, s32[22,4,256]{2,1,0:T(4,128)} %bitcast.9, s32[22,256]{1,0:T(8,128)} %bitcast.10, s32[1,256]{1,0:T(1,128)} %bitcast.12, s32[4,2,256]{2,1,0:T(2,128)} %bitcast.11), custom_call_target="tpu_custom_call" | custom-call | tf_op jit(solution)/shard_map/pack/pallas_call | solution.py:467
  2.4 4.3 %all-to-all-start = ((s32[4,80,256]{2,1,0:T(8,128)}), s32[4,80,256]{2,1,0:T(8,128)S(1)}, u32[]{:S(2)}, u32[]{:S(2)}) async-start(s32[4,80,256]{2,1,0:T(8,128)} %pack.1), calls=%async_computation | async-start | bytes 655360 | tf_op jit(solution)/shard_map/all_to_all | solution.py:434
  6.7 8.2 %all-to-all-done.slots_ref = s32[4,80,256]{2,1,0:T(8,128)S(1)} async-done(((s32[4,80,256]{2,1,0:T(8,128)}), s32[4,80,256]{2,1,0:T(8,128)S(1)}, u32[]{:S(2)}, u32[]{:S(2)}) %all-to-all-start) | async-done | bytes 327712 | tf_op jit(solution)/shard_map/all_to_all | solution.py:434
  14.9 1.3 %route.1 = s32[64,1,256]{2,1,0:T(1,128)} custom-call(s32[1,1]{1,0:T(1,128)} %bitcast.group_ref, s32[4,80,256]{2,1,0:T(8,128)S(1)} %all-to-all-done.slots_ref), custom_call_target="tpu_custom_call" | custom-call | tf_op jit(solution)/shard_map/route/pallas_call | solution.py:521
  16.2 12.2 %all-to-all-start.1 = ((s32[64,1,256]{2,1,0:T(1,128)}), s32[64,1,256]{2,1,0:T(1,128)S(1)}, u32[]{:S(2)}, u32[]{:S(2)}) async-start(s32[64,1,256]{2,1,0:T(1,128)} %route.1), calls=%async_computation.1 | async-start | bytes 131072 | tf_op jit(solution)/shard_map/all_to_all | solution.py:434
  28.4 0.7 reshape.38.one_ref
  29.1 0.7 reshape.39.two_ref
  29.8 0.0 copy-start.1
  29.8 0.7 copy-done.1
  30.4 0.0 copy-start.3
  30.5 0.7 copy-done.3
  31.1 3.1 %compat.1.compat_hbm_ref = bf16[1408,1408]{1,0:T(8,128)(2,1)S(1)} custom-call(s32[1,1408]{1,0:T(1,128)S(1)} %copy-done.3, s32[1,1408]{1,0:T(1,128)S(1)} %copy-done.1), custom_call_target="tpu_custom_call" | custom-call | tf_op jit(solution)/shard_map/compat/pallas_call | solution.py:78
  34.2 0.0 copy-start
  34.2 1.9 %copy-done = bf16[1408,1408]{1,0:T(8,128)(2,1)} copy-done((bf16[1408,1408]{1,0:T(8,128)(2,1)}, bf16[1408,1408]{1,0:T(8,128)(2,1)S(1)}, u32[]{:S(2)}) %copy-start) | copy-done | bytes 3964952
  36.1 1.8 %all-to-all-done.1.arrived_ref = s32[64,1,256]{2,1,0:T(1,128)S(1)} async-done(((s32[64,1,256]{2,1,0:T(1,128)}), s32[64,1,256]{2,1,0:T(1,128)S(1)}, u32[]{:S(2)}, u32[]{:S(2)}) %all-to-all-start.1) | async-done | bytes 65568 | tf_op jit(solution)/shard_map/all_to_all | solution.py:434
  37.9 0.0 copy-done.2
  37.9 0.0 copy-done.4
  37.9 8.2 %first.1 = (s32[3,2,1408]{2,1,0:T(2,128)S(1)}, f32[2,1408]{1,0:T(2,128)S(1)}, f32[2,1]{1,0:T(2,128)S(1)}, f32[16,1,2816]{2,1,0:T(1,128)S(1)}, f32[2,1408]{1,0:T(...) custom-call(s32[64,1,256]{2,1,0:T(1,128)S(1)} %all-to-all-done.1.arr, ...), custom_call_target="tpu_custom_call" | custom-call | tf_op jit(solution)/shard_map/first/pallas_call | solution.py:403
  46.1 9.9 %all_to_all.30 = f32[16,1,2816]{2,1,0:T(1,128)S(1)} all-to-all(f32[16,1,2816]{2,1,0:T(1,128)S(1)} %get-tuple-element.27), channel_id=1, replica_groups=mesh['grp_0'=2,'grp_1'=2,'inf_0'=4,'inf_1'=8,'inf_2'=2] {'grp_1','inf_0'..., dimensions={0} | all-to-all | bytes 360448 | tf_op jit(solution)/shard_map/all_to_all | solution.py:434
  55.9 0.1 reduce_sum.18
  56.0 0.1 broadcast_in_dim.6
  56.1 17.0 %all_to_all.31.sums_in_ref = f32[16,1,2816]{2,1,0:T(1,128)S(1)} all-to-all(f32[16,1,2816]{2,1,0:T(1,128)S(1)} %broadcast_in_dim.6), channel_id=1, replica_groups=mesh['grp_0'=2,'grp_1'=2,'inf_0'=4,'inf_1'=8,'inf_2'=2] {'grp_0','inf_1'}, dimensions={0} | all-to-all | bytes 360448 | tf_op jit(solution)/shard_map/all_to_all | solution.py:25
  73.1 7.4 %second.1 = (f32[16,1,1408]{2,1,0:T(1,128)S(1)}, f32[2,1408]{1,0:T(2,128)S(1)}, f32[2,1408]{1,0:T(2,128)S(1)}, f32[6,2,1408]{2,1,0:T(2,128)S(1)}, f32[3,1408]{1,0:T(4,128)S(1)}) custom-call(s32[3,2,1408]{2,1,0:T(2,128)S(1)} %get-tuple-element.25.key_ref, f32[2,1408]{1,0:T(2,128)S(1)} %get-tuple-element.24.live_ref, f32[1,1408]{1,0:T(1,128)S(1)} %reshape.38.one_ref, ...), custom_call_target="tpu_custom_call" | custom-call | tf_op jit(solution)/shard_map/second/pallas_call | solution.py:415
  80.6 9.0 %all_to_all.32 = f32[16,1,1408]{2,1,0:T(1,128)S(1)} all-to-all(f32[16,1,1408]{2,1,0:T(1,128)S(1)} %get-tuple-element.39), channel_id=1, replica_groups=mesh['grp_0'=2,'grp_1'=2,'inf_0'=4,'inf_1'=8,'inf_2'=2] {'grp_1','inf_0'..., dimensions={0} | all-to-all | bytes 180224 | tf_op jit(solution)/shard_map/all_to_all | solution.py:434
  89.5 0.1 reduce_sum.19
  89.6 0.7 broadcast_in_dim.7
  90.3 4.3 %all-to-all-start.5 = ((f32[16,1,1408]{2,1,0:T(1,128)}), f32[16,1,1408]{2,1,0:T(1,128)S(1)}, u32[]{:S(2)}, u32[]{:S(2)}) async-start(f32[16,1,1408]{2,1,0:T(1,128)} %broadcast_in_dim.7), calls=%async_computation.5 | async-start | bytes 180224 | tf_op jit(solution)/shard_map/all_to_all | solution.py:25
  94.6 10.0 %all-to-all-done.5.sums_in_ref = f32[16,1,1408]{2,1,0:T(1,128)S(1)} async-done(((f32[16,1,1408]{2,1,0:T(1,128)}), f32[16,1,1408]{2,1,0:T(1,128)S(1)}, u32[]{:S(2)}, u32[]{:S(2)}) %all-to-all-start.5) | async-done | bytes 90144 | tf_op jit(solution)/shard_map/all_to_all | solution.py:25
  104.7 0.7 last.1
  105.4 0.6 dynamic-slice_bitcast_fusion
Async XLA Ops:
  0.6 37.3 %copy-start.2 = (s32[1,1408]{1,0:T(1,128)S(1)}, s32[1,1408]{1,0:T(1,128)}, u32[]{:S(2)}) copy-start(s32[1,1408]{1,0:T(1,128)} %constant.43.high_ref) | copy-start | bytes 16900
  0.6 37.2 %copy-start.4 = (s32[1,1408]{1,0:T(1,128)S(1)}, s32[1,1408]{1,0:T(1,128)}, u32[]{:S(2)}) copy-start(s32[1,1408]{1,0:T(1,128)} %constant.42.low_ref) | copy-start | bytes 16900
  2.4 12.5 %all-to-all-start = ((s32[4,80,256]{2,1,0:T(8,128)}), s32[4,80,256]{2,1,0:T(8,128)S(1)}, u32[]{:S(2)}, u32[]{:S(2)}) async-start(s32[4,80,256]{2,1,0:T(8,128)} %pack.1), calls=%async_computation | async-start | bytes 655360 | tf_op jit(solution)/shard_map/all_to_all | solution.py:434
  16.2 21.7 %all-to-all-start.1 = ((s32[64,1,256]{2,1,0:T(1,128)}), s32[64,1,256]{2,1,0:T(1,128)S(1)}, u32[]{:S(2)}, u32[]{:S(2)}) async-start(s32[64,1,256]{2,1,0:T(1,128)} %route.1), calls=%async_computation.1 | async-start | bytes 131072 | tf_op jit(solution)/shard_map/all_to_all | solution.py:434
  29.8 0.7 copy-start.1
  30.4 0.7 copy-start.3
  34.2 1.9 %copy-start = (bf16[1408,1408]{1,0:T(8,128)(2,1)}, bf16[1408,1408]{1,0:T(8,128)(2,1)S(1)}, u32[]{:S(2)}) copy-start(bf16[1408,1408]{1,0:T(8,128)(2,1)S(1)} %compat.1.compat_hbm_ref) | copy-start | bytes 11894788
  90.3 14.4 %all-to-all-start.5 = ((f32[16,1,1408]{2,1,0:T(1,128)}), f32[16,1,1408]{2,1,0:T(1,128)S(1)}, u32[]{:S(2)}, u32[]{:S(2)}) async-start(f32[16,1,1408]{2,1,0:T(1,128)} %broadcast_in_dim.7), calls=%async_computation.5 | async-start | bytes 180224 | tf_op jit(solution)/shard_map/all_to_all | solution.py:25

commit v4 on v3

--- a/solution.py
+++ b/solution.py
@@ -440,33 +440,39 @@
 
 
 ROWS = 80
+FIRST_ROWS = (0, 0, FLOP_GRP // 2, FLOP_GRP)
 
 
 def pack_kernel(first_hand_ref, strength_ref, board_ref, weight_ref, cards_ref, out_ref):
-    groups, rows, capacity = out_ref.shape
-    hand_block = strength_ref.shape[0]
+    groups, rows, width = out_ref.shape
+    hand_block, _, capacity = strength_ref.shape
     used = ITERS - 1
     hand = first_hand_ref[0, 0] + lax.broadcasted_iota(jnp.int32, (hand_block, capacity), 0)
     flop_live = (board_ref[...] == 1) & (hand < HANDS)
+    keys = [jnp.where(flop_live, strength_ref[:, counter, :] + 1, 0) for counter in range(used)]
+    weights = weight_ref[...]
+    cards = [cards_ref[counter] for counter in range(used)]
+    count = jnp.zeros((1, width), jnp.int32) + jnp.sum((weights > 0).astype(jnp.int32))
     extra = used * hand_block
-    for group in range(groups):
+    for group, first in enumerate(FIRST_ROWS):
         for counter in range(used):
-            out_ref[group, hand_block * counter : hand_block * (counter + 1), :] = jnp.where(
-                flop_live, strength_ref[:, counter, :] + 1, 0
-            )
-        out_ref[group, extra : extra + 1, :] = weight_ref[...]
+            out_ref[group, hand_block * counter : hand_block * (counter + 1), :] = keys[counter][
+                :, first : first + width
+            ]
+        out_ref[group, extra : extra + 1, :] = weights[:, first : first + width]
         for counter in range(used):
             row = extra + 1 + 2 * counter
-            out_ref[group, row : row + 2, :] = cards_ref[counter]
+            out_ref[group, row : row + 2, :] = cards[counter][:, first : first + width]
         blank = extra + 1 + 2 * used
-        out_ref[group, blank:, :] = jnp.zeros((rows - blank, capacity), jnp.int32)
+        out_ref[group, blank : blank + 1, :] = count
+        out_ref[group, blank + 1 :, :] = jnp.zeros((rows - blank - 1, width), jnp.int32)
 
 
 def packed(first_hand, strength, board_mask, flop_weight, runout, groups):
     capacity = strength.shape[0]
     return pl.pallas_call(
         pack_kernel,
-        out_shape=jax.ShapeDtypeStruct((groups, ROWS, capacity), jnp.int32),
+        out_shape=jax.ShapeDtypeStruct((groups, ROWS, FLOP_GRP), jnp.int32),
         in_specs=[
             pl.BlockSpec(memory_space=pltpu.SMEM),
             *([pl.BlockSpec(memory_space=pltpu.VMEM)] * 4),
@@ -482,19 +488,18 @@
 
 
 def route_kernel(group_ref, slots_ref, out_ref):
-    groups, rows, capacity = slots_ref.shape
+    groups, rows, width = slots_ref.shape
     pairs = out_ref.shape[0]
-    weight_row = (ITERS - 1) * (H // pairs)
-    row = lax.broadcasted_iota(jnp.int32, (1, capacity), 1)
-    counts = [
-        jnp.sum((slots_ref[g, weight_row : weight_row + 1, :] > 0).astype(jnp.int32))
-        for g in range(groups)
-    ]
+    count_row = (ITERS - 1) * (H // pairs + 2) + 1
+    group = group_ref[0, 0]
+    first = jnp.where(group == 3, FIRST_ROWS[3], jnp.where(group == 2, FIRST_ROWS[2], 0))
+    row = first + lax.broadcasted_iota(jnp.int32, (1, width), 1)
+    counts = [slots_ref[g, count_row : count_row + 1, :] for g in range(groups)]
     totals = [[jnp.zeros((pairs, LINE), jnp.float32) for part in range(4)] for odd in range(2)]
-    pair = lax.broadcasted_iota(jnp.int32, (pairs, capacity), 0)
-    blank = jnp.zeros((LINE - rows, capacity), jnp.int32)
+    pair = lax.broadcasted_iota(jnp.int32, (pairs, width), 0)
+    blank = jnp.zeros((LINE - rows, width), jnp.int32)
     for g in range(groups):
-        place = -2 * pairs * group_ref[0, 0] + jnp.zeros((1, capacity), jnp.int32)
+        place = -2 * pairs * group + jnp.zeros((1, width), jnp.int32)
         for other in range(groups):
             place = place + jnp.minimum(counts[other], row + int(other < g))
         place = jnp.where(row < counts[g], place, -1)
@@ -546,7 +551,9 @@
         high,
         pltpu.with_memory_space_constraint(compat_matrix(low, high), pltpu.HBM),
     )
-    return turn_reach, lax.dynamic_slice_in_dim(pre_reach, first_hand, hand_block)
+    return turn_reach, lax.dynamic_slice(
+        pre_reach, (first_hand,), (hand_block,), allow_negative_indices=False
+    )
 
 
 def solution(mesh):

time: 107 us -> 104 us (0.972)
  blocking collectives: 35.8 us -> 50 us
  waiting for transfers between devices: 20 us -> 8.24 us
  starting transfers between devices: 20.8 us -> 16.4 us
    all_to_all x1 -> x2, blocking collectives: 17 us -> 31.1 us  [sent_to_all(): return lax.all_to_all(copies, axis, split_axis=0, concat_axis=0, tiled=True)]
    all_to_all x1 -> x0, waiting for transfers between devices: 10 us -> none  [sent_to_all(): return lax.all_to_all(copies, axis, split_axis=0, concat_axis=0, tiled=True)]
    all_to_all x1 -> x0, starting transfers between devices: 4.34 us -> none  [sent_to_all(): return lax.all_to_all(copies, axis, split_axis=0, concat_axis=0, tiled=True)]
    all_to_all x2, waiting for transfers between devices: 9.98 us -> 8.24 us  [exchanged(): return lax.all_to_all(copies, axis, split_axis=0, concat_axis=0, tiled=True)]
  transfers between devices with their start and end apart: 3 -> 2, of which waited for: 3 -> 2; matrix products, arithmetic and copies ran while one was open for 1% -> 1% of each run, Pallas kernels for 3% -> 3%
where the time goes in v4:
time: 104 us; the launch traced here: 103 us
  blocking collectives  50 us (48%)
  Pallas kernels  22.2 us (21%)
  starting transfers between devices  16.4 us (16%)
  waiting for transfers between devices  8.24 us (8%)
  local copies, waits for them, and re-layouts  5.39 us (5%)
    all_to_all x2, blocking collectives, sent_to_all(): return lax.all_to_all(copies, axis, split_axis=0, concat_axis=0, tiled=True)  31.1 us
    all_to_all x2, blocking collectives, exchanged(): return lax.all_to_all(copies, axis, split_axis=0, concat_axis=0, tiled=True)  18.9 us
    all_to_all x2, starting transfers between devices, exchanged(): return lax.all_to_all(copies, axis, split_axis=0, concat_axis=0, tiled=True)  16.4 us
    all_to_all x2, waiting for transfers between devices, exchanged(): return lax.all_to_all(copies, axis, split_axis=0, concat_axis=0, tiled=True)  8.24 us
    pallas_call x1, Pallas kernels, solve(): pl.pallas_call(first_kernel, out_shape=[jax.ShapeDtypeStruct((ITERS - 1,...  8.16 us
    pallas_call x1, Pallas kernels, solve(): pl.pallas_call(second_kernel, out_shape=rows_of((first_count, 1, H), pair...  7.43 us
    unnamed x10, local copies, waits for them, and re-layouts  3.26 us
    pallas_call x1, Pallas kernels, compat_matrix(): pl.pallas_call(compat_kernel, out_shape=jax.ShapeDtypeStruct((H, PADDED),...  3.08 us
  transfers between devices with their start and end apart: 2, of which 2 were waited for; matrix products, arithmetic and copies ran while one was open for 1% of the time, Pallas kernels for 3%

profile of v4, /device:TPU:8, one launch (start us, length us, event | category | flops | bytes accessed | tf_op | source)
XLA Modules:
  0.0 103.2 jit_solution(16598489918626885114)
XLA Ops:
  0.6 0.0 copy-start.2
  0.6 0.0 copy-start.4
  0.7 1.7 %pack.1 = s32[4,80,128]{2,1,0:T(8,128)} custom-call(s32[1,1]{1,0:T(1,128)} %bitcast.1.first_hand_ref, s32[22,4,256]{2,1,0:T(4,128)} %bitcast.9, s32[22,256]{1,0:T(8,128)} %bitcast.10, s32[1,256]{1,0:T(1,128)} %bitcast.12, s32[4,2,256]{2,1,0:T(2,128)} %bitcast.11), custom_call_target="tpu_custom_call" | custom-call | tf_op jit(solution)/shard_map/pack/pallas_call | solution.py:473
  2.4 4.3 %all-to-all-start = ((s32[4,80,128]{2,1,0:T(8,128)}), s32[4,80,128]{2,1,0:T(8,128)S(1)}, u32[]{:S(2)}, u32[]{:S(2)}) async-start(s32[4,80,128]{2,1,0:T(8,128)} %pack.1), calls=%async_computation | async-start | bytes 327680 | tf_op jit(solution)/shard_map/all_to_all | solution.py:434
  6.7 6.5 %all-to-all-done.slots_ref = s32[4,80,128]{2,1,0:T(8,128)S(1)} async-done(((s32[4,80,128]{2,1,0:T(8,128)}), s32[4,80,128]{2,1,0:T(8,128)S(1)}, u32[]{:S(2)}, u32[]{:S(2)}) %all-to-all-start) | async-done | bytes 163872 | tf_op jit(solution)/shard_map/all_to_all | solution.py:434
  13.1 1.2 %route.1 = s32[64,1,256]{2,1,0:T(1,128)} custom-call(s32[1,1]{1,0:T(1,128)} %bitcast.group_ref, s32[4,80,128]{2,1,0:T(8,128)S(1)} %all-to-all-done.slots_ref), custom_call_target="tpu_custom_call" | custom-call | tf_op jit(solution)/shard_map/route/pallas_call | solution.py:526
  14.3 12.1 %all-to-all-start.1 = ((s32[64,1,256]{2,1,0:T(1,128)}), s32[64,1,256]{2,1,0:T(1,128)S(1)}, u32[]{:S(2)}, u32[]{:S(2)}) async-start(s32[64,1,256]{2,1,0:T(1,128)} %route.1), calls=%async_computation.1 | async-start | bytes 131072 | tf_op jit(solution)/shard_map/all_to_all | solution.py:434
  26.4 0.7 reshape.38.one_ref
  27.1 0.7 reshape.39.two_ref
  27.8 0.0 copy-start.1
  27.8 0.7 copy-done.1
  28.5 0.0 copy-start.3
  28.5 0.7 copy-done.3
  29.2 3.1 %compat.1.compat_hbm_ref = bf16[1408,1408]{1,0:T(8,128)(2,1)S(1)} custom-call(s32[1,1408]{1,0:T(1,128)S(1)} %copy-done.3, s32[1,1408]{1,0:T(1,128)S(1)} %copy-done.1), custom_call_target="tpu_custom_call" | custom-call | tf_op jit(solution)/shard_map/compat/pallas_call | solution.py:78
  32.3 0.0 copy-start
  32.3 1.9 %copy-done = bf16[1408,1408]{1,0:T(8,128)(2,1)} copy-done((bf16[1408,1408]{1,0:T(8,128)(2,1)}, bf16[1408,1408]{1,0:T(8,128)(2,1)S(1)}, u32[]{:S(2)}) %copy-start) | copy-done | bytes 3964952
  34.2 1.8 %all-to-all-done.1.arrived_ref = s32[64,1,256]{2,1,0:T(1,128)S(1)} async-done(((s32[64,1,256]{2,1,0:T(1,128)}), s32[64,1,256]{2,1,0:T(1,128)S(1)}, u32[]{:S(2)}, u32[]{:S(2)}) %all-to-all-start.1) | async-done | bytes 65568 | tf_op jit(solution)/shard_map/all_to_all | solution.py:434
  36.0 0.0 copy-done.2
  36.0 0.0 copy-done.4
  36.0 8.2 %first.1 = (s32[3,2,1408]{2,1,0:T(2,128)S(1)}, f32[2,1408]{1,0:T(2,128)S(1)}, f32[2,1]{1,0:T(2,128)S(1)}, f32[16,1,2816]{2,1,0:T(1,128)S(1)}, f32[2,1408]{1,0:T(...) custom-call(s32[64,1,256]{2,1,0:T(1,128)S(1)} %all-to-all-done.1.arr, ...), custom_call_target="tpu_custom_call" | custom-call | tf_op jit(solution)/shard_map/first/pallas_call | solution.py:403
  44.1 9.9 %all_to_all.30 = f32[16,1,2816]{2,1,0:T(1,128)S(1)} all-to-all(f32[16,1,2816]{2,1,0:T(1,128)S(1)} %get-tuple-element.27), channel_id=1, replica_groups=mesh['grp_0'=2,'grp_1'=2,'inf_0'=4,'inf_1'=8,'inf_2'=2] {'grp_1','inf_0'..., dimensions={0} | all-to-all | bytes 360448 | tf_op jit(solution)/shard_map/all_to_all | solution.py:434
  54.0 0.1 reduce_sum.18
  54.1 0.1 broadcast_in_dim.6
  54.2 17.0 %all_to_all.31.sums_in_ref = f32[16,1,2816]{2,1,0:T(1,128)S(1)} all-to-all(f32[16,1,2816]{2,1,0:T(1,128)S(1)} %broadcast_in_dim.6), channel_id=1, replica_groups=mesh['grp_0'=2,'grp_1'=2,'inf_0'=4,'inf_1'=8,'inf_2'=2] {'grp_0','inf_1'}, dimensions={0} | all-to-all | bytes 360448 | tf_op jit(solution)/shard_map/all_to_all | solution.py:25
  71.2 7.4 %second.1 = (f32[16,1,1408]{2,1,0:T(1,128)S(1)}, f32[2,1408]{1,0:T(2,128)S(1)}, f32[2,1408]{1,0:T(2,128)S(1)}, f32[6,2,1408]{2,1,0:T(2,128)S(1)}, f32[3,1408]{1,0:T(4,128)S(1)}) custom-call(s32[3,2,1408]{2,1,0:T(2,128)S(1)} %get-tuple-element.25.key_ref, f32[2,1408]{1,0:T(2,128)S(1)} %get-tuple-element.24.live_ref, f32[1,1408]{1,0:T(1,128)S(1)} %reshape.38.one_ref, ...), custom_call_target="tpu_custom_call" | custom-call | tf_op jit(solution)/shard_map/second/pallas_call | solution.py:415
  78.6 9.0 %all_to_all.32 = f32[16,1,1408]{2,1,0:T(1,128)S(1)} all-to-all(f32[16,1,1408]{2,1,0:T(1,128)S(1)} %get-tuple-element.39), channel_id=1, replica_groups=mesh['grp_0'=2,'grp_1'=2,'inf_0'=4,'inf_1'=8,'inf_2'=2] {'grp_1','inf_0'..., dimensions={0} | all-to-all | bytes 180224 | tf_op jit(solution)/shard_map/all_to_all | solution.py:434
  87.6 0.1 reduce_sum.19
  87.7 14.2 %all_to_all.33.sums_in_ref = f32[16,1,1408]{2,1,0:T(1,128)S(1)} all-to-all(f32[16,1,1408]{2,1,0:T(1,128)S(1)} %broadcast_in_dim.7), channel_id=1, replica_groups=mesh['grp_0'=2,'grp_1'=2,'inf_0'=4,'inf_1'=8,'inf_2'=2] {'grp_0','inf_1'}, dimensions={0} | all-to-all | bytes 180224 | tf_op jit(solution)/shard_map/all_to_all | solution.py:25
  101.9 0.7 last.1
  102.6 0.6 dynamic-slice_bitcast_fusion
  (1 shorter events, 0.0 us)
Async XLA Ops:
  0.6 35.3 %copy-start.2 = (s32[1,1408]{1,0:T(1,128)S(1)}, s32[1,1408]{1,0:T(1,128)}, u32[]{:S(2)}) copy-start(s32[1,1408]{1,0:T(1,128)} %constant.40.high_ref) | copy-start | bytes 16900
  0.6 35.3 %copy-start.4 = (s32[1,1408]{1,0:T(1,128)S(1)}, s32[1,1408]{1,0:T(1,128)}, u32[]{:S(2)}) copy-start(s32[1,1408]{1,0:T(1,128)} %constant.39.low_ref) | copy-start | bytes 16900
  2.4 10.7 %all-to-all-start = ((s32[4,80,128]{2,1,0:T(8,128)}), s32[4,80,128]{2,1,0:T(8,128)S(1)}, u32[]{:S(2)}, u32[]{:S(2)}) async-start(s32[4,80,128]{2,1,0:T(8,128)} %pack.1), calls=%async_computation | async-start | bytes 327680 | tf_op jit(solution)/shard_map/all_to_all | solution.py:434
  14.3 21.7 %all-to-all-start.1 = ((s32[64,1,256]{2,1,0:T(1,128)}), s32[64,1,256]{2,1,0:T(1,128)S(1)}, u32[]{:S(2)}, u32[]{:S(2)}) async-start(s32[64,1,256]{2,1,0:T(1,128)} %route.1), calls=%async_computation.1 | async-start | bytes 131072 | tf_op jit(solution)/shard_map/all_to_all | solution.py:434
  27.8 0.7 copy-start.1
  28.5 0.7 copy-start.3
  32.3 1.9 %copy-start = (bf16[1408,1408]{1,0:T(8,128)(2,1)}, bf16[1408,1408]{1,0:T(8,128)(2,1)S(1)}, u32[]{:S(2)}) copy-start(bf16[1408,1408]{1,0:T(8,128)(2,1)S(1)} %compat.1.compat_hbm_ref) | copy-start | bytes 11894788

commit v5 on v4

--- a/solution.py
+++ b/solution.py
@@ -56,7 +56,10 @@
 SECOND_SUM = ("grp_0", "inf_1")
 
 
-def compat_kernel(low_ref, high_ref, out_ref):
+def compat_kernel(cards_ref, out_ref):
+    low_ref = cards_ref.at[0:1]
+    high_ref = cards_ref.at[1:2]
+
     def rows(step, carry):
         first = pl.multiple_of(step * BLOCK, BLOCK)
         low_col = jnp.broadcast_to(low_ref[:, pl.ds(first, BLOCK)], (BLOCK, BLOCK)).T
@@ -74,13 +77,13 @@
     lax.fori_loop(0, H // BLOCK, rows, 0)
 
 
-def compat_matrix(low, high):
+def compat_matrix(cards):
     return pl.pallas_call(
         compat_kernel,
         out_shape=jax.ShapeDtypeStruct((H, PADDED), jnp.bfloat16),
         name="compat",
         compiler_params=pltpu.CompilerParams(vmem_limit_bytes=12 << 20),
-    )(low, high)
+    )(cards)
 
 
 def pair_sums(key_ref, counter, columns, compat_ref, lhs_ref, low_ref, sums_ref, col_ref, fetch=None):
@@ -212,19 +215,20 @@
     return part[0:1, :] + part[1:2, :]
 
 
-def add_parts(parts_ref, start):
-    total = parts_ref[0, :, start : start + H]
+def add_parts(parts_ref):
+    total = parts_ref[0]
     for k in range(1, parts_ref.shape[0]):
-        total = total + parts_ref[k, :, start : start + H]
+        total = total + parts_ref[k]
     return total
 
 
-def spread(copies_ref, start, value):
-    for k in range(copies_ref.shape[0]):
-        copies_ref[k, :, start : start + H] = value
-
-
-def read_flops(arrived_ref, low_ref, high_ref, key_ref, live_ref, share_ref):
+def spread(copies_ref, value, part=0, parts=1):
+    count = copies_ref.shape[0] // parts
+    for k in range(count * part, count * (part + 1)):
+        copies_ref[k] = value
+
+
+def read_flops(arrived_ref, cards_ref, key_ref, live_ref, share_ref):
     used = key_ref.shape[0]
     shards = arrived_ref.shape[0]
     hand_block = H // shards
@@ -237,8 +241,8 @@
                     counter, flop : flop + 1, hand_block * shard : hand_block * (shard + 1)
                 ] = line[:, first : first + hand_block]
     live_ref[...] = (key_ref[0, :, :H] >= 0).astype(jnp.float32)
-    low = low_ref[...]
-    high = high_ref[...]
+    low = cards_ref[0:1, :]
+    high = cards_ref[1:2, :]
     for flop in range(2):
         first = LINE * flop + hand_block * used
         extra = arrived_ref[0, :, first : first + 1 + 2 * used]
@@ -253,7 +257,7 @@
 
 
 def first_kernel(
-    arrived_ref, low_ref, high_ref, one_ref, two_ref, compat_hbm_ref,
+    arrived_ref, cards_ref, one_ref, two_ref, compat_hbm_ref,
     key_ref, live_ref, share_ref, cont_ref,
     root_check_ref, root_bet_ref, fc_fold_ref, fc_call_ref,
     ac_check_ref, ac_bet_ref, fb_fold_ref, fb_call_ref, share_root_ref, share_fc_ref, turn_ref,
@@ -262,7 +266,7 @@
     fetch = pltpu.make_async_copy(compat_hbm_ref, compat_ref, compat_sem)
     fetch.start()
     scratch = (compat_ref, lhs_ref, low_part_ref, sums_ref, col_ref)
-    read_flops(arrived_ref, low_ref, high_ref, key_ref, live_ref, share_ref)
+    read_flops(arrived_ref, cards_ref, key_ref, live_ref, share_ref)
     live = live_ref[...]
     share = share_ref[...]
     zero = jnp.zeros((2, H), jnp.float32)
@@ -274,7 +278,7 @@
     two_cols = two_columns(two_all, start, start)
     sign_sum, weight_sum = pair_sums(key_ref, 0, {**two_cols, **one_cols}, *scratch, fetch)
     values = two_values(sign_sum, weight_sum, start, start)
-    spread(cont_ref, 0, flop_value(share, values[5]))
+    spread(cont_ref, flop_value(share, values[5]), 0, 2)
     regrets = two_regrets((zero, zero, zero, zero), values)
     others = one_regrets((zero, zero, zero, zero), one_values(sign_sum, weight_sum, start, start))
     turns = [*one_rows(one_cols), *two_rows(two_cols)]
@@ -286,7 +290,7 @@
     )
     sign_sum, weight_sum = pair_sums(key_ref, 1, two_cols, *scratch)
     values = two_values(sign_sum, weight_sum, share_root, share_fc)
-    spread(cont_ref, H, flop_value(share, values[5]))
+    spread(cont_ref, flop_value(share, values[5]), 1, 2)
     regrets = two_regrets(regrets, values)
     for k, row in enumerate(two_rows(two_cols)):
         turns[3 + k] = turns[3 + k] + 2.0 * row
@@ -299,7 +303,8 @@
 
 
 def second_kernel(
-    key_ref, live_ref, one_ref, two_ref, share_ref, compat_hbm_ref, sums_in_ref,
+    key_ref, live_ref, one_ref, two_ref, share_ref, compat_hbm_ref,
+    core_ref, own_sum_ref, other_sum_ref,
     root_check_ref, root_bet_ref, fc_fold_ref, fc_call_ref,
     ac_check_ref, ac_bet_ref, fb_fold_ref, fb_call_ref, share_root_ref, share_fc_ref, turn_ref,
     cont_ref, out_root_ref, out_fc_ref, out_turn_ref, out_pre_ref,
@@ -308,13 +313,16 @@
     fetch = pltpu.make_async_copy(compat_hbm_ref, compat_ref, compat_sem)
     fetch.start()
     scratch = (compat_ref, lhs_ref, low_ref, sums_ref, col_ref)
+    first_core = core_ref[0, 0] == 0
+    own_sum = own_sum_ref[...]
+    other_sum = other_sum_ref[...]
     live = live_ref[...]
     zero_row = jnp.zeros((1, H), jnp.float32)
     two_all = two_ref[...] * live
     one_range = one_ref[...]
     turns = [turn_ref[k] for k in range(6)]
     pre_sum = one_range * action_share(zero_row, zero_row)
-    pre_cont, pre_fold = pre_step(zero_row, zero_row, add_parts(sums_in_ref, 0))
+    pre_cont, pre_fold = pre_step(zero_row, zero_row, jnp.where(first_core, own_sum, other_sum))
     one_now = one_range * action_share(pre_cont, pre_fold)
     pre_sum = pre_sum + 2.0 * one_now
     one_cols = one_columns(one_now * live, share_root_ref[...], share_fc_ref[...])
@@ -326,7 +334,7 @@
     sign_sum, weight_sum = pair_sums(key_ref, 1, one_cols, *scratch, fetch)
     others = one_regrets(others, one_values(sign_sum, weight_sum, share_ac, share_fb))
 
-    pre_cont, pre_fold = pre_step(pre_cont, pre_fold, add_parts(sums_in_ref, H))
+    pre_cont, pre_fold = pre_step(pre_cont, pre_fold, jnp.where(first_core, other_sum, own_sum))
     one_now = one_range * action_share(pre_cont, pre_fold)
     pre_sum = pre_sum + 3.0 * one_now
     regrets = (root_check_ref[...], root_bet_ref[...], fc_fold_ref[...], fc_call_ref[...])
@@ -340,7 +348,7 @@
         turns[k] = turns[k] + 3.0 * row
     sign_sum, weight_sum = pair_sums(key_ref, 2, {**two_cols, **one_cols}, *scratch)
     values = two_values(sign_sum, weight_sum, share_root, share_fc)
-    spread(cont_ref, 0, flop_value(share_ref[...], values[5]))
+    spread(cont_ref, flop_value(share_ref[...], values[5]))
     regrets = two_regrets(regrets, values)
     others = one_regrets(others, one_values(sign_sum, weight_sum, share_ac, share_fb))
     two_cols = two_columns(
@@ -385,7 +393,7 @@
     out_ref, pre_out_ref,
 ):
     total_weight = ITERS * (ITERS + 1) / 2.0
-    pre_cont, pre_fold = pre_step(pre_ref[0:1, :], pre_ref[1:2, :], add_parts(sums_in_ref, 0))
+    pre_cont, pre_fold = pre_step(pre_ref[0:1, :], pre_ref[1:2, :], add_parts(sums_in_ref))
     one_now = one_ref[...] * action_share(pre_cont, pre_fold)
     columns = one_columns(one_now * live_ref[...], share_root_ref[...], share_fc_ref[...])
     for k, row in enumerate(one_rows(columns)):
@@ -395,7 +403,7 @@
     pre_out_ref[...] = (pre_ref[2:3, :] + 4.0 * one_now) / total_weight
 
 
-def solve(arrived, range_one, range_two, low, high, compat):
+def solve(arrived, range_one, range_two, cards, compat):
     one_row = range_one.reshape(1, H)
     two_row = range_two.reshape(1, H)
     pair = (2, H)
@@ -404,22 +412,26 @@
         first_kernel,
         out_shape=[
             jax.ShapeDtypeStruct((ITERS - 1, 2, PADDED), jnp.int32),
-            *rows_of(pair, (2, 1), (first_count, 1, 2 * H), *([pair] * 10), (6, 2, H)),
+            *rows_of(pair, (2, 1), (first_count, 1, H), *([pair] * 10), (6, 2, H)),
         ],
-        in_specs=[*in_vmem(5), in_hbm()],
+        in_specs=[*in_vmem(4), in_hbm()],
         scratch_shapes=pair_scratch(),
         name="first",
         compiler_params=pltpu.CompilerParams(vmem_limit_bytes=20 << 20),
-    )(arrived, low, high, one_row, two_row, compat)
-    parts = whole_parts(cont)
+    )(arrived, cards, one_row, two_row, compat)
+    own_sum = jnp.sum(whole_parts(cont), axis=0)
+    other_sum = lax.ppermute(own_sum, "grp_1", [(0, 1), (1, 0)])
+    core = lax.axis_index("grp_1").astype(jnp.int32).reshape(1, 1)
     cont, share_root, share_fc, turns, pre = pl.pallas_call(
         second_kernel,
         out_shape=rows_of((first_count, 1, H), pair, pair, (6, 2, H), (3, H)),
-        in_specs=[*in_vmem(5), in_hbm(), *in_vmem(12)],
+        in_specs=[
+            *in_vmem(5), in_hbm(), pl.BlockSpec(memory_space=pltpu.SMEM), *in_vmem(13)
+        ],
         scratch_shapes=pair_scratch(),
         name="second",
         compiler_params=pltpu.CompilerParams(vmem_limit_bytes=20 << 20),
-    )(key_now, live, one_row, two_row, share, compat, parts, *state)
+    )(key_now, live, one_row, two_row, share, compat, core, own_sum, other_sum, *state)
     parts = whole_parts(cont)
     turns, pre = pl.pallas_call(
         last_kernel,
@@ -538,19 +550,16 @@
     shard_id = lax.axis_index(INF)
     hand_block = strength.shape[2]
     first_hand = shard_id * hand_block
-    low, high = (jnp.asarray(table).reshape(1, PADDED) for table in hand_cards(PADDED, HANDS))
+    cards = jnp.asarray(np.stack(hand_cards(PADDED, HANDS)))
     slots = exchanged(
         packed(first_hand, strength, board_mask, flop_weight, runout, groups), GRP
     )
-    arrived = exchanged(route(slots, lax.axis_index(GRP), shards), INF)
-    turn_reach, pre_reach = solve(
-        arrived,
-        range_one,
-        range_two,
-        low,
-        high,
-        pltpu.with_memory_space_constraint(compat_matrix(low, high), pltpu.HBM),
-    )
+    slots, compat = lax.optimization_barrier((slots, compat_matrix(cards)))
+    routed = route(slots, lax.axis_index(GRP), shards)
+    routed, compat = lax.optimization_barrier((routed, compat))
+    arrived = exchanged(routed, INF)
+    compat = pltpu.with_memory_space_constraint(compat, pltpu.HBM)
+    turn_reach, pre_reach = solve(arrived, range_one, range_two, cards, compat)
     return turn_reach, lax.dynamic_slice(
         pre_reach, (first_hand,), (hand_block,), allow_negative_indices=False
     )

time: 104 us -> 101 us (0.971)
  blocking collectives: 50 us -> 45.6 us
  waiting for transfers between devices: 8.24 us -> 11.4 us
  local copies, waits for them, and re-layouts: 5.39 us -> 3.29 us
    all_to_all x2, blocking collectives: 31.1 us -> 27.6 us  [sent_to_all(): return lax.all_to_all(copies, axis, split_axis=0, concat_axis=0, tiled=True)]
    all_to_all x2, waiting for transfers between devices: 8.24 us -> 10.3 us  [exchanged(): return lax.all_to_all(copies, axis, split_axis=0, concat_axis=0, tiled=True)]
    ppermute x0 -> x1, waiting for transfers between devices: none -> 1.16 us  [solve(): other_sum = lax.ppermute(own_sum, 'grp_1', [(0, 1), (1, 0)])]
  transfers between devices with their start and end apart: 2 -> 3, of which waited for: 2 -> 3; matrix products, arithmetic and copies ran while one was open for 1% -> 0% of each run, Pallas kernels for 3% -> 3%
where the time goes in v5:
time: 101 us; the launch traced here: 100 us
  blocking collectives  45.6 us (45%)
  Pallas kernels  22.3 us (22%)
  starting transfers between devices  16.7 us (17%)
  waiting for transfers between devices  11.4 us (11%)
  local copies, waits for them, and re-layouts  3.29 us (3%)
    all_to_all x2, blocking collectives, sent_to_all(): return lax.all_to_all(copies, axis, split_axis=0, concat_axis=0, tiled=True)  27.6 us
    all_to_all x2, blocking collectives, exchanged(): return lax.all_to_all(copies, axis, split_axis=0, concat_axis=0, tiled=True)  18.1 us
    all_to_all x2, starting transfers between devices, exchanged(): return lax.all_to_all(copies, axis, split_axis=0, concat_axis=0, tiled=True)  16.4 us
    all_to_all x2, waiting for transfers between devices, exchanged(): return lax.all_to_all(copies, axis, split_axis=0, concat_axis=0, tiled=True)  10.3 us
    pallas_call x1, Pallas kernels, solve(): pl.pallas_call(first_kernel, out_shape=[jax.ShapeDtypeStruct((ITERS - 1,...  8.21 us
    pallas_call x1, Pallas kernels, solve(): pl.pallas_call(second_kernel, out_shape=rows_of((first_count, 1, H), pair...  7.46 us
    pallas_call x1, Pallas kernels, compat_matrix(): pl.pallas_call(compat_kernel, out_shape=jax.ShapeDtypeStruct((H, PADDED),...  3.08 us
    unnamed x10, local copies, waits for them, and re-layouts  2.59 us
  transfers between devices with their start and end apart: 3, of which 3 were waited for; matrix products, arithmetic and copies ran while one was open for 0% of the time, Pallas kernels for 3%

profile of v5, /device:TPU:8, one launch (start us, length us, event | category | flops | bytes accessed | tf_op | source)
XLA Modules:
  0.0 100.3 jit_solution(14104682069834879365)
XLA Ops:
  0.6 0.0 copy-start.2
  0.6 0.0 copy-start.3
  0.7 0.0 copy-start.4
  0.7 1.7 %pack.1 = s32[4,80,128]{2,1,0:T(8,128)} custom-call(s32[1,1]{1,0:T(1,128)} %bitcast.1.first_hand_ref, s32[22,4,256]{2,1,0:T(4,128)} %bitcast.10, s32[22,256]{1,0:T(8,128)} %bitcast.11, s32[1,256]{1,0:T(1,128)} %bitcast.13, s32[4,2,256]{2,1,0:T(2,128)} %bitcast.12), custom_call_target="tpu_custom_call" | custom-call | tf_op jit(solution)/shard_map/pack/pallas_call | solution.py:485
  2.4 4.3 %all-to-all-start = ((s32[4,80,128]{2,1,0:T(8,128)}), s32[4,80,128]{2,1,0:T(8,128)S(1)}, u32[]{:S(2)}, u32[]{:S(2)}) async-start(s32[4,80,128]{2,1,0:T(8,128)} %pack.1), calls=%async_computation | async-start | bytes 327680 | tf_op jit(solution)/shard_map/all_to_all | solution.py:446
  6.7 0.0 copy-start.1
  6.7 0.7 copy-done.1
  7.4 3.1 %compat.1.compat_hbm_ref = bf16[1408,1408]{1,0:T(8,128)(2,1)S(1)} custom-call(s32[2,1408]{1,0:T(2,128)S(1)} %copy-done.1), custom_call_target="tpu_custom_call" | custom-call | tf_op jit(solution)/shard_map/compat/pallas_call | solution.py:81
  10.5 0.0 copy-start
  10.5 1.9 %copy-done = bf16[1408,1408]{1,0:T(8,128)(2,1)} copy-done((bf16[1408,1408]{1,0:T(8,128)(2,1)}, bf16[1408,1408]{1,0:T(8,128)(2,1)S(1)}, u32[]{:S(2)}) %copy-start) | copy-done | bytes 3964952
  12.4 0.8 all-to-all-done.slots_ref
  13.1 1.2 %route.1 = s32[64,1,256]{2,1,0:T(1,128)} custom-call(s32[1,1]{1,0:T(1,128)} %bitcast.group_ref, s32[4,80,128]{2,1,0:T(8,128)S(1)} %all-to-all-done.slots_ref), custom_call_target="tpu_custom_call" | custom-call | tf_op jit(solution)/shard_map/route/pallas_call | solution.py:538
  14.3 12.1 %all-to-all-start.1 = ((s32[64,1,256]{2,1,0:T(1,128)}), s32[64,1,256]{2,1,0:T(1,128)S(1)}, u32[]{:S(2)}, u32[]{:S(2)}) async-start(s32[64,1,256]{2,1,0:T(1,128)} %route.1), calls=%async_computation.1 | async-start | bytes 131072 | tf_op jit(solution)/shard_map/all_to_all | solution.py:446
  26.4 0.0 copy-done.3
  26.5 0.0 copy-done.4
  26.5 9.5 %all-to-all-done.1.arrived_ref = s32[64,1,256]{2,1,0:T(1,128)S(1)} async-done(((s32[64,1,256]{2,1,0:T(1,128)}), s32[64,1,256]{2,1,0:T(1,128)S(1)}, u32[]{:S(2)}, u32[]{:S(2)}) %all-to-all-start.1) | async-done | bytes 65568 | tf_op jit(solution)/shard_map/all_to_all | solution.py:446
  36.0 0.0 copy-done.2
  36.0 8.2 %first.1 = (s32[3,2,1408]{2,1,0:T(2,128)S(1)}, f32[2,1408]{1,0:T(2,128)S(1)}, f32[2,1]{1,0:T(2,128)S(1)}, f32[16,1,1408]{2,1,0:T(1,128)S(1)}, f32[2,1408]{1,0:T(...) custom-call(s32[64,1,256]{2,1,0:T(1,128)S(1)} %all-to-all-done.1.arr, ...), custom_call_target="tpu_custom_call" | custom-call | tf_op jit(solution)/shard_map/first/pallas_call | solution.py:411
  44.2 9.1 %all_to_all.30 = f32[16,1,1408]{2,1,0:T(1,128)S(1)} all-to-all(f32[16,1,1408]{2,1,0:T(1,128)S(1)} %get-tuple-element.35), channel_id=1, replica_groups=mesh['grp_0'=2,'grp_1'=2,'inf_0'=4,'inf_1'=8,'inf_2'=2] {'grp_1','inf_0'..., dimensions={0} | all-to-all | bytes 180224 | tf_op jit(solution)/shard_map/all_to_all | solution.py:446
  53.3 0.1 reduce_sum.29
  53.4 14.9 %all_to_all.31 = f32[16,1,1408]{2,1,0:T(1,128)S(1)} all-to-all(f32[16,1,1408]{2,1,0:T(1,128)S(1)} %broadcast_in_dim.6), channel_id=1, replica_groups=mesh['grp_0'=2,'grp_1'=2,'inf_0'=4,'inf_1'=8,'inf_2'=2] {'grp_0','inf_1'}, dimensions={0} | all-to-all | bytes 180224 | tf_op jit(solution)/shard_map/all_to_all | solution.py:25
  68.3 0.1 reduce_sum.30
  68.4 0.3 collective-permute-start
  68.6 1.2 %collective-permute-done.other_sum_ref = f32[1,1408]{1,0:T(1,128)S(1)} collective-permute-done((f32[1,1408]{1,0:T(1,128)S(1)}, f32[1,1408]{1,0:T(1,128)S(1)}, u32[]{:S(2)}, u32[]{:S(2)}) %collective-permute-start) | collective-permute-done | bytes 5664 | tf_op jit(solution)/shard_map/ppermute | solution.py:423
  69.8 7.5 %second.1 = (f32[16,1,1408]{2,1,0:T(1,128)S(1)}, f32[2,1408]{1,0:T(2,128)S(1)}, f32[2,1408]{1,0:T(2,128)S(1)}, f32[6,2,1408]{2,1,0:T(2,128)S(1)}, f32[3,1408]{1,0:T(4,128)S(1)}) custom-call(s32[3,2,1408]{2,1,0:T(2,128)S(1)} %get-tuple-element.33.key_ref, f32[2,1408]{1,0:T(2,128)S(1)} %get-tuple-element.32.live_ref, f32[1,1408]{1,0:T(1,128)S(1)} %reshape.34.one_ref, ...), custom_call_target="tpu_custom_call" | custom-call | tf_op jit(solution)/shard_map/second/pallas_call | solution.py:425
  77.3 9.0 %all_to_all.32 = f32[16,1,1408]{2,1,0:T(1,128)S(1)} all-to-all(f32[16,1,1408]{2,1,0:T(1,128)S(1)} %get-tuple-element.47), channel_id=1, replica_groups=mesh['grp_0'=2,'grp_1'=2,'inf_0'=4,'inf_1'=8,'inf_2'=2] {'grp_1','inf_0'..., dimensions={0} | all-to-all | bytes 180224 | tf_op jit(solution)/shard_map/all_to_all | solution.py:446
  86.2 0.1 reduce_sum.32
  86.4 12.7 %all_to_all.33.sums_in_ref = f32[16,1,1408]{2,1,0:T(1,128)S(1)} all-to-all(f32[16,1,1408]{2,1,0:T(1,128)S(1)} %broadcast_in_dim.7), channel_id=1, replica_groups=mesh['grp_0'=2,'grp_1'=2,'inf_0'=4,'inf_1'=8,'inf_2'=2] {'grp_0','inf_1'}, dimensions={0} | all-to-all | bytes 180224 | tf_op jit(solution)/shard_map/all_to_all | solution.py:25
  99.1 0.7 last.1
  99.7 0.6 dynamic-slice_bitcast_fusion
  (5 shorter events, 0.1 us)
Async XLA Ops:
  0.6 35.3 %copy-start.2 = (s32[2,1408]{1,0:T(2,128)S(1)}, s32[2,1408]{1,0:T(2,128)}, u32[]{:S(2)}) copy-start(s32[2,1408]{1,0:T(2,128)} %constant.33.clone.cards_ref) | copy-start | bytes 33796
  0.6 25.8 %copy-start.3 = (f32[1408]{0:T(1024)S(1)}, f32[1408]{0:T(1024)}, u32[]{:S(2)}) copy-start(f32[1408]{0:T(1024)} %param.7) | copy-start | bytes 16900
  0.7 25.8 %copy-start.4 = (f32[1408]{0:T(1024)S(1)}, f32[1408]{0:T(1024)}, u32[]{:S(2)}) copy-start(f32[1408]{0:T(1024)} %param.8) | copy-start | bytes 16900
  2.4 10.7 %all-to-all-start = ((s32[4,80,128]{2,1,0:T(8,128)}), s32[4,80,128]{2,1,0:T(8,128)S(1)}, u32[]{:S(2)}, u32[]{:S(2)}) async-start(s32[4,80,128]{2,1,0:T(8,128)} %pack.1), calls=%async_computation | async-start | bytes 327680 | tf_op jit(solution)/shard_map/all_to_all | solution.py:446
  6.7 0.7 copy-start.1
  10.5 1.9 %copy-start = (bf16[1408,1408]{1,0:T(8,128)(2,1)}, bf16[1408,1408]{1,0:T(8,128)(2,1)S(1)}, u32[]{:S(2)}) copy-start(bf16[1408,1408]{1,0:T(8,128)(2,1)S(1)} %compat.1.compat_hbm_ref) | copy-start | bytes 11894788
  14.3 21.7 %all-to-all-start.1 = ((s32[64,1,256]{2,1,0:T(1,128)}), s32[64,1,256]{2,1,0:T(1,128)S(1)}, u32[]{:S(2)}, u32[]{:S(2)}) async-start(s32[64,1,256]{2,1,0:T(1,128)} %route.1), calls=%async_computation.1 | async-start | bytes 131072 | tf_op jit(solution)/shard_map/all_to_all | solution.py:446
  68.4 1.4 %collective-permute-start = (f32[1,1408]{1,0:T(1,128)S(1)}, f32[1,1408]{1,0:T(1,128)S(1)}, u32[]{:S(2)}, u32[]{:S(2)}) collective-permute-start(f32[1,1408]{1,0:T(1,128)S(1)} %reduce_sum.31.own_sum_ref), channel_id=1, source_target_pairs={{0,64},{64,0},{1,65},{65,1},{2,66},{66,2},{3,67},{67,3},{4,68},{68... | collective-permute-start | bytes 16904 | tf_op jit(solution)/shard_map/ppermute | solution.py:423

commit v6 on v5

--- a/solution.py
+++ b/solution.py
@@ -56,9 +56,15 @@
 SECOND_SUM = ("grp_0", "inf_1")
 
 
-def compat_kernel(cards_ref, out_ref):
+def compat_kernel(cards_ref, out_ref, rows_ref, sems):
     low_ref = cards_ref.at[0:1]
     high_ref = cards_ref.at[1:2]
+
+    def sent(step):
+        first = pl.multiple_of(step * BLOCK, BLOCK)
+        return pltpu.make_async_copy(
+            rows_ref.at[step], out_ref.at[pl.ds(first, BLOCK)], sems.at[step]
+        )
 
     def rows(step, carry):
         first = pl.multiple_of(step * BLOCK, BLOCK)
@@ -69,18 +75,26 @@
             high_here = high_ref[:, start : start + BLOCK]
             apart = (low_col != low_here) & (low_col != high_here)
             apart = apart & (high_col != low_here) & (high_col != high_here)
-            out_ref[pl.ds(first, BLOCK), start : start + BLOCK] = jnp.where(
-                apart, 1.0, 0.0
-            ).astype(jnp.bfloat16)
+            rows_ref[step, :, start : start + BLOCK] = jnp.where(apart, 1.0, 0.0).astype(
+                jnp.bfloat16
+            )
+        sent(step).start()
         return carry
 
     lax.fori_loop(0, H // BLOCK, rows, 0)
+    for step in range(H // BLOCK):
+        sent(step).wait()
 
 
 def compat_matrix(cards):
     return pl.pallas_call(
         compat_kernel,
-        out_shape=jax.ShapeDtypeStruct((H, PADDED), jnp.bfloat16),
+        out_shape=pltpu.HBM((H, PADDED), jnp.bfloat16),
+        out_specs=pl.BlockSpec(memory_space=pltpu.HBM),
+        scratch_shapes=[
+            pltpu.VMEM((H // BLOCK, BLOCK, PADDED), jnp.bfloat16),
+            pltpu.SemaphoreType.DMA((H // BLOCK,)),
+        ],
         name="compat",
         compiler_params=pltpu.CompilerParams(vmem_limit_bytes=12 << 20),
     )(cards)

time: 101 us -> 100 us (0.990)
  local copies, waits for them, and re-layouts: 3.29 us -> 1.41 us
  waiting for transfers between devices: 11.4 us -> 12.5 us
    unnamed x10 -> x8, local copies, waits for them, and re-layouts: 2.59 us -> 0.72 us
    all_to_all x2, blocking collectives: 27.6 us -> 26.5 us  [sent_to_all(): return lax.all_to_all(copies, axis, split_axis=0, concat_axis=0, tiled=True)]
    all_to_all x2, waiting for transfers between devices: 10.3 us -> 11.3 us  [exchanged(): return lax.all_to_all(copies, axis, split_axis=0, concat_axis=0, tiled=True)]
  transfers between devices with their start and end apart: 3 -> 3, of which waited for: 3 -> 3; matrix products, arithmetic and copies ran while one was open for 0% -> 0% of each run, Pallas kernels for 3% -> 4%
where the time goes in v6:
time: 100 us; the launch traced here: 99.3 us
  blocking collectives  44.6 us (45%)
  Pallas kernels  23.1 us (23%)
  starting transfers between devices  16.7 us (17%)
  waiting for transfers between devices  12.5 us (12%)
  local copies, waits for them, and re-layouts  1.41 us (1%)
    all_to_all x2, blocking collectives, sent_to_all(): return lax.all_to_all(copies, axis, split_axis=0, concat_axis=0, tiled=True)  26.5 us
    all_to_all x2, blocking collectives, exchanged(): return lax.all_to_all(copies, axis, split_axis=0, concat_axis=0, tiled=True)  18.1 us
    all_to_all x2, starting transfers between devices, exchanged(): return lax.all_to_all(copies, axis, split_axis=0, concat_axis=0, tiled=True)  16.4 us
    all_to_all x2, waiting for transfers between devices, exchanged(): return lax.all_to_all(copies, axis, split_axis=0, concat_axis=0, tiled=True)  11.3 us
    pallas_call x1, Pallas kernels, solve(): pl.pallas_call(first_kernel, out_shape=[jax.ShapeDtypeStruct((ITERS - 1,...  8.21 us
    pallas_call x1, Pallas kernels, solve(): pl.pallas_call(second_kernel, out_shape=rows_of((first_count, 1, H), pair...  7.46 us
    pallas_call x1, Pallas kernels, compat_matrix(): pl.pallas_call(compat_kernel, out_shape=pltpu.HBM((H, PADDED), jnp.bfloat...  3.91 us
  transfers between devices with their start and end apart: 3, of which 3 were waited for; matrix products, arithmetic and copies ran while one was open for 0% of the time, Pallas kernels for 4%

profile of v6, /device:TPU:8, one launch (start us, length us, event | category | flops | bytes accessed | tf_op | source)
XLA Modules:
  0.0 99.3 jit_solution(13930616828768501669)
XLA Ops:
  0.6 0.0 copy-start.1
  0.6 0.0 copy-start.2
  0.7 0.0 copy-start.3
  0.7 1.7 %pack.1 = s32[4,80,128]{2,1,0:T(8,128)} custom-call(s32[1,1]{1,0:T(1,128)} %bitcast.1.first_hand_ref, s32[22,4,256]{2,1,0:T(4,128)} %bitcast.10, s32[22,256]{1,0:T(8,128)} %bitcast.11, s32[1,256]{1,0:T(1,128)} %bitcast.13, s32[4,2,256]{2,1,0:T(2,128)} %bitcast.12), custom_call_target="tpu_custom_call" | custom-call | tf_op jit(solution)/shard_map/pack/pallas_call | solution.py:499
  2.4 4.3 %all-to-all-start = ((s32[4,80,128]{2,1,0:T(8,128)}), s32[4,80,128]{2,1,0:T(8,128)S(1)}, u32[]{:S(2)}, u32[]{:S(2)}) async-start(s32[4,80,128]{2,1,0:T(8,128)} %pack.1), calls=%async_computation | async-start | bytes 327680 | tf_op jit(solution)/shard_map/all_to_all | solution.py:460
  6.7 0.0 copy-start
  6.7 0.7 copy-done
  7.4 3.9 %compat.1.compat_hbm_ref = bf16[1408,1408]{1,0:T(8,128)(2,1)} custom-call(s32[2,1408]{1,0:T(2,128)S(1)} %copy-done), custom_call_target="tpu_custom_call" | custom-call | tf_op jit(solution)/shard_map/compat/pallas_call | solution.py:90
  11.3 1.8 %all-to-all-done.slots_ref = s32[4,80,128]{2,1,0:T(8,128)S(1)} async-done(((s32[4,80,128]{2,1,0:T(8,128)}), s32[4,80,128]{2,1,0:T(8,128)S(1)}, u32[]{:S(2)}, u32[]{:S(2)}) %all-to-all-start) | async-done | bytes 163872 | tf_op jit(solution)/shard_map/all_to_all | solution.py:460
  13.1 1.2 %route.1 = s32[64,1,256]{2,1,0:T(1,128)} custom-call(s32[1,1]{1,0:T(1,128)} %bitcast.group_ref, s32[4,80,128]{2,1,0:T(8,128)S(1)} %all-to-all-done.slots_ref), custom_call_target="tpu_custom_call" | custom-call | tf_op jit(solution)/shard_map/route/pallas_call | solution.py:552
  14.3 12.1 %all-to-all-start.1 = ((s32[64,1,256]{2,1,0:T(1,128)}), s32[64,1,256]{2,1,0:T(1,128)S(1)}, u32[]{:S(2)}, u32[]{:S(2)}) async-start(s32[64,1,256]{2,1,0:T(1,128)} %route.1), calls=%async_computation.1 | async-start | bytes 131072 | tf_op jit(solution)/shard_map/all_to_all | solution.py:460
  26.5 0.0 copy-done.2
  26.5 0.0 copy-done.3
  26.5 9.5 %all-to-all-done.1.arrived_ref = s32[64,1,256]{2,1,0:T(1,128)S(1)} async-done(((s32[64,1,256]{2,1,0:T(1,128)}), s32[64,1,256]{2,1,0:T(1,128)S(1)}, u32[]{:S(2)}, u32[]{:S(2)}) %all-to-all-start.1) | async-done | bytes 65568 | tf_op jit(solution)/shard_map/all_to_all | solution.py:460
  36.0 0.0 copy-done.1
  36.0 8.2 %first.1 = (s32[3,2,1408]{2,1,0:T(2,128)S(1)}, f32[2,1408]{1,0:T(2,128)S(1)}, f32[2,1]{1,0:T(2,128)S(1)}, f32[16,1,1408]{2,1,0:T(1,128)S(1)}, f32[2,1408]{1,0:T(...) custom-call(s32[64,1,256]{2,1,0:T(1,128)S(1)} %all-to-all-done.1.arr, ...), custom_call_target="tpu_custom_call" | custom-call | tf_op jit(solution)/shard_map/first/pallas_call | solution.py:425
  44.2 9.1 %all_to_all.30 = f32[16,1,1408]{2,1,0:T(1,128)S(1)} all-to-all(f32[16,1,1408]{2,1,0:T(1,128)S(1)} %get-tuple-element.35), channel_id=1, replica_groups=mesh['grp_0'=2,'grp_1'=2,'inf_0'=4,'inf_1'=8,'inf_2'=2] {'grp_1','inf_0'..., dimensions={0} | all-to-all | bytes 180224 | tf_op jit(solution)/shard_map/all_to_all | solution.py:460
  53.3 0.1 reduce_sum.29
  53.5 13.8 %all_to_all.31 = f32[16,1,1408]{2,1,0:T(1,128)S(1)} all-to-all(f32[16,1,1408]{2,1,0:T(1,128)S(1)} %broadcast_in_dim.6), channel_id=1, replica_groups=mesh['grp_0'=2,'grp_1'=2,'inf_0'=4,'inf_1'=8,'inf_2'=2] {'grp_0','inf_1'}, dimensions={0} | all-to-all | bytes 180224 | tf_op jit(solution)/shard_map/all_to_all | solution.py:25
  67.2 0.1 reduce_sum.30
  67.3 0.3 collective-permute-start
  67.6 1.2 %collective-permute-done.other_sum_ref = f32[1,1408]{1,0:T(1,128)S(1)} collective-permute-done((f32[1,1408]{1,0:T(1,128)S(1)}, f32[1,1408]{1,0:T(1,128)S(1)}, u32[]{:S(2)}, u32[]{:S(2)}) %collective-permute-start) | collective-permute-done | bytes 5664 | tf_op jit(solution)/shard_map/ppermute | solution.py:437
  68.8 7.5 %second.1 = (f32[16,1,1408]{2,1,0:T(1,128)S(1)}, f32[2,1408]{1,0:T(2,128)S(1)}, f32[2,1408]{1,0:T(2,128)S(1)}, f32[6,2,1408]{2,1,0:T(2,128)S(1)}, f32[3,1408]{1,0:T(4,128)S(1)}) custom-call(s32[3,2,1408]{2,1,0:T(2,128)S(1)} %get-tuple-element.33.key_ref, f32[2,1408]{1,0:T(2,128)S(1)} %get-tuple-element.32.live_ref, f32[1,1408]{1,0:T(1,128)S(1)} %reshape.34.one_ref, ...), custom_call_target="tpu_custom_call" | custom-call | tf_op jit(solution)/shard_map/second/pallas_call | solution.py:439
  76.2 9.0 %all_to_all.32 = f32[16,1,1408]{2,1,0:T(1,128)S(1)} all-to-all(f32[16,1,1408]{2,1,0:T(1,128)S(1)} %get-tuple-element.47), channel_id=1, replica_groups=mesh['grp_0'=2,'grp_1'=2,'inf_0'=4,'inf_1'=8,'inf_2'=2] {'grp_1','inf_0'..., dimensions={0} | all-to-all | bytes 180224 | tf_op jit(solution)/shard_map/all_to_all | solution.py:460
  85.2 0.1 reduce_sum.32
  85.3 12.7 %all_to_all.33.sums_in_ref = f32[16,1,1408]{2,1,0:T(1,128)S(1)} all-to-all(f32[16,1,1408]{2,1,0:T(1,128)S(1)} %broadcast_in_dim.7), channel_id=1, replica_groups=mesh['grp_0'=2,'grp_1'=2,'inf_0'=4,'inf_1'=8,'inf_2'=2] {'grp_0','inf_1'}, dimensions={0} | all-to-all | bytes 180224 | tf_op jit(solution)/shard_map/all_to_all | solution.py:25
  98.0 0.7 last.1
  98.7 0.6 dynamic-slice_bitcast_fusion
  (5 shorter events, 0.1 us)
Async XLA Ops:
  0.6 35.4 %copy-start.1 = (s32[2,1408]{1,0:T(2,128)S(1)}, s32[2,1408]{1,0:T(2,128)}, u32[]{:S(2)}) copy-start(s32[2,1408]{1,0:T(2,128)} %constant.33.clone.cards_ref) | copy-start | bytes 33796
  0.6 25.8 %copy-start.2 = (f32[1408]{0:T(1024)S(1)}, f32[1408]{0:T(1024)}, u32[]{:S(2)}) copy-start(f32[1408]{0:T(1024)} %param.7) | copy-start | bytes 16900
  0.7 25.8 %copy-start.3 = (f32[1408]{0:T(1024)S(1)}, f32[1408]{0:T(1024)}, u32[]{:S(2)}) copy-start(f32[1408]{0:T(1024)} %param.8) | copy-start | bytes 16900
  2.4 10.7 %all-to-all-start = ((s32[4,80,128]{2,1,0:T(8,128)}), s32[4,80,128]{2,1,0:T(8,128)S(1)}, u32[]{:S(2)}, u32[]{:S(2)}) async-start(s32[4,80,128]{2,1,0:T(8,128)} %pack.1), calls=%async_computation | async-start | bytes 327680 | tf_op jit(solution)/shard_map/all_to_all | solution.py:460
  6.7 0.7 copy-start
  14.3 21.7 %all-to-all-start.1 = ((s32[64,1,256]{2,1,0:T(1,128)}), s32[64,1,256]{2,1,0:T(1,128)S(1)}, u32[]{:S(2)}, u32[]{:S(2)}) async-start(s32[64,1,256]{2,1,0:T(1,128)} %route.1), calls=%async_computation.1 | async-start | bytes 131072 | tf_op jit(solution)/shard_map/all_to_all | solution.py:460
  67.3 1.4 %collective-permute-start = (f32[1,1408]{1,0:T(1,128)S(1)}, f32[1,1408]{1,0:T(1,128)S(1)}, u32[]{:S(2)}, u32[]{:S(2)}) collective-permute-start(f32[1,1408]{1,0:T(1,128)S(1)} %reduce_sum.31.own_sum_ref), channel_id=1, source_target_pairs={{0,64},{64,0},{1,65},{65,1},{2,66},{66,2},{3,67},{67,3},{4,68},{68... | collective-permute-start | bytes 16904 | tf_op jit(solution)/shard_map/ppermute | solution.py:437

commit v7 on v6

--- a/solution.py
+++ b/solution.py
@@ -1,3 +1,5 @@
+from functools import partial
+
 import jax
 import jax.numpy as jnp
 import numpy as np
@@ -49,6 +51,7 @@
 LINE = 128
 PART = 256
 BLOCK = 128
+UPPER = 6
 WIDE = 1408
 DEEP = 128
 PADDED = 1408
@@ -56,7 +59,7 @@
 SECOND_SUM = ("grp_0", "inf_1")
 
 
-def compat_kernel(cards_ref, out_ref, rows_ref, sems):
+def compat_kernel(first_block, cards_ref, out_ref, rows_ref, sems):
     low_ref = cards_ref.at[0:1]
     high_ref = cards_ref.at[1:2]
 
@@ -67,7 +70,7 @@
         )
 
     def rows(step, carry):
-        first = pl.multiple_of(step * BLOCK, BLOCK)
+        first = pl.multiple_of((first_block + step) * BLOCK, BLOCK)
         low_col = jnp.broadcast_to(low_ref[:, pl.ds(first, BLOCK)], (BLOCK, BLOCK)).T
         high_col = jnp.broadcast_to(high_ref[:, pl.ds(first, BLOCK)], (BLOCK, BLOCK)).T
         for start in range(0, PADDED, BLOCK):
@@ -81,26 +84,34 @@
         sent(step).start()
         return carry
 
-    lax.fori_loop(0, H // BLOCK, rows, 0)
-    for step in range(H // BLOCK):
+    lax.fori_loop(0, rows_ref.shape[0], rows, 0)
+    for step in range(rows_ref.shape[0]):
         sent(step).wait()
 
 
-def compat_matrix(cards):
+def compat_rows(cards, first_block, blocks):
     return pl.pallas_call(
-        compat_kernel,
-        out_shape=pltpu.HBM((H, PADDED), jnp.bfloat16),
+        partial(compat_kernel, first_block),
+        out_shape=pltpu.HBM((blocks * BLOCK, PADDED), jnp.bfloat16),
         out_specs=pl.BlockSpec(memory_space=pltpu.HBM),
         scratch_shapes=[
-            pltpu.VMEM((H // BLOCK, BLOCK, PADDED), jnp.bfloat16),
-            pltpu.SemaphoreType.DMA((H // BLOCK,)),
+            pltpu.VMEM((blocks, BLOCK, PADDED), jnp.bfloat16),
+            pltpu.SemaphoreType.DMA((blocks,)),
         ],
         name="compat",
         compiler_params=pltpu.CompilerParams(vmem_limit_bytes=12 << 20),
     )(cards)
 
 
-def pair_sums(key_ref, counter, columns, compat_ref, lhs_ref, low_ref, sums_ref, col_ref, fetch=None):
+def compat_copies(upper_ref, lower_ref, compat_ref, sems):
+    middle = upper_ref.shape[0]
+    return (
+        pltpu.make_async_copy(upper_ref, compat_ref.at[pl.ds(0, middle)], sems.at[0]),
+        pltpu.make_async_copy(lower_ref, compat_ref.at[pl.ds(middle, H - middle)], sems.at[1]),
+    )
+
+
+def pair_sums(key_ref, counter, columns, compat_ref, lhs_ref, low_ref, sums_ref, col_ref, fetch=()):
     alive = (key_ref[counter, :, :H] >= 0).astype(jnp.float32)
     lhs_ref[...] = jnp.zeros((16, H), jnp.float32)
     for k, column in columns.items():
@@ -115,8 +126,8 @@
         return carry
 
     lax.fori_loop(0, H // BLOCK, key_column, 0)
-    if fetch is not None:
-        fetch.wait()
+    for part in fetch:
+        part.wait()
 
     def mine(step, carry):
         start = pl.multiple_of(step * WIDE, WIDE)
@@ -271,14 +282,15 @@
 
 
 def first_kernel(
-    arrived_ref, cards_ref, one_ref, two_ref, compat_hbm_ref,
+    arrived_ref, cards_ref, one_ref, two_ref, upper_ref, lower_ref,
     key_ref, live_ref, share_ref, cont_ref,
     root_check_ref, root_bet_ref, fc_fold_ref, fc_call_ref,
     ac_check_ref, ac_bet_ref, fb_fold_ref, fb_call_ref, share_root_ref, share_fc_ref, turn_ref,
     lhs_ref, low_part_ref, sums_ref, col_ref, compat_ref, compat_sem,
 ):
-    fetch = pltpu.make_async_copy(compat_hbm_ref, compat_ref, compat_sem)
-    fetch.start()
+    fetch = compat_copies(upper_ref, lower_ref, compat_ref, compat_sem)
+    for part in fetch:
+        part.start()
     scratch = (compat_ref, lhs_ref, low_part_ref, sums_ref, col_ref)
     read_flops(arrived_ref, cards_ref, key_ref, live_ref, share_ref)
     live = live_ref[...]
@@ -317,15 +329,16 @@
 
 
 def second_kernel(
-    key_ref, live_ref, one_ref, two_ref, share_ref, compat_hbm_ref,
+    key_ref, live_ref, one_ref, two_ref, share_ref, upper_ref, lower_ref,
     core_ref, own_sum_ref, other_sum_ref,
     root_check_ref, root_bet_ref, fc_fold_ref, fc_call_ref,
     ac_check_ref, ac_bet_ref, fb_fold_ref, fb_call_ref, share_root_ref, share_fc_ref, turn_ref,
     cont_ref, out_root_ref, out_fc_ref, out_turn_ref, out_pre_ref,
     lhs_ref, low_ref, sums_ref, col_ref, compat_ref, compat_sem,
 ):
-    fetch = pltpu.make_async_copy(compat_hbm_ref, compat_ref, compat_sem)
-    fetch.start()
+    fetch = compat_copies(upper_ref, lower_ref, compat_ref, compat_sem)
+    for part in fetch:
+        part.start()
     scratch = (compat_ref, lhs_ref, low_ref, sums_ref, col_ref)
     first_core = core_ref[0, 0] == 0
     own_sum = own_sum_ref[...]
@@ -386,7 +399,7 @@
         pltpu.VMEM((2, 16, PADDED), jnp.float32),
         pltpu.VMEM((2, H, BLOCK), jnp.int32),
         pltpu.VMEM((H, PADDED), jnp.bfloat16),
-        pltpu.SemaphoreType.DMA,
+        pltpu.SemaphoreType.DMA((2,)),
     ]
 
 
@@ -428,11 +441,11 @@
             jax.ShapeDtypeStruct((ITERS - 1, 2, PADDED), jnp.int32),
             *rows_of(pair, (2, 1), (first_count, 1, H), *([pair] * 10), (6, 2, H)),
         ],
-        in_specs=[*in_vmem(4), in_hbm()],
+        in_specs=[*in_vmem(4), in_hbm(), in_hbm()],
         scratch_shapes=pair_scratch(),
         name="first",
         compiler_params=pltpu.CompilerParams(vmem_limit_bytes=20 << 20),
-    )(arrived, cards, one_row, two_row, compat)
+    )(arrived, cards, one_row, two_row, *compat)
     own_sum = jnp.sum(whole_parts(cont), axis=0)
     other_sum = lax.ppermute(own_sum, "grp_1", [(0, 1), (1, 0)])
     core = lax.axis_index("grp_1").astype(jnp.int32).reshape(1, 1)
@@ -440,12 +453,12 @@
         second_kernel,
         out_shape=rows_of((first_count, 1, H), pair, pair, (6, 2, H), (3, H)),
         in_specs=[
-            *in_vmem(5), in_hbm(), pl.BlockSpec(memory_space=pltpu.SMEM), *in_vmem(13)
+            *in_vmem(5), in_hbm(), in_hbm(), pl.BlockSpec(memory_space=pltpu.SMEM), *in_vmem(13)
         ],
         scratch_shapes=pair_scratch(),
         name="second",
         compiler_params=pltpu.CompilerParams(vmem_limit_bytes=20 << 20),
-    )(key_now, live, one_row, two_row, share, compat, core, own_sum, other_sum, *state)
+    )(key_now, live, one_row, two_row, share, *compat, core, own_sum, other_sum, *state)
     parts = whole_parts(cont)
     turns, pre = pl.pallas_call(
         last_kernel,
@@ -568,11 +581,10 @@
     slots = exchanged(
         packed(first_hand, strength, board_mask, flop_weight, runout, groups), GRP
     )
-    slots, compat = lax.optimization_barrier((slots, compat_matrix(cards)))
-    routed = route(slots, lax.axis_index(GRP), shards)
-    routed, compat = lax.optimization_barrier((routed, compat))
-    arrived = exchanged(routed, INF)
-    compat = pltpu.with_memory_space_constraint(compat, pltpu.HBM)
+    slots, upper = lax.optimization_barrier((slots, compat_rows(cards, 0, UPPER)))
+    arrived = exchanged(route(slots, lax.axis_index(GRP), shards), INF)
+    lower = compat_rows(cards, UPPER, H // BLOCK - UPPER)
+    compat = [pltpu.with_memory_space_constraint(part, pltpu.HBM) for part in (upper, lower)]
     turn_reach, pre_reach = solve(arrived, range_one, range_two, cards, compat)
     return turn_reach, lax.dynamic_slice(
         pre_reach, (first_hand,), (hand_block,), allow_negative_indices=False

time: 100 us -> 99.4 us (level)
    pallas_call x1 -> x2, Pallas kernels: 3.91 us -> 4.64 us  [compat_rows(): pl.pallas_call(partial(compat_kernel, first_block), out_shape=pltpu.HBM((...]
  transfers between devices with their start and end apart: 3 -> 3, of which waited for: 3 -> 3; matrix products, arithmetic and copies ran while one was open for 0% -> 0% of each run, Pallas kernels for 4% -> 5%
where the time goes in v7:
time: 99.4 us; the launch traced here: 98.7 us
  blocking collectives  44 us (44%)
  Pallas kernels  23.9 us (24%)
  starting transfers between devices  16.7 us (17%)
  waiting for transfers between devices  11.7 us (12%)
  local copies, waits for them, and re-layouts  1.41 us (1%)
    all_to_all x2, blocking collectives, sent_to_all(): return lax.all_to_all(copies, axis, split_axis=0, concat_axis=0, tiled=True)  25.9 us
    all_to_all x2, blocking collectives, exchanged(): return lax.all_to_all(copies, axis, split_axis=0, concat_axis=0, tiled=True)  18.1 us
    all_to_all x2, starting transfers between devices, exchanged(): return lax.all_to_all(copies, axis, split_axis=0, concat_axis=0, tiled=True)  16.4 us
    all_to_all x2, waiting for transfers between devices, exchanged(): return lax.all_to_all(copies, axis, split_axis=0, concat_axis=0, tiled=True)  10.6 us
    pallas_call x1, Pallas kernels, solve(): pl.pallas_call(first_kernel, out_shape=[jax.ShapeDtypeStruct((ITERS - 1,...  8.23 us
    pallas_call x1, Pallas kernels, solve(): pl.pallas_call(second_kernel, out_shape=rows_of((first_count, 1, H), pair...  7.48 us
    pallas_call x2, Pallas kernels, compat_rows(): pl.pallas_call(partial(compat_kernel, first_block), out_shape=pltpu.HBM((...  4.64 us
  transfers between devices with their start and end apart: 3, of which 3 were waited for; matrix products, arithmetic and copies ran while one was open for 0% of the time, Pallas kernels for 5%

profile of v7, /device:TPU:8, one launch (start us, length us, event | category | flops | bytes accessed | tf_op | source)
XLA Modules:
  0.0 98.7 jit_solution(15707262717685930589)
XLA Ops:
  0.6 0.0 copy-start.1
  0.7 1.7 %pack.1 = s32[4,80,128]{2,1,0:T(8,128)} custom-call(s32[1,1]{1,0:T(1,128)} %bitcast.1.first_hand_ref, s32[22,4,256]{2,1,0:T(4,128)} %bitcast.10, s32[22,256]{1,0:T(8,128)} %bitcast.11, s32[1,256]{1,0:T(1,128)} %bitcast.13, s32[4,2,256]{2,1,0:T(2,128)} %bitcast.12), custom_call_target="tpu_custom_call" | custom-call | tf_op jit(solution)/shard_map/pack/pallas_call | solution.py:512
  2.4 4.3 %all-to-all-start = ((s32[4,80,128]{2,1,0:T(8,128)}), s32[4,80,128]{2,1,0:T(8,128)S(1)}, u32[]{:S(2)}, u32[]{:S(2)}) async-start(s32[4,80,128]{2,1,0:T(8,128)} %pack.1), calls=%async_computation | async-start | bytes 327680 | tf_op jit(solution)/shard_map/all_to_all | solution.py:473
  6.7 0.0 copy-start
  6.7 0.7 copy-done
  7.4 0.0 copy-start.2
  7.4 0.0 copy-start.3
  7.4 2.5 %compat.2.upper_ref = bf16[768,1408]{1,0:T(8,128)(2,1)} custom-call(s32[2,1408]{1,0:T(2,128)S(1)} %copy-done), custom_call_target="tpu_custom_call" | custom-call | tf_op jit(solution)/shard_map/compat/pallas_call | solution.py:93
  9.8 3.3 %all-to-all-done.slots_ref = s32[4,80,128]{2,1,0:T(8,128)S(1)} async-done(((s32[4,80,128]{2,1,0:T(8,128)}), s32[4,80,128]{2,1,0:T(8,128)S(1)}, u32[]{:S(2)}, u32[]{:S(2)}) %all-to-all-start) | async-done | bytes 163872 | tf_op jit(solution)/shard_map/all_to_all | solution.py:473
  13.1 1.2 %route.1 = s32[64,1,256]{2,1,0:T(1,128)} custom-call(s32[1,1]{1,0:T(1,128)} %bitcast.group_ref, s32[4,80,128]{2,1,0:T(8,128)S(1)} %all-to-all-done.slots_ref), custom_call_target="tpu_custom_call" | custom-call | tf_op jit(solution)/shard_map/route/pallas_call | solution.py:565
  14.3 12.1 %all-to-all-start.1 = ((s32[64,1,256]{2,1,0:T(1,128)}), s32[64,1,256]{2,1,0:T(1,128)S(1)}, u32[]{:S(2)}, u32[]{:S(2)}) async-start(s32[64,1,256]{2,1,0:T(1,128)} %route.1), calls=%async_computation.1 | async-start | bytes 131072 | tf_op jit(solution)/shard_map/all_to_all | solution.py:473
  26.4 0.0 copy-done.1
  26.4 2.2 %compat.3.lower_ref = bf16[640,1408]{1,0:T(8,128)(2,1)} custom-call(s32[2,1408]{1,0:T(2,128)S(1)} %copy-done.1), custom_call_target="tpu_custom_call" | custom-call | tf_op jit(solution)/shard_map/compat/pallas_call | solution.py:93
  28.6 0.0 copy-done.2
  28.6 0.0 copy-done.3
  28.6 7.3 %all-to-all-done.1.arrived_ref = s32[64,1,256]{2,1,0:T(1,128)S(1)} async-done(((s32[64,1,256]{2,1,0:T(1,128)}), s32[64,1,256]{2,1,0:T(1,128)S(1)}, u32[]{:S(2)}, u32[]{:S(2)}) %all-to-all-start.1) | async-done | bytes 65568 | tf_op jit(solution)/shard_map/all_to_all | solution.py:473
  35.9 8.2 %first.1 = (s32[3,2,1408]{2,1,0:T(2,128)S(1)}, f32[2,1408]{1,0:T(2,128)S(1)}, f32[2,1]{1,0:T(2,128)S(1)}, f32[16,1,1408]{2,1,0:T(1,128)S(1)}, f32[2,1408]{1,0:T(...) custom-call(s32[64,1,256]{2,1,0:T(1,128)S(1)} %all-to-all-done.1.arr, ...), custom_call_target="tpu_custom_call" | custom-call | tf_op jit(solution)/shard_map/first/pallas_call | solution.py:438
  44.2 9.1 %all_to_all.30 = f32[16,1,1408]{2,1,0:T(1,128)S(1)} all-to-all(f32[16,1,1408]{2,1,0:T(1,128)S(1)} %get-tuple-element.31), channel_id=1, replica_groups=mesh['grp_0'=2,'grp_1'=2,'inf_0'=4,'inf_1'=8,'inf_2'=2] {'grp_1','inf_0'..., dimensions={0} | all-to-all | bytes 180224 | tf_op jit(solution)/shard_map/all_to_all | solution.py:473
  53.3 0.1 reduce_sum.29
  53.4 12.6 %all_to_all.31 = f32[16,1,1408]{2,1,0:T(1,128)S(1)} all-to-all(f32[16,1,1408]{2,1,0:T(1,128)S(1)} %broadcast_in_dim.6), channel_id=1, replica_groups=mesh['grp_0'=2,'grp_1'=2,'inf_0'=4,'inf_1'=8,'inf_2'=2] {'grp_0','inf_1'}, dimensions={0} | all-to-all | bytes 180224 | tf_op jit(solution)/shard_map/all_to_all | solution.py:27
  66.1 0.1 reduce_sum.30
  66.1 0.3 collective-permute-start
  66.4 1.2 %collective-permute-done.other_sum_ref = f32[1,1408]{1,0:T(1,128)S(1)} collective-permute-done((f32[1,1408]{1,0:T(1,128)S(1)}, f32[1,1408]{1,0:T(1,128)S(1)}, u32[]{:S(2)}, u32[]{:S(2)}) %collective-permute-start) | collective-permute-done | bytes 5664 | tf_op jit(solution)/shard_map/ppermute | solution.py:450
  67.6 7.5 %second.1 = (f32[16,1,1408]{2,1,0:T(1,128)S(1)}, f32[2,1408]{1,0:T(2,128)S(1)}, f32[2,1408]{1,0:T(2,128)S(1)}, f32[6,2,1408]{2,1,0:T(2,128)S(1)}, f32[3,1408]{1,0:T(4,128)S(1)}) custom-call(s32[3,2,1408]{2,1,0:T(2,128)S(1)} %get-tuple-element.29.key_ref, f32[2,1408]{1,0:T(2,128)S(1)} %get-tuple-element.28.live_ref, f32[1,1408]{1,0:T(1,128)S(1)} %reshape.34.one_ref, ...), custom_call_target="tpu_custom_call" | custom-call | tf_op jit(solution)/shard_map/second/pallas_call | solution.py:452
  75.1 9.0 %all_to_all.32 = f32[16,1,1408]{2,1,0:T(1,128)S(1)} all-to-all(f32[16,1,1408]{2,1,0:T(1,128)S(1)} %get-tuple-element.43), channel_id=1, replica_groups=mesh['grp_0'=2,'grp_1'=2,'inf_0'=4,'inf_1'=8,'inf_2'=2] {'grp_1','inf_0'..., dimensions={0} | all-to-all | bytes 180224 | tf_op jit(solution)/shard_map/all_to_all | solution.py:473
  84.0 0.1 reduce_sum.32
  84.2 13.2 %all_to_all.33.sums_in_ref = f32[16,1,1408]{2,1,0:T(1,128)S(1)} all-to-all(f32[16,1,1408]{2,1,0:T(1,128)S(1)} %broadcast_in_dim.7), channel_id=1, replica_groups=mesh['grp_0'=2,'grp_1'=2,'inf_0'=4,'inf_1'=8,'inf_2'=2] {'grp_0','inf_1'}, dimensions={0} | all-to-all | bytes 180224 | tf_op jit(solution)/shard_map/all_to_all | solution.py:27
  97.4 0.7 last.1
  98.1 0.6 dynamic-slice_bitcast_fusion
  (5 shorter events, 0.1 us)
Async XLA Ops:
  0.6 25.8 %copy-start.1 = (s32[2,1408]{1,0:T(2,128)S(1)}, s32[2,1408]{1,0:T(2,128)}, u32[]{:S(2)}) copy-start(s32[2,1408]{1,0:T(2,128)} %constant.33.clone.cards_ref) | copy-start | bytes 33796
  2.4 10.7 %all-to-all-start = ((s32[4,80,128]{2,1,0:T(8,128)}), s32[4,80,128]{2,1,0:T(8,128)S(1)}, u32[]{:S(2)}, u32[]{:S(2)}) async-start(s32[4,80,128]{2,1,0:T(8,128)} %pack.1), calls=%async_computation | async-start | bytes 327680 | tf_op jit(solution)/shard_map/all_to_all | solution.py:473
  6.7 0.7 copy-start
  7.4 21.2 %copy-start.2 = (f32[1408]{0:T(1024)S(1)}, f32[1408]{0:T(1024)}, u32[]{:S(2)}) copy-start(f32[1408]{0:T(1024)} %param.7) | copy-start | bytes 16900
  7.4 21.3 %copy-start.3 = (f32[1408]{0:T(1024)S(1)}, f32[1408]{0:T(1024)}, u32[]{:S(2)}) copy-start(f32[1408]{0:T(1024)} %param.8) | copy-start | bytes 16900
  14.3 21.7 %all-to-all-start.1 = ((s32[64,1,256]{2,1,0:T(1,128)}), s32[64,1,256]{2,1,0:T(1,128)S(1)}, u32[]{:S(2)}, u32[]{:S(2)}) async-start(s32[64,1,256]{2,1,0:T(1,128)} %route.1), calls=%async_computation.1 | async-start | bytes 131072 | tf_op jit(solution)/shard_map/all_to_all | solution.py:473
  66.1 1.4 %collective-permute-start = (f32[1,1408]{1,0:T(1,128)S(1)}, f32[1,1408]{1,0:T(1,128)S(1)}, u32[]{:S(2)}, u32[]{:S(2)}) collective-permute-start(f32[1,1408]{1,0:T(1,128)S(1)} %reduce_sum.31.own_sum_ref), channel_id=1, source_target_pairs={{0,64},{64,0},{1,65},{65,1},{2,66},{66,2},{3,67},{67,3},{4,68},{68... | collective-permute-start | bytes 16904 | tf_op jit(solution)/shard_map/ppermute | solution.py:450

commit v8 on v7

--- a/solution.py
+++ b/solution.py
@@ -51,7 +51,7 @@
 LINE = 128
 PART = 256
 BLOCK = 128
-UPPER = 6
+UPPER = 5
 WIDE = 1408
 DEEP = 128
 PADDED = 1408

time: 99.4 us -> 99.4 us (level)
  no operation moved by 1% of the time
where the time goes in v8:
time: 99.4 us; the launch traced here: 98.7 us
  blocking collectives  44 us (44%)
  Pallas kernels  23.9 us (24%)
  starting transfers between devices  16.7 us (17%)
  waiting for transfers between devices  11.7 us (12%)
  local copies, waits for them, and re-layouts  1.41 us (1%)
    all_to_all x2, blocking collectives, sent_to_all(): return lax.all_to_all(copies, axis, split_axis=0, concat_axis=0, tiled=True)  25.9 us
    all_to_all x2, blocking collectives, exchanged(): return lax.all_to_all(copies, axis, split_axis=0, concat_axis=0, tiled=True)  18.1 us
    all_to_all x2, starting transfers between devices, exchanged(): return lax.all_to_all(copies, axis, split_axis=0, concat_axis=0, tiled=True)  16.4 us
    all_to_all x2, waiting for transfers between devices, exchanged(): return lax.all_to_all(copies, axis, split_axis=0, concat_axis=0, tiled=True)  10.6 us
    pallas_call x1, Pallas kernels, solve(): pl.pallas_call(first_kernel, out_shape=[jax.ShapeDtypeStruct((ITERS - 1,...  8.25 us
    pallas_call x1, Pallas kernels, solve(): pl.pallas_call(second_kernel, out_shape=rows_of((first_count, 1, H), pair...  7.5 us
    pallas_call x2, Pallas kernels, compat_rows(): pl.pallas_call(partial(compat_kernel, first_block), out_shape=pltpu.HBM((...  4.65 us
  transfers between devices with their start and end apart: 3, of which 3 were waited for; matrix products, arithmetic and copies ran while one was open for 0% of the time, Pallas kernels for 5%

profile of v8, /device:TPU:8, one launch (start us, length us, event | category | flops | bytes accessed | tf_op | source)
XLA Modules:
  0.0 98.7 jit_solution(16533016774023036401)
XLA Ops:
  0.6 0.0 copy-start.1
  0.7 1.7 %pack.1 = s32[4,80,128]{2,1,0:T(8,128)} custom-call(s32[1,1]{1,0:T(1,128)} %bitcast.1.first_hand_ref, s32[22,4,256]{2,1,0:T(4,128)} %bitcast.10, s32[22,256]{1,0:T(8,128)} %bitcast.11, s32[1,256]{1,0:T(1,128)} %bitcast.13, s32[4,2,256]{2,1,0:T(2,128)} %bitcast.12), custom_call_target="tpu_custom_call" | custom-call | tf_op jit(solution)/shard_map/pack/pallas_call | solution.py:512
  2.3 4.3 %all-to-all-start = ((s32[4,80,128]{2,1,0:T(8,128)}), s32[4,80,128]{2,1,0:T(8,128)S(1)}, u32[]{:S(2)}, u32[]{:S(2)}) async-start(s32[4,80,128]{2,1,0:T(8,128)} %pack.1), calls=%async_computation | async-start | bytes 327680 | tf_op jit(solution)/shard_map/all_to_all | solution.py:473
  6.6 0.0 copy-start
  6.6 0.7 copy-done
  7.3 0.0 copy-start.2
  7.3 0.0 copy-start.3
  7.4 2.2 %compat.2.upper_ref = bf16[640,1408]{1,0:T(8,128)(2,1)} custom-call(s32[2,1408]{1,0:T(2,128)S(1)} %copy-done), custom_call_target="tpu_custom_call" | custom-call | tf_op jit(solution)/shard_map/compat/pallas_call | solution.py:93
  9.5 3.6 %all-to-all-done.slots_ref = s32[4,80,128]{2,1,0:T(8,128)S(1)} async-done(((s32[4,80,128]{2,1,0:T(8,128)}), s32[4,80,128]{2,1,0:T(8,128)S(1)}, u32[]{:S(2)}, u32[]{:S(2)}) %all-to-all-start) | async-done | bytes 163872 | tf_op jit(solution)/shard_map/all_to_all | solution.py:473
  13.1 1.2 %route.1 = s32[64,1,256]{2,1,0:T(1,128)} custom-call(s32[1,1]{1,0:T(1,128)} %bitcast.group_ref, s32[4,80,128]{2,1,0:T(8,128)S(1)} %all-to-all-done.slots_ref), custom_call_target="tpu_custom_call" | custom-call | tf_op jit(solution)/shard_map/route/pallas_call | solution.py:565
  14.3 12.1 %all-to-all-start.1 = ((s32[64,1,256]{2,1,0:T(1,128)}), s32[64,1,256]{2,1,0:T(1,128)S(1)}, u32[]{:S(2)}, u32[]{:S(2)}) async-start(s32[64,1,256]{2,1,0:T(1,128)} %route.1), calls=%async_computation.1 | async-start | bytes 131072 | tf_op jit(solution)/shard_map/all_to_all | solution.py:473
  26.4 0.0 copy-done.1
  26.4 2.5 %compat.3.lower_ref = bf16[768,1408]{1,0:T(8,128)(2,1)} custom-call(s32[2,1408]{1,0:T(2,128)S(1)} %copy-done.1), custom_call_target="tpu_custom_call" | custom-call | tf_op jit(solution)/shard_map/compat/pallas_call | solution.py:93
  28.9 0.0 copy-done.2
  28.9 0.0 copy-done.3
  28.9 7.0 %all-to-all-done.1.arrived_ref = s32[64,1,256]{2,1,0:T(1,128)S(1)} async-done(((s32[64,1,256]{2,1,0:T(1,128)}), s32[64,1,256]{2,1,0:T(1,128)S(1)}, u32[]{:S(2)}, u32[]{:S(2)}) %all-to-all-start.1) | async-done | bytes 65568 | tf_op jit(solution)/shard_map/all_to_all | solution.py:473
  35.9 8.2 %first.1 = (s32[3,2,1408]{2,1,0:T(2,128)S(1)}, f32[2,1408]{1,0:T(2,128)S(1)}, f32[2,1]{1,0:T(2,128)S(1)}, f32[16,1,1408]{2,1,0:T(1,128)S(1)}, f32[2,1408]{1,0:T(...) custom-call(s32[64,1,256]{2,1,0:T(1,128)S(1)} %all-to-all-done.1.arr, ...), custom_call_target="tpu_custom_call" | custom-call | tf_op jit(solution)/shard_map/first/pallas_call | solution.py:438
  44.2 9.1 %all_to_all.30 = f32[16,1,1408]{2,1,0:T(1,128)S(1)} all-to-all(f32[16,1,1408]{2,1,0:T(1,128)S(1)} %get-tuple-element.31), channel_id=1, replica_groups=mesh['grp_0'=2,'grp_1'=2,'inf_0'=4,'inf_1'=8,'inf_2'=2] {'grp_1','inf_0'..., dimensions={0} | all-to-all | bytes 180224 | tf_op jit(solution)/shard_map/all_to_all | solution.py:473
  53.3 0.1 reduce_sum.29
  53.4 12.6 %all_to_all.31 = f32[16,1,1408]{2,1,0:T(1,128)S(1)} all-to-all(f32[16,1,1408]{2,1,0:T(1,128)S(1)} %broadcast_in_dim.6), channel_id=1, replica_groups=mesh['grp_0'=2,'grp_1'=2,'inf_0'=4,'inf_1'=8,'inf_2'=2] {'grp_0','inf_1'}, dimensions={0} | all-to-all | bytes 180224 | tf_op jit(solution)/shard_map/all_to_all | solution.py:27
  66.1 0.1 reduce_sum.30
  66.1 0.3 collective-permute-start
  66.4 1.2 %collective-permute-done.other_sum_ref = f32[1,1408]{1,0:T(1,128)S(1)} collective-permute-done((f32[1,1408]{1,0:T(1,128)S(1)}, f32[1,1408]{1,0:T(1,128)S(1)}, u32[]{:S(2)}, u32[]{:S(2)}) %collective-permute-start) | collective-permute-done | bytes 5664 | tf_op jit(solution)/shard_map/ppermute | solution.py:450
  67.6 7.5 %second.1 = (f32[16,1,1408]{2,1,0:T(1,128)S(1)}, f32[2,1408]{1,0:T(2,128)S(1)}, f32[2,1408]{1,0:T(2,128)S(1)}, f32[6,2,1408]{2,1,0:T(2,128)S(1)}, f32[3,1408]{1,0:T(4,128)S(1)}) custom-call(s32[3,2,1408]{2,1,0:T(2,128)S(1)} %get-tuple-element.29.key_ref, f32[2,1408]{1,0:T(2,128)S(1)} %get-tuple-element.28.live_ref, f32[1,1408]{1,0:T(1,128)S(1)} %reshape.34.one_ref, ...), custom_call_target="tpu_custom_call" | custom-call | tf_op jit(solution)/shard_map/second/pallas_call | solution.py:452
  75.1 9.0 %all_to_all.32 = f32[16,1,1408]{2,1,0:T(1,128)S(1)} all-to-all(f32[16,1,1408]{2,1,0:T(1,128)S(1)} %get-tuple-element.43), channel_id=1, replica_groups=mesh['grp_0'=2,'grp_1'=2,'inf_0'=4,'inf_1'=8,'inf_2'=2] {'grp_1','inf_0'..., dimensions={0} | all-to-all | bytes 180224 | tf_op jit(solution)/shard_map/all_to_all | solution.py:473
  84.1 0.1 reduce_sum.32
  84.2 13.2 %all_to_all.33.sums_in_ref = f32[16,1,1408]{2,1,0:T(1,128)S(1)} all-to-all(f32[16,1,1408]{2,1,0:T(1,128)S(1)} %broadcast_in_dim.7), channel_id=1, replica_groups=mesh['grp_0'=2,'grp_1'=2,'inf_0'=4,'inf_1'=8,'inf_2'=2] {'grp_0','inf_1'}, dimensions={0} | all-to-all | bytes 180224 | tf_op jit(solution)/shard_map/all_to_all | solution.py:27
  97.4 0.7 last.1
  98.1 0.6 dynamic-slice_bitcast_fusion
  (5 shorter events, 0.1 us)
Async XLA Ops:
  0.6 25.8 %copy-start.1 = (s32[2,1408]{1,0:T(2,128)S(1)}, s32[2,1408]{1,0:T(2,128)}, u32[]{:S(2)}) copy-start(s32[2,1408]{1,0:T(2,128)} %constant.33.clone.cards_ref) | copy-start | bytes 33796
  2.3 10.7 %all-to-all-start = ((s32[4,80,128]{2,1,0:T(8,128)}), s32[4,80,128]{2,1,0:T(8,128)S(1)}, u32[]{:S(2)}, u32[]{:S(2)}) async-start(s32[4,80,128]{2,1,0:T(8,128)} %pack.1), calls=%async_computation | async-start | bytes 327680 | tf_op jit(solution)/shard_map/all_to_all | solution.py:473
  6.6 0.7 copy-start
  7.3 21.6 %copy-start.2 = (f32[1408]{0:T(1024)S(1)}, f32[1408]{0:T(1024)}, u32[]{:S(2)}) copy-start(f32[1408]{0:T(1024)} %param.7) | copy-start | bytes 16900
  7.3 21.6 %copy-start.3 = (f32[1408]{0:T(1024)S(1)}, f32[1408]{0:T(1024)}, u32[]{:S(2)}) copy-start(f32[1408]{0:T(1024)} %param.8) | copy-start | bytes 16900
  14.3 21.7 %all-to-all-start.1 = ((s32[64,1,256]{2,1,0:T(1,128)}), s32[64,1,256]{2,1,0:T(1,128)S(1)}, u32[]{:S(2)}, u32[]{:S(2)}) async-start(s32[64,1,256]{2,1,0:T(1,128)} %route.1), calls=%async_computation.1 | async-start | bytes 131072 | tf_op jit(solution)/shard_map/all_to_all | solution.py:473
  66.1 1.4 %collective-permute-start = (f32[1,1408]{1,0:T(1,128)S(1)}, f32[1,1408]{1,0:T(1,128)S(1)}, u32[]{:S(2)}, u32[]{:S(2)}) collective-permute-start(f32[1,1408]{1,0:T(1,128)S(1)} %reduce_sum.31.own_sum_ref), channel_id=1, source_target_pairs={{0,64},{64,0},{1,65},{65,1},{2,66},{66,2},{3,67},{67,3},{4,68},{68... | collective-permute-start | bytes 16904 | tf_op jit(solution)/shard_map/ppermute | solution.py:450
